TPU v7x, 128 devices: a whole 4x4x4 slice. The times are simulated.
128 devices in a mesh: seq: 32 (over y_lo, z, x), head: 4 (over y_hi, core).
Axes of the slice: x: 4, y: 4 (y_hi: 2, y_lo: 2; y = y_hi * 2 + y_lo), z: 4, core: 2. Of those that a mesh axis runs over, the one named last changes fastest.
Arguments:
- queries: bfloat16 [4096, 3072], P('seq', 'head'), may hold values from -8 to 8
- latents: bfloat16 [4096, 576], P('seq'), may hold values from -8 to 8
- key_up: bfloat16 [512, 2048], P(None, 'head'), may hold values from -0.25 to 0.25
- value_up: bfloat16 [512, 2048], P(None, 'head'), may hold values from -0.25 to 0.25
- out_grad: bfloat16 [4096, 2048], P('seq', 'head'), may hold values from -48 to 48
- positions: int32 [4096], P('seq'), may hold values from 0 to 4095, as said below
Outputs:
- query_grad: bfloat16 [4096, 3072], P('seq', 'head')
- latent_grad: float32 [4096, 576], P('seq')
- key_up_grad: float32 [512, 2048], P(None, 'head')
- value_up_grad: float32 [512, 2048], P(None, 'head')
Inputs may be any that keep to these rules, and one draw needn't show every extreme that they name: Every position from 0 to 4095 occurs once; positions come in stripes of 128 consecutive positions in ascending order, each stripe whole within the rows of one device.
All inputs are finite; a program needn't handle non-finite values.
Results may differ from a plain program's by a relative error of at most 0.0084.
Values may be sent and summed in bfloat16 or wider, within the bound.
A program may use at most 64 MiB of HBM per device.

v0:
```python
import math

import jax
import jax.numpy as jnp
from jax import lax
from jax.sharding import PartitionSpec as P

D_LAT = 512
D_ROPE = 64
D_NOPE = 128
D_V = 128


NEG = -1e30


def joined_along(tiles, dim):
    tiles = jnp.moveaxis(tiles, 0, dim)
    dims = tiles.shape
    return tiles.reshape(*dims[:dim], dims[dim] * dims[dim + 1], *dims[dim + 2 :])


def from_everyone(shard, axis):
    size = lax.axis_size(axis)
    return lax.all_to_all(
        jnp.broadcast_to(shard[None], (size, *shard.shape)), axis, 0, 0, tiled=True
    )


def collect(shard, axis, dim):
    return joined_along(from_everyone(shard, axis), dim)


def shifted(value, axis, steps):
    count = lax.axis_size(axis)
    pairs = [(source, (source + steps) % count) for source in range(count)]
    return lax.ppermute(value, axis, pairs)


def taken_together(shard, axis):
    return from_everyone(shard, axis).sum(axis=0)


def cut_along(shard, dim, size):
    before, after = (shard.shape[:dim], shard.shape[dim + 1 :])
    return jnp.moveaxis(shard.reshape(*before, size, -1, *after), dim, 0)


def summed_on_arrival(shard, axis, dim):
    tiles = cut_along(shard, dim, lax.axis_size(axis))
    arrived = lax.all_to_all(tiles, axis, split_axis=0, concat_axis=0, tiled=True)
    return arrived.sum(axis=0)


def filled_up(lines, size):
    spare = -len(lines) % size
    return jnp.pad(lines, [(0, spare)] + [(0, 0)] * (lines.ndim - 1))


def sum_by_parts(shard, axes):
    own = summed_on_arrival(filled_up(shard, lax.axis_size(axes)), axes, 0)
    whole = collect(own, axes, 0)
    return whole[: len(shard)].reshape(shard.shape)


def together(arrays, axis):
    vector, at, done = (jnp.concatenate([a.reshape(-1) for a in arrays]), 0, [])
    so_far = sum_by_parts(vector, axis)
    for a in arrays:
        done.append(so_far[at : at + a.size].reshape(a.shape))
        at += a.size
    return tuple(done)


def up_project(block, key_up, value_up):
    compressed = block[:, :D_LAT]
    key_nope = jnp.dot(compressed, key_up, preferred_element_type=jnp.float32).astype(jnp.bfloat16)
    values = jnp.dot(compressed, value_up, preferred_element_type=jnp.float32).astype(jnp.bfloat16)
    return (key_nope, block[:, D_LAT:], values)


def split_heads(queries, out_grad, key_nope, values):
    heads = key_nope.shape[1] // D_NOPE
    shaped = queries.reshape(queries.shape[0], heads, D_NOPE + D_ROPE)
    grads = out_grad.reshape(out_grad.shape[0], heads, D_V)
    key3 = key_nope.reshape(key_nope.shape[0], heads, D_NOPE)
    value3 = values.reshape(values.shape[0], heads, D_V)
    return (shaped[:, :, :D_NOPE], shaped[:, :, D_NOPE:], grads, key3, value3)


def scores_of(q_nope, q_rope, key3, rope_keys, query_pos, key_pos):
    scale = 1.0 / math.sqrt(D_NOPE + D_ROPE)
    raw = jnp.einsum("bhd,khd->hbk", q_nope, key3, preferred_element_type=jnp.float32)
    raw = raw + jnp.einsum("bhd,kd->hbk", q_rope, rope_keys, preferred_element_type=jnp.float32)
    visible = (key_pos[None, :] <= query_pos[:, None])[None]
    return (raw * scale, visible)


def forward_update(stats, queries, out_grad, query_pos, key_nope, rope_keys, values, key_pos):
    top, total, weighted = stats
    q_nope, q_rope, grads, key3, value3 = split_heads(queries, out_grad, key_nope, values)
    scores, visible = scores_of(q_nope, q_rope, key3, rope_keys, query_pos, key_pos)
    dprobs = jnp.einsum("bhd,khd->hbk", grads, value3, preferred_element_type=jnp.float32)
    masked = jnp.where(visible, scores, NEG)
    new_top = jnp.maximum(top, jnp.max(masked, axis=2))
    weights = jnp.exp(jnp.where(visible, scores - new_top[:, :, None], NEG))
    fade = jnp.exp(top - new_top)
    total = total * fade + jnp.sum(weights, axis=2)
    weighted = weighted * fade + jnp.sum(weights * dprobs, axis=2)
    return (new_top, total, weighted)


def backward_terms(queries, out_grad, query_pos, lse, delta, key_nope, rope_keys, values, key_pos):
    scale = 1.0 / math.sqrt(D_NOPE + D_ROPE)
    q_nope, q_rope, grads, key3, value3 = split_heads(queries, out_grad, key_nope, values)
    scores, visible = scores_of(q_nope, q_rope, key3, rope_keys, query_pos, key_pos)
    probs = jnp.exp(jnp.where(visible, scores - lse[:, :, None], NEG))
    dprobs = jnp.einsum("bhd,khd->hbk", grads, value3, preferred_element_type=jnp.float32)
    dscore = (probs * (dprobs - delta[:, :, None]) * scale).astype(jnp.bfloat16)
    probs16 = probs.astype(jnp.bfloat16)
    grad_nope = jnp.einsum("hbk,khd->bhd", dscore, key3, preferred_element_type=jnp.float32)
    grad_rope = jnp.einsum("hbk,kd->bhd", dscore, rope_keys, preferred_element_type=jnp.float32)
    q_grad = jnp.concatenate([grad_nope, grad_rope], axis=2).reshape(queries.shape[0], -1)
    key_part = jnp.einsum("hbk,bhd->khd", dscore, q_nope, preferred_element_type=jnp.float32)
    value_part = jnp.einsum("hbk,bhd->khd", probs16, grads, preferred_element_type=jnp.float32)
    rope_part = jnp.einsum("hbk,bhd->kd", dscore, q_rope, preferred_element_type=jnp.float32)
    key_rows = key3.shape[0]
    part = jnp.concatenate(
        [key_part.reshape(key_rows, -1), value_part.reshape(key_rows, -1), rope_part], axis=1
    )
    return (q_grad, part)


def shards(queries, latents, key_up, value_up, out_grad, positions):
    rows = queries.shape[0]
    heads = key_up.shape[1] // D_NOPE
    qcols = queries.shape[1]
    nseq = lax.axis_size("seq")
    here = lax.axis_index("seq")
    every_pos = collect(positions, "seq", 0)
    part_width = heads * (D_NOPE + D_V) + D_ROPE

    def owner_start(step):
        return (here - step) % nseq * rows

    def owner_pos(step):
        return lax.dynamic_slice_in_dim(every_pos, owner_start(step), rows, 0)

    start_stats = (
        jnp.full((heads, rows), NEG, jnp.float32),
        jnp.zeros((heads, rows), jnp.float32),
        jnp.zeros((heads, rows), jnp.float32),
    )
    zero_grads = jnp.zeros((rows, part_width), jnp.float32)
    zero_query = jnp.zeros((rows, qcols), jnp.float32)

    def fold_block(stats, block, start):
        key_nope, rope_keys, values = up_project(block, key_up, value_up)
        key_pos = lax.dynamic_slice_in_dim(every_pos, start, block.shape[0], 0)
        return forward_update(
            stats, queries, out_grad, positions, key_nope, rope_keys, values, key_pos
        )

    def grad_block(block, grads, q_acc, step, lse, delta):
        key_nope, rope_keys, values = up_project(block, key_up, value_up)
        q_grad, part = backward_terms(
            queries, out_grad, positions, lse, delta, key_nope, rope_keys, values, owner_pos(step)
        )
        return (grads + part, q_acc + q_grad)

    gathered = lax.all_gather(latents, "seq", axis=0, tiled=True)
    count = gathered.shape[0]
    width = math.gcd(count, 512)

    def turn(index, carry):
        block = lax.dynamic_slice_in_dim(gathered, index * width, width, 0)
        return fold_block(carry, block, index * width)

    top, total, weighted = lax.fori_loop(0, count // width, turn, start_stats)
    lse = top + jnp.log(total)
    delta = weighted / total

    def kept_turn(step, carry):
        grads, q_acc = carry
        block = lax.dynamic_slice_in_dim(gathered, owner_start(step), rows, 0)
        grads, q_acc = grad_block(block, grads, q_acc, step, lse, delta)
        grads = shifted(grads, "seq", 1)
        return (grads, q_acc)

    grads, q_acc = lax.fori_loop(0, nseq - 1, kept_turn, (zero_grads, zero_query))
    last_block = lax.dynamic_slice_in_dim(gathered, owner_start(nseq - 1), rows, 0)
    grads, q_acc = grad_block(last_block, grads, q_acc, nseq - 1, lse, delta)
    key_grads = shifted(grads, "seq", 1)
    split_one = heads * D_NOPE
    split_two = split_one + heads * D_V
    key_grad = key_grads[:, :split_one]
    value_grad = key_grads[:, split_one:split_two]
    key_up32 = key_up.astype(jnp.float32)
    value_up32 = value_up.astype(jnp.float32)
    inner = (((1,), (1,)), ((), ()))
    folded = lax.dot_general(key_grad, key_up32, inner)
    folded = folded + lax.dot_general(value_grad, value_up32, inner)
    latent_part = jnp.concatenate([folded, key_grads[:, split_two:]], axis=1)
    latent_grad = taken_together(latent_part, "head")
    compressed = latents[:, :D_LAT].astype(jnp.float32)
    outer = (((0,), (0,)), ((), ()))
    key_term = lax.dot_general(compressed, key_grad, outer)
    value_term = lax.dot_general(compressed, value_grad, outer)
    key_up_grad, value_up_grad = together((key_term, value_term), "seq")
    return (q_acc.astype(jnp.bfloat16), latent_grad, key_up_grad, value_up_grad)


def solution(mesh):
    in_specs = (
        P("seq", "head"),
        P("seq", None),
        P(None, "head"),
        P(None, "head"),
        P("seq", "head"),
        P("seq"),
    )
    out_specs = (P("seq", "head"), P("seq", None), P(None, "head"), P(None, "head"))
    return jax.shard_map(shards, mesh=mesh, in_specs=in_specs, out_specs=out_specs, check_vma=False)
```

profile of v0, /device:TPU:0, one launch (start us, length us, event | category | flops | bytes accessed | tf_op | source)
XLA Modules:
  0.0 1031.5 jit_solution(13648473115734894433)
XLA Ops:
  9.2 9.4 all-to-all-start
  20.8 6.0 all-to-all-done
  28.9 123.4 %all-gather.2.cloned.1.call-done = bf16[4096,576]{0,1:T(8,128)(2,1)} async-done(((bf16[128,576]{0,1:T(8,128)(2,1)}), bf16[4096,576]{0,1:T(8,128)(2,1)}) %all-gather.2.cloned.1.call-update) | async-done | bytes 4718608 | tf_op jit(solution)/shard_map/all_gather | solution.py:171
  152.4 67.2 %while.36 = (s32[]{:T(128)}, f32[4,128]{1,0:T(4,128)S(1)}, f32[4,128]{1,0:T(4,128)S(1)}, f32[4,128]{1,0:T(4,128)}, s32[4096]{0:T(1024)}, /*index=5*/s32[128]{0:T...) while((s32[]{:T(128)}, f32[4,128]{1,0:T(4,128)S(1)}, ...), condition=%wide.region_4.5_spmd.clone, body=%wide.region_0.4_spmd.clone.sunk | while | flops 708120064 | bytes 10660626 | solution.py:179
  226.1 677.1 %while.37 = (s32[]{:T(128)}, f32[128,1088]{0,1:T(8,128)S(1)}, f32[128,768]{0,1:T(8,128)S(1)}, s32[]{:T(128)}, s32[4096]{0:T(1024)}, /*index=5*/s32[128]{0:T(128)...) while((s32[]{:T(128)}, f32[128,1088]{0,1:T(8,128)S(1)}, ...), condition=%wide.region_6.7_spmd.clone, body=%wide.region_5.6_spmd.clone.sunk | while | flops 244719632 | bytes 11737526 | solution.py:190
  233.8 15.9 %collective-permute-done = f32[128,1088]{0,1:T(8,128)S(1)} collective-permute-done((f32[128,1088]{0,1:T(8,128)}, f32[128,1088]{0,1:T(8,128)S(1)}, u32[]{:S(2)}, u32[]{:S(2)}) %collective-permute-start) | collective-permute-done | bytes 557088 | tf_op jit(solution)/shard_map/while/body/eval_jaxpr/ppermute | solution.py:37
  257.0 15.4 %collective-permute-done = f32[128,1088]{0,1:T(8,128)S(1)} collective-permute-done((f32[128,1088]{0,1:T(8,128)}, f32[128,1088]{0,1:T(8,128)S(1)}, u32[]{:S(2)}, u32[]{:S(2)}) %collective-permute-start) | collective-permute-done | bytes 557088 | tf_op jit(solution)/shard_map/while/body/eval_jaxpr/ppermute | solution.py:37
  279.7 14.5 %collective-permute-done = f32[128,1088]{0,1:T(8,128)S(1)} collective-permute-done((f32[128,1088]{0,1:T(8,128)}, f32[128,1088]{0,1:T(8,128)S(1)}, u32[]{:S(2)}, u32[]{:S(2)}) %collective-permute-start) | collective-permute-done | bytes 557088 | tf_op jit(solution)/shard_map/while/body/eval_jaxpr/ppermute | solution.py:37
  301.6 13.7 %collective-permute-done = f32[128,1088]{0,1:T(8,128)S(1)} collective-permute-done((f32[128,1088]{0,1:T(8,128)}, f32[128,1088]{0,1:T(8,128)S(1)}, u32[]{:S(2)}, u32[]{:S(2)}) %collective-permute-start) | collective-permute-done | bytes 557088 | tf_op jit(solution)/shard_map/while/body/eval_jaxpr/ppermute | solution.py:37
  322.6 12.8 %collective-permute-done = f32[128,1088]{0,1:T(8,128)S(1)} collective-permute-done((f32[128,1088]{0,1:T(8,128)}, f32[128,1088]{0,1:T(8,128)S(1)}, u32[]{:S(2)}, u32[]{:S(2)}) %collective-permute-start) | collective-permute-done | bytes 557088 | tf_op jit(solution)/shard_map/while/body/eval_jaxpr/ppermute | solution.py:37
  342.7 12.8 %collective-permute-done = f32[128,1088]{0,1:T(8,128)S(1)} collective-permute-done((f32[128,1088]{0,1:T(8,128)}, f32[128,1088]{0,1:T(8,128)S(1)}, u32[]{:S(2)}, u32[]{:S(2)}) %collective-permute-start) | collective-permute-done | bytes 557088 | tf_op jit(solution)/shard_map/while/body/eval_jaxpr/ppermute | solution.py:37
  362.8 12.8 %collective-permute-done = f32[128,1088]{0,1:T(8,128)S(1)} collective-permute-done((f32[128,1088]{0,1:T(8,128)}, f32[128,1088]{0,1:T(8,128)S(1)}, u32[]{:S(2)}, u32[]{:S(2)}) %collective-permute-start) | collective-permute-done | bytes 557088 | tf_op jit(solution)/shard_map/while/body/eval_jaxpr/ppermute | solution.py:37
  382.9 12.8 %collective-permute-done = f32[128,1088]{0,1:T(8,128)S(1)} collective-permute-done((f32[128,1088]{0,1:T(8,128)}, f32[128,1088]{0,1:T(8,128)S(1)}, u32[]{:S(2)}, u32[]{:S(2)}) %collective-permute-start) | collective-permute-done | bytes 557088 | tf_op jit(solution)/shard_map/while/body/eval_jaxpr/ppermute | solution.py:37
  403.0 12.8 %collective-permute-done = f32[128,1088]{0,1:T(8,128)S(1)} collective-permute-done((f32[128,1088]{0,1:T(8,128)}, f32[128,1088]{0,1:T(8,128)S(1)}, u32[]{:S(2)}, u32[]{:S(2)}) %collective-permute-start) | collective-permute-done | bytes 557088 | tf_op jit(solution)/shard_map/while/body/eval_jaxpr/ppermute | solution.py:37
  423.1 12.8 %collective-permute-done = f32[128,1088]{0,1:T(8,128)S(1)} collective-permute-done((f32[128,1088]{0,1:T(8,128)}, f32[128,1088]{0,1:T(8,128)S(1)}, u32[]{:S(2)}, u32[]{:S(2)}) %collective-permute-start) | collective-permute-done | bytes 557088 | tf_op jit(solution)/shard_map/while/body/eval_jaxpr/ppermute | solution.py:37
  443.2 12.8 %collective-permute-done = f32[128,1088]{0,1:T(8,128)S(1)} collective-permute-done((f32[128,1088]{0,1:T(8,128)}, f32[128,1088]{0,1:T(8,128)S(1)}, u32[]{:S(2)}, u32[]{:S(2)}) %collective-permute-start) | collective-permute-done | bytes 557088 | tf_op jit(solution)/shard_map/while/body/eval_jaxpr/ppermute | solution.py:37
  463.4 13.4 %collective-permute-done = f32[128,1088]{0,1:T(8,128)S(1)} collective-permute-done((f32[128,1088]{0,1:T(8,128)}, f32[128,1088]{0,1:T(8,128)S(1)}, u32[]{:S(2)}, u32[]{:S(2)}) %collective-permute-start) | collective-permute-done | bytes 557088 | tf_op jit(solution)/shard_map/while/body/eval_jaxpr/ppermute | solution.py:37
  484.0 14.5 %collective-permute-done = f32[128,1088]{0,1:T(8,128)S(1)} collective-permute-done((f32[128,1088]{0,1:T(8,128)}, f32[128,1088]{0,1:T(8,128)S(1)}, u32[]{:S(2)}, u32[]{:S(2)}) %collective-permute-start) | collective-permute-done | bytes 557088 | tf_op jit(solution)/shard_map/while/body/eval_jaxpr/ppermute | solution.py:37
  505.9 15.7 %collective-permute-done = f32[128,1088]{0,1:T(8,128)S(1)} collective-permute-done((f32[128,1088]{0,1:T(8,128)}, f32[128,1088]{0,1:T(8,128)S(1)}, u32[]{:S(2)}, u32[]{:S(2)}) %collective-permute-start) | collective-permute-done | bytes 557088 | tf_op jit(solution)/shard_map/while/body/eval_jaxpr/ppermute | solution.py:37
  528.9 16.8 %collective-permute-done = f32[128,1088]{0,1:T(8,128)S(1)} collective-permute-done((f32[128,1088]{0,1:T(8,128)}, f32[128,1088]{0,1:T(8,128)S(1)}, u32[]{:S(2)}, u32[]{:S(2)}) %collective-permute-start) | collective-permute-done | bytes 557088 | tf_op jit(solution)/shard_map/while/body/eval_jaxpr/ppermute | solution.py:37
  553.0 17.9 %collective-permute-done = f32[128,1088]{0,1:T(8,128)S(1)} collective-permute-done((f32[128,1088]{0,1:T(8,128)}, f32[128,1088]{0,1:T(8,128)S(1)}, u32[]{:S(2)}, u32[]{:S(2)}) %collective-permute-start) | collective-permute-done | bytes 557088 | tf_op jit(solution)/shard_map/while/body/eval_jaxpr/ppermute | solution.py:37
  578.3 18.4 %collective-permute-done = f32[128,1088]{0,1:T(8,128)S(1)} collective-permute-done((f32[128,1088]{0,1:T(8,128)}, f32[128,1088]{0,1:T(8,128)S(1)}, u32[]{:S(2)}, u32[]{:S(2)}) %collective-permute-start) | collective-permute-done | bytes 557088 | tf_op jit(solution)/shard_map/while/body/eval_jaxpr/ppermute | solution.py:37
  604.0 17.6 %collective-permute-done = f32[128,1088]{0,1:T(8,128)S(1)} collective-permute-done((f32[128,1088]{0,1:T(8,128)}, f32[128,1088]{0,1:T(8,128)S(1)}, u32[]{:S(2)}, u32[]{:S(2)}) %collective-permute-start) | collective-permute-done | bytes 557088 | tf_op jit(solution)/shard_map/while/body/eval_jaxpr/ppermute | solution.py:37
  628.9 16.7 %collective-permute-done = f32[128,1088]{0,1:T(8,128)S(1)} collective-permute-done((f32[128,1088]{0,1:T(8,128)}, f32[128,1088]{0,1:T(8,128)S(1)}, u32[]{:S(2)}, u32[]{:S(2)}) %collective-permute-start) | collective-permute-done | bytes 557088 | tf_op jit(solution)/shard_map/while/body/eval_jaxpr/ppermute | solution.py:37
  653.0 15.8 %collective-permute-done = f32[128,1088]{0,1:T(8,128)S(1)} collective-permute-done((f32[128,1088]{0,1:T(8,128)}, f32[128,1088]{0,1:T(8,128)S(1)}, u32[]{:S(2)}, u32[]{:S(2)}) %collective-permute-start) | collective-permute-done | bytes 557088 | tf_op jit(solution)/shard_map/while/body/eval_jaxpr/ppermute | solution.py:37
  676.2 15.0 %collective-permute-done = f32[128,1088]{0,1:T(8,128)S(1)} collective-permute-done((f32[128,1088]{0,1:T(8,128)}, f32[128,1088]{0,1:T(8,128)S(1)}, u32[]{:S(2)}, u32[]{:S(2)}) %collective-permute-start) | collective-permute-done | bytes 557088 | tf_op jit(solution)/shard_map/while/body/eval_jaxpr/ppermute | solution.py:37
  698.5 14.1 %collective-permute-done = f32[128,1088]{0,1:T(8,128)S(1)} collective-permute-done((f32[128,1088]{0,1:T(8,128)}, f32[128,1088]{0,1:T(8,128)S(1)}, u32[]{:S(2)}, u32[]{:S(2)}) %collective-permute-start) | collective-permute-done | bytes 557088 | tf_op jit(solution)/shard_map/while/body/eval_jaxpr/ppermute | solution.py:37
  719.9 13.2 %collective-permute-done = f32[128,1088]{0,1:T(8,128)S(1)} collective-permute-done((f32[128,1088]{0,1:T(8,128)}, f32[128,1088]{0,1:T(8,128)S(1)}, u32[]{:S(2)}, u32[]{:S(2)}) %collective-permute-start) | collective-permute-done | bytes 557088 | tf_op jit(solution)/shard_map/while/body/eval_jaxpr/ppermute | solution.py:37
  740.5 12.8 %collective-permute-done = f32[128,1088]{0,1:T(8,128)S(1)} collective-permute-done((f32[128,1088]{0,1:T(8,128)}, f32[128,1088]{0,1:T(8,128)S(1)}, u32[]{:S(2)}, u32[]{:S(2)}) %collective-permute-start) | collective-permute-done | bytes 557088 | tf_op jit(solution)/shard_map/while/body/eval_jaxpr/ppermute | solution.py:37
  760.6 12.8 %collective-permute-done = f32[128,1088]{0,1:T(8,128)S(1)} collective-permute-done((f32[128,1088]{0,1:T(8,128)}, f32[128,1088]{0,1:T(8,128)S(1)}, u32[]{:S(2)}, u32[]{:S(2)}) %collective-permute-start) | collective-permute-done | bytes 557088 | tf_op jit(solution)/shard_map/while/body/eval_jaxpr/ppermute | solution.py:37
  780.8 12.8 %collective-permute-done = f32[128,1088]{0,1:T(8,128)S(1)} collective-permute-done((f32[128,1088]{0,1:T(8,128)}, f32[128,1088]{0,1:T(8,128)S(1)}, u32[]{:S(2)}, u32[]{:S(2)}) %collective-permute-start) | collective-permute-done | bytes 557088 | tf_op jit(solution)/shard_map/while/body/eval_jaxpr/ppermute | solution.py:37
  800.9 12.8 %collective-permute-done = f32[128,1088]{0,1:T(8,128)S(1)} collective-permute-done((f32[128,1088]{0,1:T(8,128)}, f32[128,1088]{0,1:T(8,128)S(1)}, u32[]{:S(2)}, u32[]{:S(2)}) %collective-permute-start) | collective-permute-done | bytes 557088 | tf_op jit(solution)/shard_map/while/body/eval_jaxpr/ppermute | solution.py:37
  821.0 12.8 %collective-permute-done = f32[128,1088]{0,1:T(8,128)S(1)} collective-permute-done((f32[128,1088]{0,1:T(8,128)}, f32[128,1088]{0,1:T(8,128)S(1)}, u32[]{:S(2)}, u32[]{:S(2)}) %collective-permute-start) | collective-permute-done | bytes 557088 | tf_op jit(solution)/shard_map/while/body/eval_jaxpr/ppermute | solution.py:37
  841.1 18.2 %collective-permute-done = f32[128,1088]{0,1:T(8,128)S(1)} collective-permute-done((f32[128,1088]{0,1:T(8,128)}, f32[128,1088]{0,1:T(8,128)S(1)}, u32[]{:S(2)}, u32[]{:S(2)}) %collective-permute-start) | collective-permute-done | bytes 557088 | tf_op jit(solution)/shard_map/while/body/eval_jaxpr/ppermute | solution.py:37
  866.6 12.8 %collective-permute-done = f32[128,1088]{0,1:T(8,128)S(1)} collective-permute-done((f32[128,1088]{0,1:T(8,128)}, f32[128,1088]{0,1:T(8,128)S(1)}, u32[]{:S(2)}, u32[]{:S(2)}) %collective-permute-start) | collective-permute-done | bytes 557088 | tf_op jit(solution)/shard_map/while/body/eval_jaxpr/ppermute | solution.py:37
  886.8 16.4 %collective-permute-done = f32[128,1088]{0,1:T(8,128)S(1)} collective-permute-done((f32[128,1088]{0,1:T(8,128)}, f32[128,1088]{0,1:T(8,128)S(1)}, u32[]{:S(2)}, u32[]{:S(2)}) %collective-permute-start) | collective-permute-done | bytes 557088 | tf_op jit(solution)/shard_map/while/body/eval_jaxpr/ppermute | solution.py:37
  903.3 13.7 %collective-permute-done.1 = f32[128,1088]{0,1:T(8,128)S(1)} collective-permute-done((f32[128,1088]{0,1:T(8,128)S(1)}, f32[128,1088]{0,1:T(8,128)S(1)}, u32[]{:S(2)}, u32[]{:S(2)}) %collective-permute-start.1) | collective-permute-done | bytes 557088 | tf_op jit(solution)/shard_map/ppermute | solution.py:37
  927.6 3.5 copy.122
  931.2 4.8 all-to-all-start.2
  936.9 17.7 %all-to-all-done.2 = f32[32,1,16384]{2,1,0:T(1,128)} async-done(((f32[32,1,16384]{2,1,0:T(1,128)}), f32[32,1,16384]{2,1,0:T(1,128)}, u32[]{:S(2)}, u32[]{:S(2)}) %all-to-all-start.2) | async-done | bytes 2097184 | tf_op jit(solution)/shard_map/all_to_all | solution.py:51
  955.7 4.5 all-to-all-start.1
  960.1 3.0 reduce_sum.45
  963.1 14.3 %all-to-all-done.1 = f32[4,128,576]{1,2,0:T(8,128)S(1)} async-done(((f32[4,128,576]{1,2,0:T(8,128)}), f32[4,128,576]{1,2,0:T(8,128)S(1)}, u32[]{:S(2)}, u32[]{:S(2)}) %all-to-all-start.1) | async-done | bytes 1179680 | tf_op jit(solution)/shard_map/all_to_all | solution.py:25
  977.5 3.3 broadcast_in_dim.137
  980.7 4.2 all-to-all-start.3
  990.9 22.2 %all-to-all-done.3 = f32[32,1,16384]{2,1,0:T(1,128)S(1)} async-done(((f32[32,1,16384]{2,1,0:T(1,128)}), f32[32,1,16384]{2,1,0:T(1,128)S(1)}, u32[]{:S(2)}, u32[]{:S(2)}) %all-to-all-start.3) | async-done | bytes 2097184 | tf_op jit(solution)/shard_map/all_to_all | solution.py:25
  1013.1 6.8 slice_reduce_fusion
  1022.3 2.4 reshape.263
  (691 shorter events, 325.3 us)
Async XLA Ops:
  7.2 145.2 %all-gather.2.cloned.1.call-start = ((), (), s32[]{:S(2)}) async-start(), calls=%async_computation.4 | async-start | bytes 4866048 | tf_op jit(solution)/shard_map/all_gather | solution.py:171
  9.2 17.6 %all-to-all-start = ((s32[32,1,128]{2,1,0:T(1,128)}), s32[32,1,128]{2,1,0:T(1,128)}, u32[]{:S(2)}, u32[]{:S(2)}) async-start(s32[32,1,128]{2,1,0:T(1,128)} %broadcast_in_dim.132), calls=%async_computation | async-start | bytes 32768 | tf_op jit(solution)/shard_map/all_to_all | solution.py:25
  152.4 6.6 copy-start.6
  160.2 6.6 copy-start.6
  168.7 6.6 copy-start.6
  177.2 6.6 copy-start.6
  185.7 6.6 copy-start.6
  194.1 6.6 copy-start.6
  202.6 6.5 copy-start.6
  211.1 6.5 copy-start.6
  219.6 6.5 copy-start.7
  232.3 17.4 %collective-permute-start = (f32[128,1088]{0,1:T(8,128)}, f32[128,1088]{0,1:T(8,128)S(1)}, u32[]{:S(2)}, u32[]{:S(2)}) collective-permute-start(f32[128,1088]{0,1:T(8,128)} %maximum_add_fusion.3), channel_id=1, source_target_pairs={{0,4},{4,8},{8,12},{12,16},{16,20},{20,24},{24,28},{28,32},{32,36}... | collective-permute-start | bytes 1671176 | tf_op jit(solution)/shard_map/while/body/eval_jaxpr/ppermute | solution.py:37
  255.8 16.6 %collective-permute-start = (f32[128,1088]{0,1:T(8,128)}, f32[128,1088]{0,1:T(8,128)S(1)}, u32[]{:S(2)}, u32[]{:S(2)}) collective-permute-start(f32[128,1088]{0,1:T(8,128)} %maximum_add_fusion.3), channel_id=1, source_target_pairs={{0,4},{4,8},{8,12},{12,16},{16,20},{20,24},{24,28},{28,32},{32,36}... | collective-permute-start | bytes 1671176 | tf_op jit(solution)/shard_map/while/body/eval_jaxpr/ppermute | solution.py:37
  278.5 15.7 %collective-permute-start = (f32[128,1088]{0,1:T(8,128)}, f32[128,1088]{0,1:T(8,128)S(1)}, u32[]{:S(2)}, u32[]{:S(2)}) collective-permute-start(f32[128,1088]{0,1:T(8,128)} %maximum_add_fusion.3), channel_id=1, source_target_pairs={{0,4},{4,8},{8,12},{12,16},{16,20},{20,24},{24,28},{28,32},{32,36}... | collective-permute-start | bytes 1671176 | tf_op jit(solution)/shard_map/while/body/eval_jaxpr/ppermute | solution.py:37
  300.4 14.9 %collective-permute-start = (f32[128,1088]{0,1:T(8,128)}, f32[128,1088]{0,1:T(8,128)S(1)}, u32[]{:S(2)}, u32[]{:S(2)}) collective-permute-start(f32[128,1088]{0,1:T(8,128)} %maximum_add_fusion.3), channel_id=1, source_target_pairs={{0,4},{4,8},{8,12},{12,16},{16,20},{20,24},{24,28},{28,32},{32,36}... | collective-permute-start | bytes 1671176 | tf_op jit(solution)/shard_map/while/body/eval_jaxpr/ppermute | solution.py:37
  321.4 14.0 %collective-permute-start = (f32[128,1088]{0,1:T(8,128)}, f32[128,1088]{0,1:T(8,128)S(1)}, u32[]{:S(2)}, u32[]{:S(2)}) collective-permute-start(f32[128,1088]{0,1:T(8,128)} %maximum_add_fusion.3), channel_id=1, source_target_pairs={{0,4},{4,8},{8,12},{12,16},{16,20},{20,24},{24,28},{28,32},{32,36}... | collective-permute-start | bytes 1671176 | tf_op jit(solution)/shard_map/while/body/eval_jaxpr/ppermute | solution.py:37
  341.5 14.0 %collective-permute-start = (f32[128,1088]{0,1:T(8,128)}, f32[128,1088]{0,1:T(8,128)S(1)}, u32[]{:S(2)}, u32[]{:S(2)}) collective-permute-start(f32[128,1088]{0,1:T(8,128)} %maximum_add_fusion.3), channel_id=1, source_target_pairs={{0,4},{4,8},{8,12},{12,16},{16,20},{20,24},{24,28},{28,32},{32,36}... | collective-permute-start | bytes 1671176 | tf_op jit(solution)/shard_map/while/body/eval_jaxpr/ppermute | solution.py:37
  361.6 14.0 %collective-permute-start = (f32[128,1088]{0,1:T(8,128)}, f32[128,1088]{0,1:T(8,128)S(1)}, u32[]{:S(2)}, u32[]{:S(2)}) collective-permute-start(f32[128,1088]{0,1:T(8,128)} %maximum_add_fusion.3), channel_id=1, source_target_pairs={{0,4},{4,8},{8,12},{12,16},{16,20},{20,24},{24,28},{28,32},{32,36}... | collective-permute-start | bytes 1671176 | tf_op jit(solution)/shard_map/while/body/eval_jaxpr/ppermute | solution.py:37
  381.7 14.0 %collective-permute-start = (f32[128,1088]{0,1:T(8,128)}, f32[128,1088]{0,1:T(8,128)S(1)}, u32[]{:S(2)}, u32[]{:S(2)}) collective-permute-start(f32[128,1088]{0,1:T(8,128)} %maximum_add_fusion.3), channel_id=1, source_target_pairs={{0,4},{4,8},{8,12},{12,16},{16,20},{20,24},{24,28},{28,32},{32,36}... | collective-permute-start | bytes 1671176 | tf_op jit(solution)/shard_map/while/body/eval_jaxpr/ppermute | solution.py:37
  401.8 14.0 %collective-permute-start = (f32[128,1088]{0,1:T(8,128)}, f32[128,1088]{0,1:T(8,128)S(1)}, u32[]{:S(2)}, u32[]{:S(2)}) collective-permute-start(f32[128,1088]{0,1:T(8,128)} %maximum_add_fusion.3), channel_id=1, source_target_pairs={{0,4},{4,8},{8,12},{12,16},{16,20},{20,24},{24,28},{28,32},{32,36}... | collective-permute-start | bytes 1671176 | tf_op jit(solution)/shard_map/while/body/eval_jaxpr/ppermute | solution.py:37
  422.0 14.0 %collective-permute-start = (f32[128,1088]{0,1:T(8,128)}, f32[128,1088]{0,1:T(8,128)S(1)}, u32[]{:S(2)}, u32[]{:S(2)}) collective-permute-start(f32[128,1088]{0,1:T(8,128)} %maximum_add_fusion.3), channel_id=1, source_target_pairs={{0,4},{4,8},{8,12},{12,16},{16,20},{20,24},{24,28},{28,32},{32,36}... | collective-permute-start | bytes 1671176 | tf_op jit(solution)/shard_map/while/body/eval_jaxpr/ppermute | solution.py:37
  442.1 14.0 %collective-permute-start = (f32[128,1088]{0,1:T(8,128)}, f32[128,1088]{0,1:T(8,128)S(1)}, u32[]{:S(2)}, u32[]{:S(2)}) collective-permute-start(f32[128,1088]{0,1:T(8,128)} %maximum_add_fusion.3), channel_id=1, source_target_pairs={{0,4},{4,8},{8,12},{12,16},{16,20},{20,24},{24,28},{28,32},{32,36}... | collective-permute-start | bytes 1671176 | tf_op jit(solution)/shard_map/while/body/eval_jaxpr/ppermute | solution.py:37
  462.2 14.5 %collective-permute-start = (f32[128,1088]{0,1:T(8,128)}, f32[128,1088]{0,1:T(8,128)S(1)}, u32[]{:S(2)}, u32[]{:S(2)}) collective-permute-start(f32[128,1088]{0,1:T(8,128)} %maximum_add_fusion.3), channel_id=1, source_target_pairs={{0,4},{4,8},{8,12},{12,16},{16,20},{20,24},{24,28},{28,32},{32,36}... | collective-permute-start | bytes 1671176 | tf_op jit(solution)/shard_map/while/body/eval_jaxpr/ppermute | solution.py:37
  482.9 15.7 %collective-permute-start = (f32[128,1088]{0,1:T(8,128)}, f32[128,1088]{0,1:T(8,128)S(1)}, u32[]{:S(2)}, u32[]{:S(2)}) collective-permute-start(f32[128,1088]{0,1:T(8,128)} %maximum_add_fusion.3), channel_id=1, source_target_pairs={{0,4},{4,8},{8,12},{12,16},{16,20},{20,24},{24,28},{28,32},{32,36}... | collective-permute-start | bytes 1671176 | tf_op jit(solution)/shard_map/while/body/eval_jaxpr/ppermute | solution.py:37
  504.7 16.8 %collective-permute-start = (f32[128,1088]{0,1:T(8,128)}, f32[128,1088]{0,1:T(8,128)S(1)}, u32[]{:S(2)}, u32[]{:S(2)}) collective-permute-start(f32[128,1088]{0,1:T(8,128)} %maximum_add_fusion.3), channel_id=1, source_target_pairs={{0,4},{4,8},{8,12},{12,16},{16,20},{20,24},{24,28},{28,32},{32,36}... | collective-permute-start | bytes 1671176 | tf_op jit(solution)/shard_map/while/body/eval_jaxpr/ppermute | solution.py:37
  527.7 18.0 %collective-permute-start = (f32[128,1088]{0,1:T(8,128)}, f32[128,1088]{0,1:T(8,128)S(1)}, u32[]{:S(2)}, u32[]{:S(2)}) collective-permute-start(f32[128,1088]{0,1:T(8,128)} %maximum_add_fusion.3), channel_id=1, source_target_pairs={{0,4},{4,8},{8,12},{12,16},{16,20},{20,24},{24,28},{28,32},{32,36}... | collective-permute-start | bytes 1671176 | tf_op jit(solution)/shard_map/while/body/eval_jaxpr/ppermute | solution.py:37
  551.8 19.1 %collective-permute-start = (f32[128,1088]{0,1:T(8,128)}, f32[128,1088]{0,1:T(8,128)S(1)}, u32[]{:S(2)}, u32[]{:S(2)}) collective-permute-start(f32[128,1088]{0,1:T(8,128)} %maximum_add_fusion.3), channel_id=1, source_target_pairs={{0,4},{4,8},{8,12},{12,16},{16,20},{20,24},{24,28},{28,32},{32,36}... | collective-permute-start | bytes 1671176 | tf_op jit(solution)/shard_map/while/body/eval_jaxpr/ppermute | solution.py:37
  577.1 19.6 %collective-permute-start = (f32[128,1088]{0,1:T(8,128)}, f32[128,1088]{0,1:T(8,128)S(1)}, u32[]{:S(2)}, u32[]{:S(2)}) collective-permute-start(f32[128,1088]{0,1:T(8,128)} %maximum_add_fusion.3), channel_id=1, source_target_pairs={{0,4},{4,8},{8,12},{12,16},{16,20},{20,24},{24,28},{28,32},{32,36}... | collective-permute-start | bytes 1671176 | tf_op jit(solution)/shard_map/while/body/eval_jaxpr/ppermute | solution.py:37
  602.9 18.7 %collective-permute-start = (f32[128,1088]{0,1:T(8,128)}, f32[128,1088]{0,1:T(8,128)S(1)}, u32[]{:S(2)}, u32[]{:S(2)}) collective-permute-start(f32[128,1088]{0,1:T(8,128)} %maximum_add_fusion.3), channel_id=1, source_target_pairs={{0,4},{4,8},{8,12},{12,16},{16,20},{20,24},{24,28},{28,32},{32,36}... | collective-permute-start | bytes 1671176 | tf_op jit(solution)/shard_map/while/body/eval_jaxpr/ppermute | solution.py:37
  627.8 17.9 %collective-permute-start = (f32[128,1088]{0,1:T(8,128)}, f32[128,1088]{0,1:T(8,128)S(1)}, u32[]{:S(2)}, u32[]{:S(2)}) collective-permute-start(f32[128,1088]{0,1:T(8,128)} %maximum_add_fusion.3), channel_id=1, source_target_pairs={{0,4},{4,8},{8,12},{12,16},{16,20},{20,24},{24,28},{28,32},{32,36}... | collective-permute-start | bytes 1671176 | tf_op jit(solution)/shard_map/while/body/eval_jaxpr/ppermute | solution.py:37
  651.8 17.0 %collective-permute-start = (f32[128,1088]{0,1:T(8,128)}, f32[128,1088]{0,1:T(8,128)S(1)}, u32[]{:S(2)}, u32[]{:S(2)}) collective-permute-start(f32[128,1088]{0,1:T(8,128)} %maximum_add_fusion.3), channel_id=1, source_target_pairs={{0,4},{4,8},{8,12},{12,16},{16,20},{20,24},{24,28},{28,32},{32,36}... | collective-permute-start | bytes 1671176 | tf_op jit(solution)/shard_map/while/body/eval_jaxpr/ppermute | solution.py:37
  675.0 16.2 %collective-permute-start = (f32[128,1088]{0,1:T(8,128)}, f32[128,1088]{0,1:T(8,128)S(1)}, u32[]{:S(2)}, u32[]{:S(2)}) collective-permute-start(f32[128,1088]{0,1:T(8,128)} %maximum_add_fusion.3), channel_id=1, source_target_pairs={{0,4},{4,8},{8,12},{12,16},{16,20},{20,24},{24,28},{28,32},{32,36}... | collective-permute-start | bytes 1671176 | tf_op jit(solution)/shard_map/while/body/eval_jaxpr/ppermute | solution.py:37
  697.3 15.3 %collective-permute-start = (f32[128,1088]{0,1:T(8,128)}, f32[128,1088]{0,1:T(8,128)S(1)}, u32[]{:S(2)}, u32[]{:S(2)}) collective-permute-start(f32[128,1088]{0,1:T(8,128)} %maximum_add_fusion.3), channel_id=1, source_target_pairs={{0,4},{4,8},{8,12},{12,16},{16,20},{20,24},{24,28},{28,32},{32,36}... | collective-permute-start | bytes 1671176 | tf_op jit(solution)/shard_map/while/body/eval_jaxpr/ppermute | solution.py:37
  718.7 14.4 %collective-permute-start = (f32[128,1088]{0,1:T(8,128)}, f32[128,1088]{0,1:T(8,128)S(1)}, u32[]{:S(2)}, u32[]{:S(2)}) collective-permute-start(f32[128,1088]{0,1:T(8,128)} %maximum_add_fusion.3), channel_id=1, source_target_pairs={{0,4},{4,8},{8,12},{12,16},{16,20},{20,24},{24,28},{28,32},{32,36}... | collective-permute-start | bytes 1671176 | tf_op jit(solution)/shard_map/while/body/eval_jaxpr/ppermute | solution.py:37
  739.3 14.0 %collective-permute-start = (f32[128,1088]{0,1:T(8,128)}, f32[128,1088]{0,1:T(8,128)S(1)}, u32[]{:S(2)}, u32[]{:S(2)}) collective-permute-start(f32[128,1088]{0,1:T(8,128)} %maximum_add_fusion.3), channel_id=1, source_target_pairs={{0,4},{4,8},{8,12},{12,16},{16,20},{20,24},{24,28},{28,32},{32,36}... | collective-permute-start | bytes 1671176 | tf_op jit(solution)/shard_map/while/body/eval_jaxpr/ppermute | solution.py:37
  759.5 14.0 %collective-permute-start = (f32[128,1088]{0,1:T(8,128)}, f32[128,1088]{0,1:T(8,128)S(1)}, u32[]{:S(2)}, u32[]{:S(2)}) collective-permute-start(f32[128,1088]{0,1:T(8,128)} %maximum_add_fusion.3), channel_id=1, source_target_pairs={{0,4},{4,8},{8,12},{12,16},{16,20},{20,24},{24,28},{28,32},{32,36}... | collective-permute-start | bytes 1671176 | tf_op jit(solution)/shard_map/while/body/eval_jaxpr/ppermute | solution.py:37
  779.6 14.0 %collective-permute-start = (f32[128,1088]{0,1:T(8,128)}, f32[128,1088]{0,1:T(8,128)S(1)}, u32[]{:S(2)}, u32[]{:S(2)}) collective-permute-start(f32[128,1088]{0,1:T(8,128)} %maximum_add_fusion.3), channel_id=1, source_target_pairs={{0,4},{4,8},{8,12},{12,16},{16,20},{20,24},{24,28},{28,32},{32,36}... | collective-permute-start | bytes 1671176 | tf_op jit(solution)/shard_map/while/body/eval_jaxpr/ppermute | solution.py:37
  799.7 14.0 %collective-permute-start = (f32[128,1088]{0,1:T(8,128)}, f32[128,1088]{0,1:T(8,128)S(1)}, u32[]{:S(2)}, u32[]{:S(2)}) collective-permute-start(f32[128,1088]{0,1:T(8,128)} %maximum_add_fusion.3), channel_id=1, source_target_pairs={{0,4},{4,8},{8,12},{12,16},{16,20},{20,24},{24,28},{28,32},{32,36}... | collective-permute-start | bytes 1671176 | tf_op jit(solution)/shard_map/while/body/eval_jaxpr/ppermute | solution.py:37
  819.8 14.0 %collective-permute-start = (f32[128,1088]{0,1:T(8,128)}, f32[128,1088]{0,1:T(8,128)S(1)}, u32[]{:S(2)}, u32[]{:S(2)}) collective-permute-start(f32[128,1088]{0,1:T(8,128)} %maximum_add_fusion.3), channel_id=1, source_target_pairs={{0,4},{4,8},{8,12},{12,16},{16,20},{20,24},{24,28},{28,32},{32,36}... | collective-permute-start | bytes 1671176 | tf_op jit(solution)/shard_map/while/body/eval_jaxpr/ppermute | solution.py:37
  840.0 19.3 %collective-permute-start = (f32[128,1088]{0,1:T(8,128)}, f32[128,1088]{0,1:T(8,128)S(1)}, u32[]{:S(2)}, u32[]{:S(2)}) collective-permute-start(f32[128,1088]{0,1:T(8,128)} %maximum_add_fusion.3), channel_id=1, source_target_pairs={{0,4},{4,8},{8,12},{12,16},{16,20},{20,24},{24,28},{28,32},{32,36}... | collective-permute-start | bytes 1671176 | tf_op jit(solution)/shard_map/while/body/eval_jaxpr/ppermute | solution.py:37
  865.5 14.0 %collective-permute-start = (f32[128,1088]{0,1:T(8,128)}, f32[128,1088]{0,1:T(8,128)S(1)}, u32[]{:S(2)}, u32[]{:S(2)}) collective-permute-start(f32[128,1088]{0,1:T(8,128)} %maximum_add_fusion.3), channel_id=1, source_target_pairs={{0,4},{4,8},{8,12},{12,16},{16,20},{20,24},{24,28},{28,32},{32,36}... | collective-permute-start | bytes 1671176 | tf_op jit(solution)/shard_map/while/body/eval_jaxpr/ppermute | solution.py:37
  885.6 17.6 %collective-permute-start = (f32[128,1088]{0,1:T(8,128)}, f32[128,1088]{0,1:T(8,128)S(1)}, u32[]{:S(2)}, u32[]{:S(2)}) collective-permute-start(f32[128,1088]{0,1:T(8,128)} %maximum_add_fusion.3), channel_id=1, source_target_pairs={{0,4},{4,8},{8,12},{12,16},{16,20},{20,24},{24,28},{28,32},{32,36}... | collective-permute-start | bytes 1671176 | tf_op jit(solution)/shard_map/while/body/eval_jaxpr/ppermute | solution.py:37
  903.2 18.8 %copy-start.5 = (bf16[128,576]{0,1:T(8,128)(2,1)S(1)}, bf16[128,576]{0,1:T(8,128)(2,1)}, u32[]{:S(2)}) copy-start(bf16[128,576]{0,1:T(8,128)(2,1)} %param.11) | copy-start | bytes 442372
  903.3 13.8 %collective-permute-start.1 = (f32[128,1088]{0,1:T(8,128)S(1)}, f32[128,1088]{0,1:T(8,128)S(1)}, u32[]{:S(2)}, u32[]{:S(2)}) collective-permute-start(f32[128,1088]{0,1:T(8,128)S(1)} %maximum_add_fusion.1), channel_id=1, source_target_pairs={{0,4},{4,8},{8,12},{12,16},{16,20},{20,24},{24,28},{28,32},{32,36}... | collective-permute-start | bytes 1671176 | tf_op jit(solution)/shard_map/ppermute | solution.py:37
  931.2 23.4 %all-to-all-start.2 = ((f32[32,1,16384]{2,1,0:T(1,128)}), f32[32,1,16384]{2,1,0:T(1,128)}, u32[]{:S(2)}, u32[]{:S(2)}) async-start(f32[32,1,16384]{2,1,0:T(1,128)} %copy.122), calls=%async_computation.2 | async-start | bytes 4194304 | tf_op jit(solution)/shard_map/all_to_all | solution.py:51
  955.7 21.8 %all-to-all-start.1 = ((f32[4,128,576]{1,2,0:T(8,128)}), f32[4,128,576]{1,2,0:T(8,128)S(1)}, u32[]{:S(2)}, u32[]{:S(2)}) async-start(f32[4,128,576]{1,2,0:T(8,128)} %broadcast_in_dim.136), calls=%async_computation.1 | async-start | bytes 2359296 | tf_op jit(solution)/shard_map/all_to_all | solution.py:25
  960.1 25.9 %copy-start.4 = (bf16[128,512]{0,1:T(8,128)(2,1)S(1)}, bf16[128,512]{0,1:T(8,128)(2,1)}, u32[]{:S(2)}) copy-start(bf16[128,512]{0,1:T(8,128)(2,1)} %copy-done.3) | copy-start | bytes 393220
  980.7 32.4 %all-to-all-start.3 = ((f32[32,1,16384]{2,1,0:T(1,128)}), f32[32,1,16384]{2,1,0:T(1,128)S(1)}, u32[]{:S(2)}, u32[]{:S(2)}) async-start(f32[32,1,16384]{2,1,0:T(1,128)} %broadcast_in_dim.137), calls=%async_computation.3 | async-start | bytes 4194304 | tf_op jit(solution)/shard_map/all_to_all | solution.py:25
  (4 other events, 20.8 us)
Sparse Core Ops, SparseCore 0:
  9.5 142.7 all-gather.1
where the time goes:
time: 1040 us; the launch traced here: 1030 us
  waiting for transfers between devices  647 us (62%)
  matrix products  218 us (21%)
  local copies, waits for them, and re-layouts  63.9 us (6%)
  other arithmetic  61.2 us (6%)
  starting transfers between devices  23.4 us (2%)
  between operations  14.4 us (1%)
    ppermute x32, waiting for transfers between devices, shifted(): return lax.ppermute(value, axis, pairs)  463 us
    all_gather x1, waiting for transfers between devices, shards(): gathered = lax.all_gather(latents, 'seq', axis=0, tiled=True)  123 us
    dot_general x40, matrix products, up_project(): jnp.dot(compressed, value_up, preferred_element_type=jnp.float32)  50.9 us
    dot_general x40, matrix products, up_project(): jnp.dot(compressed, key_up, preferred_element_type=jnp.float32)  50.7 us
    all_to_all x3, waiting for transfers between devices, from_everyone(): lax.all_to_all(jnp.broadcast_to(shard[None], (size, *shard.shape)), axis,...  42.5 us
    dot_general x40, matrix products, scores_of(): jnp.einsum('bhd,kd->hbk', q_rope, rope_keys, preferred_element_type=jnp.f...  39.2 us
    add x63, other arithmetic, grad_block(): return (grads + part, q_acc + q_grad)  29.4 us
    dot_general x32, matrix products, backward_terms(): jnp.einsum('hbk,kd->bhd', dscore, rope_keys, preferred_element_type=jnp.f...  27.9 us
  transfers between devices with their start and end apart: 37, of which 37 were waited for; matrix products, arithmetic and copies ran while one was open for 5% of the time, Pallas kernels for 0%

commit v1 on v0

v1 whole, which is shorter than its diff:
```python
import math

import jax
import jax.numpy as jnp
from jax import lax
from jax.experimental import pallas as pl
from jax.experimental.pallas import tpu as pltpu
from jax.sharding import PartitionSpec as P


D_LAT = 512
D_ROPE = 64
D_NOPE = 128
D_V = 128
ROWS = 128
NA = 4
NB = 4
NY = 2
QW = 384
KW = 384
LW = 640
QTOK = NB * NA * ROWS
KTOK = NY * NA * ROWS
TILE = 256
NEG = -1e30
FLOOR = -1e29
SCALE = 1.0 / math.sqrt(D_NOPE + D_ROPE)
LOG2E = math.log2(math.e)
MESH = pl.DeviceIdType.MESH
F32 = jnp.float32
BF16 = jnp.bfloat16
VMEM = pl.BlockSpec(memory_space=pltpu.VMEM)
SMEM = pl.BlockSpec(memory_space=pltpu.SMEM)
NT = (((1,), (1,)), ((), ()))
TN = (((0,), (0,)), ((), ()))


def coords():
    seq = lax.axis_index("seq")
    head = lax.axis_index("head")
    core = head % 2
    y = seq // 16
    z = (seq // 4) % 4
    x = seq % 4
    a = x + core * (z - x)
    b = z + core * (x - z)
    sa = 1 + 3 * core
    sb = 4 - 3 * core

    def dev(a2, b2, y2):
        return (y2 * 16 + a2 * sa + b2 * sb, head)

    return seq, head, y, a, b, dev


def meet(partners):
    barrier = pltpu.get_barrier_semaphore()
    for p in partners:
        pl.semaphore_signal(barrier, inc=1, device_id=p, device_id_type=MESH)
    pl.semaphore_wait(barrier, len(partners))


def rcopy(src, dst, send, recv, device):
    return pltpu.make_async_remote_copy(
        src_ref=src, dst_ref=dst, send_sem=send, recv_sem=recv, device_id=device, device_id_type=MESH
    )


def dot(u, v, dims=(((1,), (0,)), ((), ()))):
    return lax.dot_general(u, v, dims, preferred_element_type=F32)


def shape(dims, dtype=BF16):
    return jax.ShapeDtypeStruct(dims, dtype)


def compute_params():
    return pltpu.CompilerParams(vmem_limit_bytes=56 * 1024 * 1024)


def comm_params(which):
    return pltpu.CompilerParams(
        collective_id=which, has_side_effects=True, vmem_limit_bytes=40 * 1024 * 1024
    )


def prologue_kernel(pos_ref, q_ref, lat_ref, ku_ref, vu_ref, g_ref, pq_ref, pk_ref):
    stripe = lax.shift_right_logical(pos_ref[0], 7).astype(F32)
    lane = lax.broadcasted_iota(jnp.int32, (ROWS, 64), 1)
    q_tail = jnp.where(lane == 0, stripe, 0.0).astype(BF16)
    k_tail = jnp.where(lane == 1, stripe, 0.0).astype(BF16)
    comp = lat_ref[:, :D_LAT]
    kn = dot(comp, ku_ref[...]).astype(BF16)
    vv = dot(comp, vu_ref[...]).astype(BF16)
    k_rest = jnp.concatenate([lat_ref[:, D_LAT:], k_tail], axis=1)
    for h in range(NA):
        q = q_ref[:, h * 192 : (h + 1) * 192]
        pq_ref[h, :, 0:128] = q[:, :128]
        pq_ref[h, :, 128:256] = jnp.concatenate([q[:, 128:], q_tail], axis=1)
        pq_ref[h, :, 256:384] = g_ref[:, h * 128 : (h + 1) * 128]
        pk_ref[h, :, 0:128] = kn[:, h * 128 : (h + 1) * 128]
        pk_ref[h, :, 128:256] = k_rest
        pk_ref[h, :, 256:384] = vv[:, h * 128 : (h + 1) * 128]


def key_positions(kb_ref):
    pick = (lax.broadcasted_iota(jnp.int32, (256, TILE), 0) == 193).astype(F32).astype(BF16)
    stripe = dot(kb_ref[:, :256], pick)
    row = lax.broadcasted_iota(jnp.int32, (KTOK, TILE), 0) % ROWS
    return stripe * 128.0 + row.astype(F32)


def query_positions(qp):
    pick = (lax.broadcasted_iota(jnp.int32, (8, 256), 1) == 192).astype(F32).astype(BF16)
    stripe = dot(pick, qp, NT)[0:1, :]
    col = lax.broadcasted_iota(jnp.int32, (1, TILE), 1) % ROWS
    return stripe * 128.0 + col.astype(F32)


def forward_kernel(qb_ref, kb_ref, st_ref, kpos):
    kpos[...] = key_positions(kb_ref)
    st_ref[...] = jnp.zeros_like(st_ref)

    def tile(i, _):
        at = pl.ds(pl.multiple_of(i * TILE, TILE), TILE)
        qp = qb_ref[at, :256]
        raw = dot(kb_ref[:, :256], qp, NT)
        s = jnp.where(kpos[...] <= query_positions(qp), raw * (SCALE * LOG2E), NEG)
        top = jnp.max(s, axis=0, keepdims=True)
        w = jnp.exp2(s - jnp.maximum(top, FLOOR))
        dp = dot(kb_ref[:, 256:], qb_ref[at, 256:], NT)
        st_ref[0:1, at] = top
        st_ref[1:2, at] = jnp.sum(w, axis=0, keepdims=True)
        st_ref[2:3, at] = jnp.sum(w * dp, axis=0, keepdims=True)
        return 0

    lax.fori_loop(0, QTOK // TILE, tile, 0)


def backward_kernel(qb_ref, kb_ref, sb_ref, dq_ref, dkv_ref, kpos, dk, dv):
    kpos[...] = key_positions(kb_ref)
    dk[...] = jnp.zeros_like(dk)
    dv[...] = jnp.zeros_like(dv)

    def tile(i, _):
        at = pl.ds(pl.multiple_of(i * TILE, TILE), TILE)
        tops = [sb_ref[j, 0:1, at] for j in range(NB)]
        top = jnp.maximum(jnp.maximum(tops[0], tops[1]), jnp.maximum(tops[2], tops[3]))
        fades = [jnp.exp2(t - top) for t in tops]
        total = sum(f * sb_ref[j, 1:2, at] for j, f in enumerate(fades))
        delta = sum(f * sb_ref[j, 2:3, at] for j, f in enumerate(fades)) / total
        lse = top + jnp.log(total) * LOG2E
        qp = qb_ref[at, :256]
        raw = dot(kb_ref[:, :256], qp, NT)
        s = jnp.where(kpos[...] <= query_positions(qp), raw * (SCALE * LOG2E), NEG)
        p = jnp.exp2(s - lse)
        grad = qb_ref[at, 256:]
        dp = dot(kb_ref[:, 256:], grad, NT)
        ds = (p * (dp - delta) * SCALE).astype(BF16)
        dv[...] += dot(p.astype(BF16), grad)
        dk[...] += dot(ds, qp)
        dq_ref[at, :] = dot(ds, kb_ref[:, :256], TN).astype(BF16)
        return 0

    lax.fori_loop(0, QTOK // TILE, tile, 0)
    dkv_ref[:, :256] = dk[...].astype(BF16)
    dkv_ref[:, 256:] = dv[...].astype(BF16)


def fold_kernel(rq_ref, rk_ref, cl_ref, ku_ref, vu_ref, dq_ref, lp_ref, up_ref):
    _, _, _, a, _, _ = coords()
    dq_ref[...] = sum(rq_ref[j].astype(F32) for j in range(NB)).astype(BF16)
    both = rk_ref[0].astype(F32) + rk_ref[1].astype(F32)
    g = jnp.concatenate([both[:, :128], both[:, 256:]], axis=1).astype(BF16)
    at = pl.ds(pl.multiple_of(a * 128, 128), 128)
    w = jnp.concatenate([ku_ref[:, at], vu_ref[:, at]], axis=1)
    lp_ref[:, :D_LAT] = dot(g, w, NT).astype(BF16)
    lp_ref[:, D_LAT:] = both[:, 128:256].astype(BF16)
    up_ref[...] = dot(cl_ref[...], g, TN).astype(BF16)


def own_kernel(rdq_ref, rlp_ref, rup_ref, qg_ref, ls_ref, us_ref):
    for h in range(NA):
        qg_ref[:, h * 192 : (h + 1) * 192] = rdq_ref[h, :, :192]
    ls_ref[...] = sum(rlp_ref[j].astype(F32) for j in range(NA)).astype(BF16)
    us_ref[...] = sum(rup_ref[j].astype(F32) for j in range(NB * NY)).astype(BF16)


def final_kernel(lh_ref, ug_ref, lat_ref, kug_ref, vug_ref):
    total = sum(lh_ref[j].astype(F32) for j in range(4))
    lat_ref[...] = total[:, : D_LAT + D_ROPE]
    for h in range(NA):
        for p in range(NB * NY):
            piece = ug_ref[h, p].astype(F32)
            kug_ref[p * 64 : (p + 1) * 64, h * 128 : (h + 1) * 128] = piece[:, :128]
            vug_ref[p * 64 : (p + 1) * 64, h * 128 : (h + 1) * 128] = piece[:, 128:]


def scatter_kernel(pq, pk, lat, qb, kb, cl, saq, raq, sak, rak, sal, ral, sbq, rbq, syk, ryk):
    _, _, y, a, b, dev = coords()
    meet(
        [dev((a + d) % NA, b, y) for d in (1, 2, 3)]
        + [dev(a, (b + d) % NB, y) for d in (1, 2, 3)]
        + [dev(a, b, 1 - y)]
    )
    done = []
    for d in (1, 3, 2):
        to = (a + d) % NA
        c = rcopy(pq.at[to], qb.at[b, a], saq.at[d - 1], raq.at[d - 1], dev(to, b, y))
        c.start()
        done.append(c)
    for d in (1, 3, 2):
        to = (a + d) % NA
        c = rcopy(pk.at[to], kb.at[y, a], sak.at[d - 1], rak.at[d - 1], dev(to, b, y))
        c.start()
        done.append(c)
    for d in (1, 3, 2):
        to = (a + d) % NB
        c = rcopy(pq.at[a], qb.at[b, a], sbq.at[d - 1, 0], rbq.at[d - 1, 0], dev(a, (b + d) % NB, y))
        c.start()
        done.append(c)
    c = rcopy(pk.at[a], kb.at[y, a], syk.at[0], ryk.at[0], dev(a, b, 1 - y))
    c.start()
    done.append(c)
    for d in (1, 3, 2):
        to = (a + d) % NA
        c = rcopy(lat, cl.at[a], sal.at[d - 1], ral.at[d - 1], dev(to, b, y))
        c.start()
        done.append(c)
    qb[b, a] = pq[a]
    kb[y, a] = pk[a]
    cl[a] = lat[...]
    for d in (1, 3, 2):
        src = (a + NA - d) % NA
        rcopy(qb.at[b, src], qb.at[b, src], saq.at[d - 1], raq.at[d - 1], dev(src, b, y)).wait_recv()
        for e in (1, 3, 2):
            c = rcopy(
                qb.at[b, src], qb.at[b, src], sbq.at[e - 1, d], rbq.at[e - 1, d], dev(a, (b + e) % NB, y)
            )
            c.start()
            done.append(c)
    for d in (1, 3, 2):
        src = (a + NA - d) % NA
        rcopy(kb.at[y, src], kb.at[y, src], sak.at[d - 1], rak.at[d - 1], dev(src, b, y)).wait_recv()
        c = rcopy(kb.at[y, src], kb.at[y, src], syk.at[d], ryk.at[d], dev(a, b, 1 - y))
        c.start()
        done.append(c)
    for d in range(NA):
        src = (a + NA - d) % NA
        for e in (1, 2, 3):
            sb = (b + NB - e) % NB
            rcopy(qb.at[sb, src], qb.at[sb, src], sbq.at[e - 1, d], rbq.at[e - 1, d], dev(a, sb, y)).wait_recv()
        other = kb.at[1 - y, src]
        rcopy(other, other, syk.at[d], ryk.at[d], dev(a, b, 1 - y)).wait_recv()
    for d in (1, 2, 3):
        src = (a + NA - d) % NA
        rcopy(cl.at[src], cl.at[src], sal.at[d - 1], ral.at[d - 1], dev(src, b, y)).wait_recv()
    for c in done:
        c.wait_send()


def stats_kernel(st, sb, send, recv):
    _, _, y, a, b, dev = coords()
    meet([dev(a, (b + d) % NB, y) for d in (1, 2, 3)])
    done = []
    for d in (2, 1, 3):
        c = rcopy(st, sb.at[b], send.at[d - 1], recv.at[d - 1], dev(a, (b + d) % NB, y))
        c.start()
        done.append(c)
    sb[b] = st[...]
    for d in (1, 3, 2):
        src = (b + NB - d) % NB
        rcopy(sb.at[src], sb.at[src], send.at[d - 1], recv.at[d - 1], dev(a, src, y)).wait_recv()
    for c in done:
        c.wait_send()


def partial_kernel(dq, dkv, rq, rk, sq, rcq, sk, rck):
    _, _, y, a, b, dev = coords()
    meet([dev(a, (b + d) % NB, y) for d in (1, 2, 3)] + [dev(a, b, 1 - y)])
    done = []
    c = rcopy(dkv.at[1 - y], rk.at[y], sk, rck, dev(a, b, 1 - y))
    c.start()
    done.append(c)
    for d in (2, 1, 3):
        to = (b + d) % NB
        c = rcopy(dq.at[to], rq.at[b], sq.at[d - 1], rcq.at[d - 1], dev(a, to, y))
        c.start()
        done.append(c)
    rq[b] = dq[b]
    rk[y] = dkv[y]
    for d in (1, 3, 2):
        src = (b + NB - d) % NB
        rcopy(rq.at[src], rq.at[src], sq.at[d - 1], rcq.at[d - 1], dev(a, src, y)).wait_recv()
    rcopy(rk.at[1 - y], rk.at[1 - y], sk, rck, dev(a, b, 1 - y)).wait_recv()
    for c in done:
        c.wait_send()


def return_kernel(dq, lp, up, rdq, rlp, rup, sq, rq, sl, rl, su, ru):
    _, _, y, a, b, dev = coords()
    others = [(e, f) for e in range(NB) for f in range(NY) if (e, f) != (0, 0)]
    meet(
        [dev((a + d) % NA, b, y) for d in (1, 2, 3)]
        + [dev(a, (b + e) % NB, (y + f) % NY) for e, f in others]
    )
    done = []
    mine = b * NY + y
    for d in (2, 1, 3):
        to = (a + d) % NA
        c = rcopy(lp.at[to], rlp.at[a], sl.at[d - 1], rl.at[d - 1], dev(to, b, y))
        c.start()
        done.append(c)
        c = rcopy(dq.at[to], rdq.at[a], sq.at[d - 1], rq.at[d - 1], dev(to, b, y))
        c.start()
        done.append(c)
    for i, (e, f) in enumerate(others):
        tb, ty = (b + e) % NB, (y + f) % NY
        c = rcopy(up.at[tb * NY + ty], rup.at[mine], su.at[i], ru.at[i], dev(a, tb, ty))
        c.start()
        done.append(c)
    rdq[a] = dq[a]
    rlp[a] = lp[a]
    rup[mine] = up[mine]
    for d in (1, 3, 2):
        src = (a + NA - d) % NA
        rcopy(rlp.at[src], rlp.at[src], sl.at[d - 1], rl.at[d - 1], dev(src, b, y)).wait_recv()
        rcopy(rdq.at[src], rdq.at[src], sq.at[d - 1], rq.at[d - 1], dev(src, b, y)).wait_recv()
    for i, (e, f) in enumerate(others):
        fb, fy = (b + NB - e) % NB, (y + f) % NY
        slot = rup.at[fb * NY + fy]
        rcopy(slot, slot, su.at[i], ru.at[i], dev(a, fb, fy)).wait_recv()
    for c in done:
        c.wait_send()


def share_kernel(ls, us, lh, ug, sl, rl, sy, ry, sb_, rb, sa_, ra):
    seq, head, y, a, b, dev = coords()
    meet(
        [(seq, (head + d) % 4) for d in (1, 2, 3)]
        + [dev((a + d) % NA, b, y) for d in (1, 2, 3)]
        + [dev(a, (b + d) % NB, y) for d in (1, 2, 3)]
        + [dev(a, b, 1 - y)]
    )
    done = []

    def go(src, dst, s, r, device):
        c = rcopy(src, dst, s, r, device)
        c.start()
        done.append(c)

    def landed(ref, s, r, device):
        rcopy(ref, ref, s, r, device).wait_recv()

    mine = b * NY + y
    go(us, ug.at[a, mine], sy, ry, dev(a, b, 1 - y))
    for e in (2, 1, 3):
        go(us, ug.at[a, mine], sb_.at[e - 1, 0], rb.at[e - 1, 0], dev(a, (b + e) % NB, y))
    for d in (2, 1, 3):
        go(us, ug.at[a, mine], sa_.at[d - 1, 0, 0], ra.at[d - 1, 0, 0], dev((a + d) % NA, b, y))
    for d in (1, 2, 3):
        go(ls, lh.at[head], sl.at[d - 1], rl.at[d - 1], (seq, (head + d) % 4))
    ug[a, mine] = us[...]
    lh[head] = ls[...]

    def pass_on(slot, e, f):
        for d in (2, 1, 3):
            go(slot, slot, sa_.at[d - 1, e, f], ra.at[d - 1, e, f], dev((a + d) % NA, b, y))

    across = ug.at[a, b * NY + 1 - y]
    landed(across, sy, ry, dev(a, b, 1 - y))
    for e in (2, 1, 3):
        go(across, across, sb_.at[e - 1, 1], rb.at[e - 1, 1], dev(a, (b + e) % NB, y))
    pass_on(across, 0, 1)
    for f in range(NY):
        for e in (1, 3, 2):
            fb = (b + NB - e) % NB
            slot = ug.at[a, fb * NY + (y + f) % NY]
            landed(slot, sb_.at[e - 1, f], rb.at[e - 1, f], dev(a, fb, y))
            pass_on(slot, e, f)
    for d in (1, 2, 3):
        fa = (a + NA - d) % NA
        for e in range(NB):
            for f in range(NY):
                slot = ug.at[fa, (b + NB - e) % NB * NY + (y + f) % NY]
                landed(slot, sa_.at[d - 1, e, f], ra.at[d - 1, e, f], dev(fa, b, y))
    for d in (1, 2, 3):
        fh = (head + 4 - d) % 4
        landed(lh.at[fh], sl.at[d - 1], rl.at[d - 1], (seq, fh))
    for c in done:
        c.wait_send()


def local(kernel, outs, scratch=(), specs=None):
    def call(*args):
        return pl.pallas_call(
            kernel,
            out_shape=outs,
            in_specs=specs or [VMEM] * len(args),
            out_specs=jax.tree.map(lambda _: VMEM, outs),
            scratch_shapes=list(scratch),
            compiler_params=compute_params(),
        )(*args)

    return call


def remote(kernel, which, outs, sems):
    def call(*args):
        return pl.pallas_call(
            kernel,
            out_shape=outs,
            in_specs=[VMEM] * len(args),
            out_specs=jax.tree.map(lambda _: VMEM, outs),
            scratch_shapes=[pltpu.SemaphoreType.DMA(s) if s else pltpu.SemaphoreType.DMA for s in sems],
            compiler_params=comm_params(which),
        )(*args)

    return call


def shards(queries, latents, key_up, value_up, out_grad, positions):
    pq, pk = local(
        prologue_kernel,
        (shape((NA, ROWS, QW)), shape((NA, ROWS, KW))),
        specs=[SMEM] + [VMEM] * 5,
    )(positions, queries, latents, key_up, value_up, out_grad)
    qb, kb, cl = remote(
        scatter_kernel,
        1,
        (shape((NB, NA, ROWS, QW)), shape((NY, NA, ROWS, KW)), shape((NA, ROWS, D_LAT))),
        [(3,), (3,), (3,), (3,), (3,), (3,), (3, 4), (3, 4), (4,), (4,)],
    )(pq, pk, latents[:, :D_LAT])
    qb = qb.reshape(QTOK, QW)
    kb = kb.reshape(KTOK, KW)
    st = local(forward_kernel, shape((8, QTOK), F32), [pltpu.VMEM((KTOK, TILE), F32)])(qb, kb)
    sb = remote(stats_kernel, 2, shape((NB, 8, QTOK), F32), [(3,), (3,)])(st)
    dq, dkv = local(
        backward_kernel,
        (shape((QTOK, 256)), shape((KTOK, KW))),
        [pltpu.VMEM((KTOK, TILE), F32), pltpu.VMEM((KTOK, 256), F32), pltpu.VMEM((KTOK, 128), F32)],
    )(qb, kb, sb)
    half = NA * ROWS
    rq, rk = remote(
        partial_kernel,
        3,
        (shape((NB, half, 256)), shape((NY, half, KW))),
        [(3,), (3,), (), ()],
    )(dq.reshape(NB, half, 256), dkv.reshape(NY, half, KW))
    dq, lp, up = local(
        fold_kernel, (shape((half, 256)), shape((half, LW)), shape((D_LAT, 256)))
    )(rq, rk, cl.reshape(half, D_LAT), key_up, value_up)
    rdq, rlp, rup = remote(
        return_kernel,
        4,
        (shape((NA, ROWS, 256)), shape((NA, ROWS, LW)), shape((NB * NY, 64, 256))),
        [(3,), (3,), (3,), (3,), (7,), (7,)],
    )(dq.reshape(NA, ROWS, 256), lp.reshape(NA, ROWS, LW), up.reshape(NB * NY, 64, 256))
    query_grad, ls, us = local(
        own_kernel, (shape((ROWS, 768)), shape((ROWS, LW)), shape((64, 256)))
    )(rdq, rlp, rup)
    lh, ug = remote(
        share_kernel,
        5,
        (shape((4, ROWS, LW)), shape((NA, NB * NY, 64, 256))),
        [(3,), (3,), (), (), (3, 2), (3, 2), (3, 4, 2), (3, 4, 2)],
    )(ls, us)
    latent_grad, key_up_grad, value_up_grad = local(
        final_kernel,
        (shape((ROWS, D_LAT + D_ROPE), F32), shape((D_LAT, 512), F32), shape((D_LAT, 512), F32)),
    )(lh, ug)
    return (query_grad, latent_grad, key_up_grad, value_up_grad)


def solution(mesh):
    in_specs = (
        P("seq", "head"),
        P("seq", None),
        P(None, "head"),
        P(None, "head"),
        P("seq", "head"),
        P("seq"),
    )
    out_specs = (P("seq", "head"), P("seq", None), P(None, "head"), P(None, "head"))
    return jax.shard_map(shards, mesh=mesh, in_specs=in_specs, out_specs=out_specs, check_vma=False)
```

time: 1040 us -> 125 us (0.12)
  waiting for transfers between devices: 647 us -> 0 us
  matrix products: 218 us -> 0 us
  Pallas kernels: 0 us -> 101 us
  other arithmetic: 61.2 us -> 0 us
  local copies, waits for them, and re-layouts: 63.9 us -> 22.9 us
  starting transfers between devices: 23.4 us -> 0 us
  between operations: 14.4 us -> 0.75 us
    ppermute x32 -> x0, waiting for transfers between devices: 463 us -> none  [shifted(): return lax.ppermute(value, axis, pairs)]
    dot_general x364 -> x0, matrix products: 218 us -> none  [the longest x40 50.9 us: up_project(): jnp.dot(compressed, value_up, preferred_element_type=jnp.float32)]
    all_gather x1 -> x0, waiting for transfers between devices: 123 us -> none  [shards(): gathered = lax.all_gather(latents, 'seq', axis=0, tiled=True)]
    pallas_call x0 -> x11, Pallas kernels: none -> 101 us  [the longest x5 67.7 us: call(): pl.pallas_call(kernel, out_shape=outs, in_specs=[VMEM] * len(args), out_s...]
    all_to_all x4 -> x0, waiting for transfers between devices: 60.2 us -> none  [the longest x3 42.5 us: from_everyone(): lax.all_to_all(jnp.broadcast_to(shard[None], (size, *shard.shape)), axis,...]
    add x71 -> x0, other arithmetic: 39 us -> none  [the longest x63 29.4 us: grad_block(): return (grads + part, q_acc + q_grad)]
    dynamic_slice x40 -> x0, local copies, waits for them, and re-layouts: 30.4 us -> none  [the longest x32 24.3 us: owner_pos(): return lax.dynamic_slice_in_dim(every_pos, owner_start(step), rows, 0)]
    all_to_all x4 -> x0, starting transfers between devices: 22.9 us -> none  [the longest x3 18.1 us: from_everyone(): lax.all_to_all(jnp.broadcast_to(shard[None], (size, *shard.shape)), axis,...]
  transfers between devices with their start and end apart: 37 -> 0, of which waited for: 37 -> 0; matrix products, arithmetic and copies ran while one was open for 5% -> 0% of each run, Pallas kernels for 0% -> 0%
where the time goes in v1:
time: 125 us; the launch traced here: 124 us
  Pallas kernels  101 us (81%)
  local copies, waits for them, and re-layouts  22.9 us (18%)
    pallas_call x5, Pallas kernels, call(): pl.pallas_call(kernel, out_shape=outs, in_specs=[VMEM] * len(args), out_s...  67.7 us
    pallas_call x6, Pallas kernels, call(): pl.pallas_call(kernel, out_shape=outs, in_specs=specs or [VMEM] * len(arg...  33 us
    unnamed x46, local copies, waits for them, and re-layouts  22.9 us

profile of v1, /device:TPU:0, one launch (start us, length us, event | category | flops | bytes accessed | tf_op | source)
XLA Modules:
  0.0 124.4 jit_solution(2738766101992731493)
XLA Ops:
  0.6 1.1 copy.10.lat_ref
  1.7 0.0 copy-start.21
  1.7 0.6 copy-done.21
  2.4 2.5 %shard_map.93 = (bf16[4,128,384]{2,1,0:T(8,128)(2,1)}, bf16[4,128,384]{2,1,0:T(8,128)(2,1)}) custom-call(s32[128]{0:T(128)} %pos_ref.1, bf16[128,768]{1,0:T(8,128)(2,1)} %q_ref.1, bf16[128,576]{1,0:T(8,128)(2,1)} %copy-done.21, bf16[512,512]{1,0:T(8,128)(2,1)} %ku_ref.3, bf16[512,512]{1,0:T(8,128)(2,1)} %vu_ref.3, bf16[128,512]{1,0:T(8,128)(2,1)} %g_ref.1), custom_call_target="tpu_custom_call" | custom-call | tf_op jit(solution)/shard_map/pallas_call | solution.py:396
  4.9 0.0 copy-start.12
  4.9 1.0 copy-done.12
  5.9 0.0 copy-start.13
  5.9 1.0 copy-done.13
  6.9 23.5 %shard_map.94 = (bf16[4,4,128,384]{3,2,1,0:T(8,128)(2,1)S(1)}, bf16[2,4,128,384]{3,2,1,0:T(8,128)(2,1)S(1)}, bf16[4,128,512]{2,1,0:T(8,128)(2,1)S(1)}) custom-call(bf16[4,128,384]{2,1,0:T(8,128)(2,1)S(1)} %copy-done.12, bf16[4,128,384]{2,1,0:T(8,128)(2,1)S(1)} %copy-done.13, bf16[128,512]{1,0:T(8,128)(2,1)S(1)} %slice.4.lat), custom_call_target="tpu_custom_call" | custom-call | tf_op jit(solution)/shard_map/pallas_call | solution.py:410
  30.4 0.0 copy-start
  30.4 1.2 copy-done
  31.6 0.9 copy-done.1
  32.5 0.0 copy-start.11
  32.5 0.8 copy-done.11
  33.3 9.7 %shard_map.95.st = f32[8,2048]{1,0:T(8,128)} custom-call(bf16[2048,384]{1,0:T(8,128)(2,1)} %bitcast.8, bf16[1024,384]{1,0:T(8,128)(2,1)} %bitcast.10), custom_call_target="tpu_custom_call" | custom-call | tf_op jit(solution)/shard_map/pallas_call | solution.py:396
  43.0 0.0 copy-start.14
  43.0 0.8 copy-done.14
  43.9 6.5 %shard_map.96.sb_ref = f32[4,8,2048]{2,1,0:T(8,128)S(1)} custom-call(f32[8,2048]{1,0:T(8,128)S(1)} %copy-done.14), custom_call_target="tpu_custom_call" | custom-call | tf_op jit(solution)/shard_map/pallas_call | solution.py:410
  50.4 0.0 copy-start.2
  50.4 0.7 copy-done.2
  51.1 12.2 %shard_map.97 = (bf16[2048,256]{1,0:T(8,128)(2,1)}, bf16[1024,384]{1,0:T(8,128)(2,1)}) custom-call(bf16[2048,384]{1,0:T(8,128)(2,1)} %bitcast.9, bf16[1024,384]{1,0:T(8,128)(2,1)} %bitcast.11, f32[4,8,2048]{2,1,0:T(8,128)} %copy-done.2), custom_call_target="tpu_custom_call" | custom-call | tf_op jit(solution)/shard_map/pallas_call | solution.py:396
  63.4 0.0 copy-start.3
  63.4 1.2 copy-done.3
  64.6 0.0 copy-start.6
  64.6 1.1 copy-done.6
  65.7 11.1 %shard_map.98 = (bf16[4,512,256]{2,1,0:T(8,128)(2,1)S(1)}, bf16[2,512,384]{2,1,0:T(8,128)(2,1)S(1)}) custom-call(bf16[4,512,256]{2,1,0:T(8,128)(2,1)S(1)} %bitcast.12, bf16[2,512,384]{2,1,0:T(8,128)(2,1)S(1)} %bitcast.13), custom_call_target="tpu_custom_call" | custom-call | tf_op jit(solution)/shard_map/pallas_call | solution.py:410
  76.8 0.0 copy-start.4
  76.9 1.0 copy-done.4
  77.8 0.9 copy-done.7
  78.7 3.4 %shard_map.99 = (bf16[512,256]{1,0:T(8,128)(2,1)}, bf16[512,640]{1,0:T(8,128)(2,1)}, bf16[512,256]{1,0:T(8,128)(2,1)}) custom-call(bf16[4,512,256]{2,1,0:T(8,128)(2,1)} %copy-done.4, bf16[2,512,384]{2,1,0:T(8,128)(2,1)} %copy-done.7, bf16[512,512]{1,0:T(8,128)(2,1)} %bitcast.15, bf16[512,512]{1,0:T(8,128)(2,1)} %ku_ref.3, bf16[512,512]{1,0:T(8,128)(2,1)} %vu_ref.3), custom_call_target="tpu_custom_call" | custom-call | tf_op jit(solution)/shard_map/pallas_call | solution.py:396
  82.1 0.0 copy-start.8
  82.1 1.1 copy-done.8
  83.2 0.9 copy-done.15
  84.2 0.9 copy-done.16
  85.1 10.2 %shard_map.100 = (bf16[4,128,256]{2,1,0:T(8,128)(2,1)S(1)}, bf16[4,128,640]{2,1,0:T(8,128)(2,1)S(1)}, bf16[8,64,256]{2,1,0:T(8,128)(2,1)S(1)}) custom-call(bf16[4,128,256]{2,1,0:T(8,128)(2,1)S(1)} %bitcast.16, bf16[4,128,640]{2,1,0:T(8,128)(2,1)S(1)} %bitcast.14, bf16[8,64,256]{2,1,0:T(8,128)(2,1)S(1)} %bitcast.17), custom_call_target="tpu_custom_call" | custom-call | tf_op jit(solution)/shard_map/pallas_call | solution.py:410
  95.4 0.0 copy-start.9
  95.4 0.8 copy-done.9
  96.2 0.7 copy-done.17
  96.9 0.7 copy-done.18
  97.6 2.1 %shard_map.101 = (bf16[128,768]{1,0:T(8,128)(2,1)}, bf16[128,640]{1,0:T(8,128)(2,1)}, bf16[64,256]{1,0:T(8,128)(2,1)}) custom-call(bf16[4,128,256]{2,1,0:T(8,128)(2,1)} %copy-done.17, bf16[4,128,640]{2,1,0:T(8,128)(2,1)} %copy-done.9, bf16[8,64,256]{2,1,0:T(8,128)(2,1)} %copy-done.18), custom_call_target="tpu_custom_call" | custom-call | tf_op jit(solution)/shard_map/pallas_call | solution.py:396
  99.7 0.9 copy-done.19
  100.6 0.8 copy-done.20
  101.4 16.3 %shard_map.102 = (bf16[4,128,640]{2,1,0:T(8,128)(2,1)S(1)}, bf16[4,8,64,256]{3,2,1,0:T(8,128)(2,1)S(1)}) custom-call(bf16[128,640]{1,0:T(8,128)(2,1)S(1)} %copy-done.19, bf16[64,256]{1,0:T(8,128)(2,1)S(1)} %copy-done.20), custom_call_target="tpu_custom_call" | custom-call | tf_op jit(solution)/shard_map/pallas_call | solution.py:410
  117.7 0.0 copy-start.5
  117.7 1.0 copy-done.5
  118.7 0.9 copy-done.10
  119.6 3.0 %shard_map.103 = (f32[128,576]{1,0:T(8,128)}, f32[512,512]{1,0:T(8,128)}, f32[512,512]{1,0:T(8,128)}) custom-call(bf16[4,128,640]{2,1,0:T(8,128)(2,1)} %copy-done.10, bf16[4,8,64,256]{3,2,1,0:T(8,128)(2,1)} %copy-done.5), custom_call_target="tpu_custom_call" | custom-call | tf_op jit(solution)/shard_map/pallas_call | solution.py:396
  122.5 1.8 %copy.12 = f32[128,576]{0,1:T(8,128)} copy(f32[128,576]{1,0:T(8,128)} %get-tuple-element.51) | data formatting | bytes 589824
  (10 shorter events, 0.0 us)
Async XLA Ops:
  1.7 0.7 copy-start.21
  4.9 1.0 copy-start.12
  5.9 1.0 copy-start.13
  30.4 1.2 copy-start
  31.6 0.9 copy-start.1
  32.5 0.8 copy-start.11
  43.0 0.8 copy-start.14
  50.4 0.7 copy-start.2
  63.4 1.2 copy-start.3
  64.6 1.1 copy-start.6
  76.8 1.0 copy-start.4
  77.8 0.9 copy-start.7
  82.1 1.1 copy-start.8
  83.2 0.9 copy-start.15
  84.2 0.9 copy-start.16
  95.4 0.8 copy-start.9
  96.2 0.7 copy-start.17
  96.9 0.7 copy-start.18
  99.7 0.9 copy-start.19
  100.6 0.8 copy-start.20
  117.7 1.0 copy-start.5
  118.7 0.9 copy-start.10

commit v2 on v0

v2 whole, which is shorter than its diff:
```python
import math

import jax
import jax.numpy as jnp
from jax import lax
from jax.experimental import pallas as pl
from jax.experimental.pallas import tpu as pltpu
from jax.sharding import PartitionSpec as P


D_LAT = 512
D_ROPE = 64
D_NOPE = 128
D_V = 128
ROWS = 128
NA = 4
NB = 4
NY = 2
QW = 384
KW = 384
LW = 640
QTOK = NB * NA * ROWS
KTOK = NY * NA * ROWS
TILE = 256
NEG = -1e30
FLOOR = -1e29
SCALE = 1.0 / math.sqrt(D_NOPE + D_ROPE)
LOG2E = math.log2(math.e)
MESH = pl.DeviceIdType.MESH
F32 = jnp.float32
BF16 = jnp.bfloat16
VMEM = pl.BlockSpec(memory_space=pltpu.VMEM)
SMEM = pl.BlockSpec(memory_space=pltpu.SMEM)
NT = (((1,), (1,)), ((), ()))
TN = (((0,), (0,)), ((), ()))


def coords():
    seq = lax.axis_index("seq")
    head = lax.axis_index("head")
    core = head % 2
    y = seq // 16
    z = (seq // 4) % 4
    x = seq % 4
    a = x + core * (z - x)
    b = z + core * (x - z)
    sa = 1 + 3 * core
    sb = 4 - 3 * core

    def dev(a2, b2, y2):
        return (y2 * 16 + a2 * sa + b2 * sb, head)

    return seq, head, y, a, b, dev


def rcopy(src, dst, send, recv, device):
    return pltpu.make_async_remote_copy(
        src_ref=src, dst_ref=dst, send_sem=send, recv_sem=recv, device_id=device, device_id_type=MESH
    )


def dot(u, v, dims=(((1,), (0,)), ((), ()))):
    return lax.dot_general(u, v, dims, preferred_element_type=F32)


def shape(dims, dtype=BF16):
    return jax.ShapeDtypeStruct(dims, dtype)


def whole_kernel(
    pos_ref, q_ref, latt_ref, ku_ref, vu_ref, g_ref,
    qg_ref, lg_ref, kug_ref, vug_ref,
    pq, pk, qb, kb, cl, kpos, s_all, dp_all, stl, sb, rows, dqa, dqs, rq, dka, dva, dks, rk,
    lps, rlp, dqf, rdq, ups, rup, usk, usv, ugk, ugv, lsum, lhalf, rhalf, ly, ry_, lfin, rfin,
    s_aq, r_aq, s_ak, r_ak, s_al, r_al, s_bq, r_bq, s_yk, r_yk, s_st, r_st, s_dq, r_dq, s_dk, r_dk,
    s_lp, r_lp, s_qf, r_qf, s_up, r_up, s_ky, r_ky, s_kb, r_kb, s_ka, r_ka, s_vy, r_vy, s_va, r_va, s_vb, r_vb,
    s_h, r_h,
):
    seq, head, y, a, b, dev = coords()
    core = head % 2
    twin = (seq, head + 1 - 2 * core)
    far = (seq, (head + 2) % 4)
    across = dev(a, b, 1 - y)
    near = (1, 3, 2)
    others = [(e, f) for e in range(NB) for f in range(NY) if (e, f) != (0, 0)]

    barrier = pltpu.get_barrier_semaphore()
    for p in (
        [dev((a + d) % NA, b, y) for d in near]
        + [dev(a, (b + e) % NB, (y + f) % NY) for e, f in others]
        + [twin, far]
    ):
        pl.semaphore_signal(barrier, inc=1, device_id=p, device_id_type=MESH)

    done = []

    def go(src, dst, send, recv, device):
        c = rcopy(src, dst, send, recv, device)
        c.start()
        done.append(c)

    def landed(ref, send, recv):
        rcopy(ref, ref, send, recv, across).wait_recv()

    stripe = lax.shift_right_logical(pos_ref[0], 7).astype(F32)
    lane = lax.broadcasted_iota(jnp.int32, (ROWS, 128), 1)
    q_tail = jnp.where(lane == 64, stripe, 0.0)[:, 64:].astype(BF16)
    k_tail = jnp.where(lane == 65, stripe, 0.0)
    comp = latt_ref[:D_LAT, :]
    kn = dot(comp, ku_ref[...], TN).astype(BF16)
    vv = dot(comp, vu_ref[...], TN).astype(BF16)
    eye = (
        lax.broadcasted_iota(jnp.int32, (64, 128), 0) == lax.broadcasted_iota(jnp.int32, (64, 128), 1)
    ).astype(F32).astype(BF16)
    k_rest = (dot(latt_ref[D_LAT:, :], eye, TN) + k_tail).astype(BF16)
    for h in range(NA):
        pk[h, :, 0:128] = kn[:, h * 128 : (h + 1) * 128]
        pk[h, :, 128:256] = k_rest
        pk[h, :, 256:384] = vv[:, h * 128 : (h + 1) * 128]
        q = q_ref[:, h * 192 : (h + 1) * 192]
        pq[h, :, 0:128] = q[:, :128]
        pq[h, :, 128:256] = jnp.concatenate([q[:, 128:], q_tail], axis=1)
        pq[h, :, 256:384] = g_ref[:, h * 128 : (h + 1) * 128]

    pl.semaphore_wait(barrier, 3 + len(others) + 2)

    for d in near:
        to = (a + d) % NA
        go(pk.at[to], kb.at[0, a], s_ak.at[d - 1], r_ak.at[d - 1], dev(to, b, y))
        go(pq.at[to], qb.at[b, a], s_aq.at[d - 1], r_aq.at[d - 1], dev(to, b, y))
    go(pk.at[a], kb.at[1, a], s_yk.at[0], r_yk.at[0], across)
    for e in near:
        go(pq.at[a], qb.at[b, a], s_bq.at[e - 1, 0], r_bq.at[b, 0], dev(a, (b + e) % NB, y))
    for d in near:
        go(latt_ref.at[pl.ds(0, D_LAT)], cl.at[a], s_al.at[d - 1], r_al.at[d - 1], dev((a + d) % NA, b, y))
    qb[b, a] = pq[a]
    kb[0, a] = pk[a]
    cl[a] = comp
    for d in near:
        frm = (a + NA - d) % NA
        slot = kb.at[0, frm]
        landed(slot, s_ak.at[d - 1], r_ak.at[d - 1])
        go(slot, kb.at[1, frm], s_yk.at[d], r_yk.at[d], across)
        slot = qb.at[b, frm]
        landed(slot, s_aq.at[d - 1], r_aq.at[d - 1])
        for e in near:
            go(slot, slot, s_bq.at[e - 1, d], r_bq.at[b, d], dev(a, (b + e) % NB, y))
    for d in (0, 1, 3, 2):
        landed(kb.at[1, (a + NA - d) % NA], s_yk.at[d], r_yk.at[d])

    kp = kb[...].reshape(KTOK, KW)[:, :256]
    pick = (lax.broadcasted_iota(jnp.int32, (256, TILE), 0) == 193).astype(F32).astype(BF16)
    row = lax.broadcasted_iota(jnp.int32, (KTOK, TILE), 0) % ROWS
    kpos[...] = dot(kp, pick) * 128.0 + row.astype(F32)
    stl[...] = jnp.zeros_like(stl)
    pickq = (lax.broadcasted_iota(jnp.int32, (8, 256), 1) == 192).astype(F32).astype(BF16)
    col = lax.broadcasted_iota(jnp.int32, (1, TILE), 1) % ROWS
    for j in range(NB):

        @pl.when(b != j)
        def _():
            for d in range(NA):
                landed(qb.at[j, (a + NA - d) % NA], s_bq.at[0, d], r_bq.at[j, d])

        for t in range(2):
            at = slice(t * TILE, (t + 1) * TILE)
            two = qb[j, 2 * t : 2 * t + 2].reshape(TILE, QW)
            qp = two[:, :256]
            keys = kb[...].reshape(KTOK, KW)
            qpos = dot(pickq, qp, NT)[0:1, :] * 128.0 + col.astype(F32)
            raw = dot(keys[:, :256], qp, NT)
            s = jnp.where(kpos[...] <= qpos, raw * (SCALE * LOG2E), NEG)
            s_all[j, :, at] = s
            top = jnp.max(s, axis=0, keepdims=True)
            w = jnp.exp2(s - jnp.maximum(top, FLOOR))
            dp = dot(keys[:, 256:], two[:, 256:], NT)
            dp_all[j, :, at] = dp
            stl[j, 0:1, at] = top
            stl[j, 1:2, at] = jnp.sum(w, axis=0, keepdims=True)
            stl[j, 2:3, at] = jnp.sum(w * dp, axis=0, keepdims=True)
        for e in near:
            go(stl.at[j], sb.at[j, b], s_st.at[e - 1, j], r_st.at[j, b], dev(a, (b + e) % NB, y))

    half = NA * ROWS
    for j in range(NB):
        sb[j, b] = stl[j]
        for i in range(NB):

            @pl.when(b != i)
            def _():
                landed(sb.at[j, i], s_st.at[0, j], r_st.at[j, i])

        tops = [sb[j, i, 0:1, :] for i in range(NB)]
        top = jnp.maximum(jnp.maximum(tops[0], tops[1]), jnp.maximum(tops[2], tops[3]))
        fades = [jnp.exp2(t - top) for t in tops]
        total = sum(f * sb[j, i, 1:2, :] for i, f in enumerate(fades))
        rows[j, 1:2, :] = sum(f * sb[j, i, 2:3, :] for i, f in enumerate(fades)) / total
        rows[j, 0:1, :] = top + jnp.log(total) * LOG2E

    for k in (1, 0):
        ks = slice(k * half, (k + 1) * half)
        for j in range(NB):
            qall = qb[j].reshape(half, QW)
            keys = kb[k].reshape(half, KW)
            p = jnp.exp2(s_all[j, ks, :] - rows[j, 0:1, :])
            ds = (p * (dp_all[j, ks, :] - rows[j, 1:2, :]) * SCALE).astype(BF16)
            dv = dot(p.astype(BF16), qall[:, 256:])
            dk = dot(ds, qall[:, :256])
            dq = dot(ds, keys[:, :256], TN)
            if j == 0:
                dva[ks, :] = dv
                dka[ks, :] = dk
            else:
                dva[ks, :] += dv
                dka[ks, :] += dk
            if k == 1:
                dqa[j] = dq
            else:
                dqs[j] = (dqa[j] + dq).astype(BF16)

                @pl.when(b != j)
                def _():
                    rcopy(dqs.at[j], rq.at[b], s_dq.at[j], r_dq.at[b], dev(a, j, y)).start()

        if k == 1:
            dks[:, :256] = dka[half:, :].astype(BF16)
            dks[:, 256:] = dva[half:, :].astype(BF16)
            go(dks, rk, s_dk, r_dk, across)

    for d in near:
        landed(cl.at[(a + NA - d) % NA], s_al.at[d - 1], r_al.at[d - 1])
    landed(rk, s_dk, r_dk)
    dk = dka[:half, :] + rk[:, :256].astype(F32)
    dv = dva[:half, :] + rk[:, 256:].astype(F32)
    g = jnp.concatenate([dk[:, :128], dv], axis=1).astype(BF16)
    mine_cols = pl.ds(pl.multiple_of(a * 128, 128), 128)
    w = jnp.concatenate([ku_ref[:, mine_cols], vu_ref[:, mine_cols]], axis=1)
    comps = jnp.concatenate([cl[i] for i in range(NA)], axis=1)
    up = dot(comps, g)
    for i in range(NB * NY):
        ups[i] = up[i * 64 : (i + 1) * 64, :].astype(BF16)
    lp = dot(w, g, NT)
    rope = dot(eye, dk[:, 128:].astype(BF16), NT)
    for i in range(NA):
        lps[i, :D_LAT, :] = lp[:, i * 128 : (i + 1) * 128].astype(BF16)
        lps[i, D_LAT:, :] = rope[:, i * 128 : (i + 1) * 128].astype(BF16)
    mine = b * NY + y
    for i, (e, f) in enumerate(others):
        tb, ty = (b + e) % NB, (y + f) % NY
        go(ups.at[tb * NY + ty], rup.at[mine], s_up.at[i], r_up.at[i], dev(a, tb, ty))
    for d in near:
        go(lps.at[(a + d) % NA], rlp.at[a], s_lp.at[d - 1], r_lp.at[d - 1], dev((a + d) % NA, b, y))
    rup[mine] = ups[mine]
    rlp[a] = lps[a]

    rq[b] = dqs[b]
    for j in range(NB):

        @pl.when(b != j)
        def _():
            landed(rq.at[j], s_dq.at[j], r_dq.at[j])

    dqf[...] = sum(rq[j].astype(F32) for j in range(NB)).astype(BF16).reshape(NA, ROWS, 256)
    for d in near:
        go(dqf.at[(a + d) % NA], rdq.at[a], s_qf.at[d - 1], r_qf.at[d - 1], dev((a + d) % NA, b, y))
    rdq[a] = dqf[a]

    for i, (e, f) in enumerate(others):
        fb, fy = (b + NB - e) % NB, (y + f) % NY
        landed(rup.at[fb * NY + fy], s_up.at[i], r_up.at[i])
    us = sum(rup[i].astype(F32) for i in range(NB * NY)).astype(BF16)
    usk[...] = us[:, :128]
    usv[...] = us[:, 128:]
    ugk[a, mine] = us[:, :128]
    ugv[a, mine] = us[:, 128:]
    go(usk, ugk.at[a, mine], s_ky, r_ky, across)
    go(usv, ugv.at[a, mine], s_vy, r_vy, across)
    for e in near:
        go(usk, ugk.at[a, mine], s_kb.at[e - 1, 0], r_kb.at[e - 1, 0], dev(a, (b + e) % NB, y))
    for d in near:
        go(usv, ugv.at[a, mine], s_va.at[d - 1, 0], r_va.at[d - 1, 0], dev((a + d) % NA, b, y))
    for d in near:
        go(usk, ugk.at[a, mine], s_ka.at[d - 1, 0, 0], r_ka.at[d - 1, 0, 0], dev((a + d) % NA, b, y))
    for e in near:
        go(usv, ugv.at[a, mine], s_vb.at[e - 1, 0, 0], r_vb.at[e - 1, 0, 0], dev(a, (b + e) % NB, y))

    for d in near:
        landed(rlp.at[(a + NA - d) % NA], s_lp.at[d - 1], r_lp.at[d - 1])
    lsum[...] = sum(rlp[i].astype(F32) for i in range(NA)).reshape(2, 288, 128)
    lhalf[...] = lsum[1 - core].astype(BF16)
    go(lhalf, rhalf, s_h.at[0], r_h.at[0], twin)

    def k_over_a(slot, e, f):
        for d in near:
            go(slot, slot, s_ka.at[d - 1, e, f], r_ka.at[d - 1, e, f], dev((a + d) % NA, b, y))

    def v_over_b(slot, d, f):
        for e in near:
            go(slot, slot, s_vb.at[e - 1, d, f], r_vb.at[e - 1, d, f], dev(a, (b + e) % NB, y))

    other = b * NY + 1 - y
    landed(ugk.at[a, other], s_ky, r_ky)
    for e in near:
        go(ugk.at[a, other], ugk.at[a, other], s_kb.at[e - 1, 1], r_kb.at[e - 1, 1], dev(a, (b + e) % NB, y))
    landed(ugv.at[a, other], s_vy, r_vy)
    for d in near:
        go(ugv.at[a, other], ugv.at[a, other], s_va.at[d - 1, 1], r_va.at[d - 1, 1], dev((a + d) % NA, b, y))
    k_over_a(ugk.at[a, other], 0, 1)
    v_over_b(ugv.at[a, other], 0, 1)

    landed(rhalf, s_h.at[0], r_h.at[0])
    both = lsum[core] + rhalf[...].astype(F32)
    ly[...] = both.astype(BF16)
    go(ly, ry_, s_h.at[1], r_h.at[1], far)

    for f in range(NY):
        for e in near:
            slot = ugk.at[a, (b + NB - e) % NB * NY + (y + f) % NY]
            landed(slot, s_kb.at[e - 1, f], r_kb.at[e - 1, f])
            k_over_a(slot, e, f)
            slot = ugv.at[(a + NA - e) % NA, b * NY + (y + f) % NY]
            landed(slot, s_va.at[e - 1, f], r_va.at[e - 1, f])
            v_over_b(slot, e, f)

    landed(ry_, s_h.at[1], r_h.at[1])
    whole = ly[...].astype(F32) + ry_[...].astype(F32)
    lfin[...] = whole
    go(lfin, rfin, s_h.at[2], r_h.at[2], twin)

    for d in near:
        landed(rdq.at[(a + NA - d) % NA], s_qf.at[d - 1], r_qf.at[d - 1])
    for h in range(NA):
        qg_ref[:, h * 192 : (h + 1) * 192] = rdq[h, :, :192]

    landed(rfin, s_h.at[2], r_h.at[2])
    lg_ref[core] = lfin[...]
    lg_ref[1 - core] = rfin[...]

    for d in near:
        fa = (a + NA - d) % NA
        for e in range(NB):
            for f in range(NY):
                landed(
                    ugk.at[fa, (b + NB - e) % NB * NY + (y + f) % NY],
                    s_ka.at[d - 1, e, f], r_ka.at[d - 1, e, f],
                )
                landed(
                    ugv.at[(a + NA - e) % NA, (b + NB - d) % NB * NY + (y + f) % NY],
                    s_vb.at[d - 1, e, f], r_vb.at[d - 1, e, f],
                )
    for h in range(NA):
        kug_ref[:, h * 128 : (h + 1) * 128] = ugk[h].reshape(D_LAT, 128)
        vug_ref[:, h * 128 : (h + 1) * 128] = ugv[h].reshape(D_LAT, 128)
    for j in range(NB):

        @pl.when(b != j)
        def _():
            rcopy(dqs.at[j], dqs.at[j], s_dq.at[j], r_dq.at[j], across).wait_send()

    for c in done:
        c.wait_send()


def shards(queries, latents, key_up, value_up, out_grad, positions):
    half = NA * ROWS
    dma = pltpu.SemaphoreType.DMA
    scratch = [
        pltpu.VMEM((NA, ROWS, QW), BF16),
        pltpu.VMEM((NA, ROWS, KW), BF16),
        pltpu.VMEM((NB, NA, ROWS, QW), BF16),
        pltpu.VMEM((NY, NA, ROWS, KW), BF16),
        pltpu.VMEM((NA, D_LAT, ROWS), BF16),
        pltpu.VMEM((KTOK, TILE), F32),
        pltpu.VMEM((NB, KTOK, half), F32),
        pltpu.VMEM((NB, KTOK, half), F32),
        pltpu.VMEM((NB, 8, half), F32),
        pltpu.VMEM((NB, NB, 8, half), F32),
        pltpu.VMEM((NB, 8, half), F32),
        pltpu.VMEM((NB, half, 256), F32),
        pltpu.VMEM((NB, half, 256), BF16),
        pltpu.VMEM((NB, half, 256), BF16),
        pltpu.VMEM((KTOK, 256), F32),
        pltpu.VMEM((KTOK, 128), F32),
        pltpu.VMEM((half, KW), BF16),
        pltpu.VMEM((half, KW), BF16),
        pltpu.VMEM((NA, 576, ROWS), BF16),
        pltpu.VMEM((NA, 576, ROWS), BF16),
        pltpu.VMEM((NA, ROWS, 256), BF16),
        pltpu.VMEM((NA, ROWS, 256), BF16),
        pltpu.VMEM((NB * NY, 64, 256), BF16),
        pltpu.VMEM((NB * NY, 64, 256), BF16),
        pltpu.VMEM((64, 128), BF16),
        pltpu.VMEM((64, 128), BF16),
        pltpu.VMEM((NA, NB * NY, 64, 128), BF16),
        pltpu.VMEM((NA, NB * NY, 64, 128), BF16),
        pltpu.VMEM((2, 288, ROWS), F32),
        pltpu.VMEM((288, ROWS), BF16),
        pltpu.VMEM((288, ROWS), BF16),
        pltpu.VMEM((288, ROWS), BF16),
        pltpu.VMEM((288, ROWS), BF16),
        pltpu.VMEM((288, ROWS), F32),
        pltpu.VMEM((288, ROWS), F32),
    ]
    sems = [
        dma((3,)), dma((3,)), dma((3,)), dma((3,)), dma((3,)), dma((3,)),
        dma((3, 4)), dma((4, 4)), dma((4,)), dma((4,)),
        dma((3, 4)), dma((4, 4)), dma((4,)), dma((4,)), dma, dma,
        dma((3,)), dma((3,)), dma((3,)), dma((3,)), dma((7,)), dma((7,)),
        dma, dma, dma((3, 2)), dma((3, 2)), dma((3, 4, 2)), dma((3, 4, 2)),
        dma, dma, dma((3, 2)), dma((3, 2)), dma((3, 4, 2)), dma((3, 4, 2)),
        dma((3,)), dma((3,)),
    ]
    qg, lg, kug, vug = pl.pallas_call(
        whole_kernel,
        out_shape=(
            shape((ROWS, 768)),
            shape((2, 288, ROWS), F32),
            shape((D_LAT, 512)),
            shape((D_LAT, 512)),
        ),
        in_specs=[SMEM] + [VMEM] * 5,
        out_specs=(VMEM,) * 4,
        scratch_shapes=scratch + sems,
        compiler_params=pltpu.CompilerParams(
            collective_id=0, has_side_effects=True, vmem_limit_bytes=58 * 1024 * 1024
        ),
    )(positions, queries, latents.T, key_up, value_up, out_grad)
    return (qg, lg.reshape(576, ROWS).T, kug.astype(F32), vug.astype(F32))


def solution(mesh):
    in_specs = (
        P("seq", "head"),
        P("seq", None),
        P(None, "head"),
        P(None, "head"),
        P("seq", "head"),
        P("seq"),
    )
    out_specs = (P("seq", "head"), P("seq", None), P(None, "head"), P(None, "head"))
    return jax.shard_map(shards, mesh=mesh, in_specs=in_specs, out_specs=out_specs, check_vma=False)
```

time: 1040 us -> 74.4 us (0.07)
  waiting for transfers between devices: 647 us -> 0 us
  matrix products: 218 us -> 0 us
  Pallas kernels: 0 us -> 68.5 us
  local copies, waits for them, and re-layouts: 63.9 us -> 1.75 us
  other arithmetic: 61.2 us -> 3.3 us
  starting transfers between devices: 23.4 us -> 0 us
  between operations: 14.4 us -> 0.65 us
    ppermute x32 -> x0, waiting for transfers between devices: 463 us -> none  [shifted(): return lax.ppermute(value, axis, pairs)]
    dot_general x364 -> x0, matrix products: 218 us -> none  [the longest x40 50.9 us: up_project(): jnp.dot(compressed, value_up, preferred_element_type=jnp.float32)]
    all_gather x1 -> x0, waiting for transfers between devices: 123 us -> none  [shards(): gathered = lax.all_gather(latents, 'seq', axis=0, tiled=True)]
    pallas_call x0 -> x1, Pallas kernels: none -> 68.5 us  [shards(): pl.pallas_call(whole_kernel, out_shape=(shape((ROWS, 768)), shape((2, 288...]
    all_to_all x4 -> x0, waiting for transfers between devices: 60.2 us -> none  [the longest x3 42.5 us: from_everyone(): lax.all_to_all(jnp.broadcast_to(shard[None], (size, *shard.shape)), axis,...]
    add x71 -> x0, other arithmetic: 39 us -> none  [the longest x63 29.4 us: grad_block(): return (grads + part, q_acc + q_grad)]
    dynamic_slice x40 -> x0, local copies, waits for them, and re-layouts: 30.4 us -> none  [the longest x32 24.3 us: owner_pos(): return lax.dynamic_slice_in_dim(every_pos, owner_start(step), rows, 0)]
    all_to_all x4 -> x0, starting transfers between devices: 22.9 us -> none  [the longest x3 18.1 us: from_everyone(): lax.all_to_all(jnp.broadcast_to(shard[None], (size, *shard.shape)), axis,...]
  transfers between devices with their start and end apart: 37 -> 0, of which waited for: 37 -> 0; matrix products, arithmetic and copies ran while one was open for 5% -> 0% of each run, Pallas kernels for 0% -> 0%
where the time goes in v2:
time: 74.4 us; the launch traced here: 74.2 us
  Pallas kernels  68.5 us (92%)
  other arithmetic  3.3 us (4%)
  local copies, waits for them, and re-layouts  1.75 us (2%)
    pallas_call x1, Pallas kernels, shards(): pl.pallas_call(whole_kernel, out_shape=(shape((ROWS, 768)), shape((2, 288...  68.5 us
    convert_element_type x2, other arithmetic, shards(): return (qg, lg.reshape(576, ROWS).T, kug.astype(F32), vug.astype(F32))  3.3 us
    unnamed x8, local copies, waits for them, and re-layouts  1.75 us

profile of v2, /device:TPU:0, one launch (start us, length us, event | category | flops | bytes accessed | tf_op | source)
XLA Modules:
  0.0 74.2 jit_solution(4541061031962313136)
XLA Ops:
  0.6 68.5 %shard_map.93 = (bf16[128,768]{1,0:T(8,128)(2,1)}, f32[2,288,128]{2,1,0:T(8,128)}, bf16[512,512]{1,0:T(8,128)(2,1)}, bf16[512,512]{1,0:T(8,128)(2,1)}) custom-call(s32[128]{0:T(128)} %pos_ref.1, bf16[128,768]{1,0:T(8,128)(2,1)} %q_ref.1, bf16[576,128]{1,0:T(8,128)(2,1)} %bitcast.5, bf16[512,512]{1,0:T(8,128)(2,1)} %ku_ref.1, bf16[512,512]{1,0:T(8,128)(2,1)} %vu_ref.1, ...), custom_call_target="tpu_custom_call" | custom-call | tf_op jit(solution)/shard_map/pallas_call | solution.py:413
  69.1 0.0 copy-start
  69.1 2.2 %convert_element_type.6 = f32[512,512]{1,0:T(8,128)} convert(bf16[512,512]{1,0:T(8,128)(2,1)} %get-tuple-element.10) | non-fusion elementwise | flops 262144 | bytes 1572864 | tf_op jit(solution)/shard_map/convert_element_type | solution.py:428
  71.3 0.0 copy-done
  71.4 0.0 copy-start.2
  71.4 1.1 %convert_element_type.7 = f32[512,512]{1,0:T(8,128)} convert(bf16[512,512]{1,0:T(8,128)(2,1)S(1)} %copy-done) | non-fusion elementwise | flops 262144 | bytes 1572864 | tf_op jit(solution)/shard_map/convert_element_type | solution.py:428
  72.5 0.0 copy-done.2
  72.5 0.0 copy-start.1
  72.5 0.7 copy.12
  73.1 0.4 copy-done.1
  73.5 0.7 copy.13
Async XLA Ops:
  69.1 2.2 %copy-start = (bf16[512,512]{1,0:T(8,128)(2,1)S(1)}, bf16[512,512]{1,0:T(8,128)(2,1)}, u32[]{:S(2)}) copy-start(bf16[512,512]{1,0:T(8,128)(2,1)} %get-tuple-element.11) | copy-start | bytes 1572868
  71.4 1.1 %copy-start.2 = (bf16[128,768]{1,0:T(8,128)(2,1)S(1)}, bf16[128,768]{1,0:T(8,128)(2,1)}, u32[]{:S(2)}) copy-start(bf16[128,768]{1,0:T(8,128)(2,1)} %get-tuple-element.16) | copy-start | bytes 589828
  72.5 1.0 %copy-start.1 = (f32[2,288,128]{2,1,0:T(8,128)S(1)}, f32[2,288,128]{2,1,0:T(8,128)}, u32[]{:S(2)}) copy-start(f32[2,288,128]{2,1,0:T(8,128)} %get-tuple-element.9) | copy-start | bytes 884740

commit v3 on v2

--- a/solution.py
+++ b/solution.py
@@ -23,6 +23,7 @@
 KTOK = NY * NA * ROWS
 TILE = 256
 NEG = -1e30
+LIMIT = 52
 FLOOR = -1e29
 SCALE = 1.0 / math.sqrt(D_NOPE + D_ROPE)
 LOG2E = math.log2(math.e)
@@ -68,19 +69,21 @@
 
 
 def whole_kernel(
-    pos_ref, q_ref, latt_ref, ku_ref, vu_ref, g_ref,
-    qg_ref, lg_ref, kug_ref, vug_ref,
-    pq, pk, qb, kb, cl, kpos, s_all, dp_all, stl, sb, rows, dqa, dqs, rq, dka, dva, dks, rk,
-    lps, rlp, dqf, rdq, ups, rup, usk, usv, ugk, ugv, lsum, lhalf, rhalf, ly, ry_, lfin, rfin,
-    s_aq, r_aq, s_ak, r_ak, s_al, r_al, s_bq, r_bq, s_yk, r_yk, s_st, r_st, s_dq, r_dq, s_dk, r_dk,
-    s_lp, r_lp, s_qf, r_qf, s_up, r_up, s_ky, r_ky, s_kb, r_kb, s_ka, r_ka, s_vy, r_vy, s_va, r_va, s_vb, r_vb,
-    s_h, r_h,
+    pos_ref, q_hbm, latt_hbm, ku_hbm, vu_hbm, g_hbm,
+    qg_ref, lg_ref, ugk, ugv,
+    q_ref, latt_ref, ku_ref, vu_ref, g_ref,
+    pq, pk, qb, kb, cl, kpos, s_all, dp_all, stl, sb, rows, ds_all, dqs, rq, dka, dva, gs0, gs1, rg0, rg1,
+    dqf, rdq, ups, rup, usk, usv, lsum, lhalf, rhalf, hs, rh, lfin, rfin,
+    s_in, s_aq, r_aq, s_ak, r_ak, s_al, r_al, s_bq, r_bq, s_yk, r_yk, s_yl, r_yl, s_st, r_st, s_dq, r_dq,
+    s_g0, r_g0, s_g1, r_g1, s_qf, r_qf, s_up, r_up,
+    s_ky, r_ky, s_kb, r_kb, s_ka, r_ka, s_vy, r_vy, s_va, r_va, s_vb, r_vb, s_h, r_h,
 ):
     seq, head, y, a, b, dev = coords()
     core = head % 2
     twin = (seq, head + 1 - 2 * core)
     far = (seq, (head + 2) % 4)
     across = dev(a, b, 1 - y)
+    corner = (across[0], (head + 2) % 4)
     near = (1, 3, 2)
     others = [(e, f) for e in range(NB) for f in range(NY) if (e, f) != (0, 0)]
 
@@ -88,7 +91,7 @@
     for p in (
         [dev((a + d) % NA, b, y) for d in near]
         + [dev(a, (b + e) % NB, (y + f) % NY) for e, f in others]
-        + [twin, far]
+        + [twin, far, corner]
     ):
         pl.semaphore_signal(barrier, inc=1, device_id=p, device_id_type=MESH)
 
@@ -101,6 +104,17 @@
 
     def landed(ref, send, recv):
         rcopy(ref, ref, send, recv, across).wait_recv()
+
+    loads = [
+        pltpu.make_async_copy(src, dst, s_in.at[i])
+        for i, (src, dst) in enumerate(
+            [(latt_hbm, latt_ref), (ku_hbm, ku_ref), (vu_hbm, vu_ref), (q_hbm, q_ref), (g_hbm, g_ref)]
+        )
+    ]
+    for c in loads:
+        c.start()
+    for c in loads:
+        c.wait()
 
     stripe = lax.shift_right_logical(pos_ref[0], 7).astype(F32)
     lane = lax.broadcasted_iota(jnp.int32, (ROWS, 128), 1)
@@ -122,7 +136,7 @@
         pq[h, :, 128:256] = jnp.concatenate([q[:, 128:], q_tail], axis=1)
         pq[h, :, 256:384] = g_ref[:, h * 128 : (h + 1) * 128]
 
-    pl.semaphore_wait(barrier, 3 + len(others) + 2)
+    pl.semaphore_wait(barrier, 3 + len(others) + 3)
 
     for d in near:
         to = (a + d) % NA
@@ -132,10 +146,10 @@
     for e in near:
         go(pq.at[a], qb.at[b, a], s_bq.at[e - 1, 0], r_bq.at[b, 0], dev(a, (b + e) % NB, y))
     for d in near:
-        go(latt_ref.at[pl.ds(0, D_LAT)], cl.at[a], s_al.at[d - 1], r_al.at[d - 1], dev((a + d) % NA, b, y))
+        go(latt_ref.at[pl.ds(0, D_LAT)], cl.at[0, a], s_al.at[d - 1], r_al.at[d - 1], dev((a + d) % NA, b, y))
     qb[b, a] = pq[a]
     kb[0, a] = pk[a]
-    cl[a] = comp
+    cl[0, a] = comp
     for d in near:
         frm = (a + NA - d) % NA
         slot = kb.at[0, frm]
@@ -162,6 +176,12 @@
             for d in range(NA):
                 landed(qb.at[j, (a + NA - d) % NA], s_bq.at[0, d], r_bq.at[j, d])
 
+        if j == 2:
+            go(latt_ref.at[pl.ds(0, D_LAT)], cl.at[1, a], s_yl.at[0], r_yl.at[0], across)
+            for d in near:
+                slot = cl.at[0, (a + NA - d) % NA]
+                landed(slot, s_al.at[d - 1], r_al.at[d - 1])
+                go(slot, cl.at[1, (a + NA - d) % NA], s_yl.at[d], r_yl.at[d], across)
         for t in range(2):
             at = slice(t * TILE, (t + 1) * TILE)
             two = qb[j, 2 * t : 2 * t + 2].reshape(TILE, QW)
@@ -182,88 +202,98 @@
             go(stl.at[j], sb.at[j, b], s_st.at[e - 1, j], r_st.at[j, b], dev(a, (b + e) % NB, y))
 
     half = NA * ROWS
-    for j in range(NB):
-        sb[j, b] = stl[j]
-        for i in range(NB):
-
-            @pl.when(b != i)
-            def _():
-                landed(sb.at[j, i], s_st.at[0, j], r_st.at[j, i])
-
-        tops = [sb[j, i, 0:1, :] for i in range(NB)]
-        top = jnp.maximum(jnp.maximum(tops[0], tops[1]), jnp.maximum(tops[2], tops[3]))
-        fades = [jnp.exp2(t - top) for t in tops]
-        total = sum(f * sb[j, i, 1:2, :] for i, f in enumerate(fades))
-        rows[j, 1:2, :] = sum(f * sb[j, i, 2:3, :] for i, f in enumerate(fades)) / total
-        rows[j, 0:1, :] = top + jnp.log(total) * LOG2E
-
     for k in (1, 0):
         ks = slice(k * half, (k + 1) * half)
         for j in range(NB):
+            if k == 1:
+                sb[j, b] = stl[j]
+                for i in range(NB):
+
+                    @pl.when(b != i)
+                    def _():
+                        landed(sb.at[j, i], s_st.at[0, j], r_st.at[j, i])
+
+                tops = [sb[j, i, 0:1, :] for i in range(NB)]
+                top = jnp.maximum(jnp.maximum(tops[0], tops[1]), jnp.maximum(tops[2], tops[3]))
+                fades = [jnp.exp2(t - top) for t in tops]
+                total = sum(f * sb[j, i, 1:2, :] for i, f in enumerate(fades))
+                rows[j, 1:2, :] = sum(f * sb[j, i, 2:3, :] for i, f in enumerate(fades)) / total
+                rows[j, 0:1, :] = top + jnp.log(total) * LOG2E
             qall = qb[j].reshape(half, QW)
-            keys = kb[k].reshape(half, KW)
             p = jnp.exp2(s_all[j, ks, :] - rows[j, 0:1, :])
             ds = (p * (dp_all[j, ks, :] - rows[j, 1:2, :]) * SCALE).astype(BF16)
+            ds_all[j, ks, :] = ds
             dv = dot(p.astype(BF16), qall[:, 256:])
             dk = dot(ds, qall[:, :256])
-            dq = dot(ds, keys[:, :256], TN)
             if j == 0:
                 dva[ks, :] = dv
                 dka[ks, :] = dk
             else:
                 dva[ks, :] += dv
                 dka[ks, :] += dk
-            if k == 1:
-                dqa[j] = dq
-            else:
-                dqs[j] = (dqa[j] + dq).astype(BF16)
-
-                @pl.when(b != j)
-                def _():
-                    rcopy(dqs.at[j], rq.at[b], s_dq.at[j], r_dq.at[b], dev(a, j, y)).start()
-
         if k == 1:
-            dks[:, :256] = dka[half:, :].astype(BF16)
-            dks[:, 256:] = dva[half:, :].astype(BF16)
-            go(dks, rk, s_dk, r_dk, across)
-
-    for d in near:
-        landed(cl.at[(a + NA - d) % NA], s_al.at[d - 1], r_al.at[d - 1])
-    landed(rk, s_dk, r_dk)
-    dk = dka[:half, :] + rk[:, :256].astype(F32)
-    dv = dva[:half, :] + rk[:, 256:].astype(F32)
-    g = jnp.concatenate([dk[:, :128], dv], axis=1).astype(BF16)
-    mine_cols = pl.ds(pl.multiple_of(a * 128, 128), 128)
-    w = jnp.concatenate([ku_ref[:, mine_cols], vu_ref[:, mine_cols]], axis=1)
-    comps = jnp.concatenate([cl[i] for i in range(NA)], axis=1)
+            for i in range(NA):
+                at = slice(half + i * ROWS, half + (i + 1) * ROWS)
+                gs1[i, :, :128] = dka[at, :128].astype(BF16)
+                gs1[i, :, 128:] = dva[at, :].astype(BF16)
+            for d in near:
+                go(gs1.at[(a + d) % NA], rg1.at[a], s_g1.at[d - 1], r_g1.at[d - 1], dev((a + d) % NA, b, y))
+        else:
+            for i in range(NA):
+                at = slice(i * ROWS, (i + 1) * ROWS)
+                at1 = slice(half + i * ROWS, half + (i + 1) * ROWS)
+                gs0[i, :, :128] = dka[at, :128].astype(BF16)
+                gs0[i, :, 128:256] = dva[at, :].astype(BF16)
+                gs0[i, :, 256:] = jnp.concatenate([dka[at, 128:192], dka[at1, 128:192]], axis=1).astype(BF16)
+            for d in near:
+                go(gs0.at[(a + d) % NA], rg0.at[a], s_g0.at[d - 1], r_g0.at[d - 1], dev((a + d) % NA, b, y))
+
+    for d in (0, 1, 3, 2):
+        landed(cl.at[1, (a + NA - d) % NA], s_yl.at[d], r_yl.at[d])
+    g = jnp.concatenate([dka[:, :128], dva[...]], axis=1).astype(BF16)
+    comps = jnp.concatenate([cl[k, i] for k in range(NY) for i in range(NA)], axis=1)
     up = dot(comps, g)
     for i in range(NB * NY):
         ups[i] = up[i * 64 : (i + 1) * 64, :].astype(BF16)
-    lp = dot(w, g, NT)
-    rope = dot(eye, dk[:, 128:].astype(BF16), NT)
-    for i in range(NA):
-        lps[i, :D_LAT, :] = lp[:, i * 128 : (i + 1) * 128].astype(BF16)
-        lps[i, D_LAT:, :] = rope[:, i * 128 : (i + 1) * 128].astype(BF16)
     mine = b * NY + y
     for i, (e, f) in enumerate(others):
         tb, ty = (b + e) % NB, (y + f) % NY
         go(ups.at[tb * NY + ty], rup.at[mine], s_up.at[i], r_up.at[i], dev(a, tb, ty))
-    for d in near:
-        go(lps.at[(a + d) % NA], rlp.at[a], s_lp.at[d - 1], r_lp.at[d - 1], dev((a + d) % NA, b, y))
     rup[mine] = ups[mine]
-    rlp[a] = lps[a]
-
-    rq[b] = dqs[b]
+
+    keys = kb[...].reshape(KTOK, KW)
     for j in range(NB):
+        dq = dot(ds_all[j], keys[:, :256], TN).astype(BF16)
+        for i in range(NA):
+            part = dq[i * ROWS : (i + 1) * ROWS, :]
+            dqs[j, i, :ROWS, :] = part[:, :128]
+            dqs[j, i, ROWS:, :] = jnp.concatenate([part[:64, 128:192], part[64:, 128:192]], axis=1)
 
         @pl.when(b != j)
         def _():
-            landed(rq.at[j], s_dq.at[j], r_dq.at[j])
-
-    dqf[...] = sum(rq[j].astype(F32) for j in range(NB)).astype(BF16).reshape(NA, ROWS, 256)
-    for d in near:
-        go(dqf.at[(a + d) % NA], rdq.at[a], s_qf.at[d - 1], r_qf.at[d - 1], dev((a + d) % NA, b, y))
-    rdq[a] = dqf[a]
+            rcopy(dqs.at[j], rq.at[b], s_dq.at[j], r_dq.at[b], dev(a, j, y)).start()
+
+    rq[b] = dqs[b]
+    rg0[a] = gs0[a]
+    rg1[a] = gs1[a]
+
+    for d in near:
+        landed(rg1.at[(a + NA - d) % NA], s_g1.at[d - 1], r_g1.at[d - 1])
+        landed(rg0.at[(a + NA - d) % NA], s_g0.at[d - 1], r_g0.at[d - 1])
+    dk_all = jnp.concatenate(
+        [jnp.concatenate([r[h, :, :128] for h in range(NA)], axis=1) for r in (rg0, rg1)], axis=0
+    )
+    dv_all = jnp.concatenate(
+        [jnp.concatenate([r[h, :, 128:256] for h in range(NA)], axis=1) for r in (rg0, rg1)], axis=0
+    )
+    lp = dot(ku_ref[...], dk_all, NT) + dot(vu_ref[...], dv_all, NT)
+    rope = sum(rg0[h, :, 256:].astype(F32) for h in range(NA)).T
+    for k in range(NY):
+        whole = jnp.concatenate([lp[:, k * 128 : (k + 1) * 128], rope[k * 64 : (k + 1) * 64, :]], axis=0)
+        lsum[k] = whole.reshape(2, 288, ROWS)
+    for k in range(NY):
+        lhalf[k] = lsum[k, 1 - core].astype(BF16)
+    go(lhalf, rhalf, s_h.at[0], r_h.at[0], twin)
 
     for i, (e, f) in enumerate(others):
         fb, fy = (b + NB - e) % NB, (y + f) % NY
@@ -284,11 +314,12 @@
     for e in near:
         go(usv, ugv.at[a, mine], s_vb.at[e - 1, 0, 0], r_vb.at[e - 1, 0, 0], dev(a, (b + e) % NB, y))
 
-    for d in near:
-        landed(rlp.at[(a + NA - d) % NA], s_lp.at[d - 1], r_lp.at[d - 1])
-    lsum[...] = sum(rlp[i].astype(F32) for i in range(NA)).reshape(2, 288, 128)
-    lhalf[...] = lsum[1 - core].astype(BF16)
-    go(lhalf, rhalf, s_h.at[0], r_h.at[0], twin)
+    landed(rhalf, s_h.at[0], r_h.at[0])
+    for k in range(NY):
+        hs[k] = (lsum[k, core] + rhalf[k].astype(F32)).astype(BF16)
+    go(hs.at[0], rh.at[0], s_h.at[1], r_h.at[1], far)
+    go(hs.at[1], rh.at[1], s_h.at[2], r_h.at[2], across)
+    go(hs.at[1], rh.at[2], s_h.at[3], r_h.at[3], corner)
 
     def k_over_a(slot, e, f):
         for d in near:
@@ -308,10 +339,16 @@
     k_over_a(ugk.at[a, other], 0, 1)
     v_over_b(ugv.at[a, other], 0, 1)
 
-    landed(rhalf, s_h.at[0], r_h.at[0])
-    both = lsum[core] + rhalf[...].astype(F32)
-    ly[...] = both.astype(BF16)
-    go(ly, ry_, s_h.at[1], r_h.at[1], far)
+    for j in range(NB):
+
+        @pl.when(b != j)
+        def _():
+            landed(rq.at[j], s_dq.at[j], r_dq.at[j])
+
+    dqf[...] = sum(rq[j].astype(F32) for j in range(NB)).astype(BF16)
+    for d in near:
+        go(dqf.at[(a + d) % NA], rdq.at[a], s_qf.at[d - 1], r_qf.at[d - 1], dev((a + d) % NA, b, y))
+    rdq[a] = dqf[a]
 
     for f in range(NY):
         for e in near:
@@ -322,17 +359,19 @@
             landed(slot, s_va.at[e - 1, f], r_va.at[e - 1, f])
             v_over_b(slot, e, f)
 
-    landed(ry_, s_h.at[1], r_h.at[1])
-    whole = ly[...].astype(F32) + ry_[...].astype(F32)
+    for i in range(3):
+        landed(rh.at[i], s_h.at[1 + i], r_h.at[1 + i])
+    whole = hs[0].astype(F32) + rh[0].astype(F32) + rh[1].astype(F32) + rh[2].astype(F32)
     lfin[...] = whole
-    go(lfin, rfin, s_h.at[2], r_h.at[2], twin)
+    go(lfin, rfin, s_h.at[4], r_h.at[4], twin)
 
     for d in near:
         landed(rdq.at[(a + NA - d) % NA], s_qf.at[d - 1], r_qf.at[d - 1])
     for h in range(NA):
-        qg_ref[:, h * 192 : (h + 1) * 192] = rdq[h, :, :192]
-
-    landed(rfin, s_h.at[2], r_h.at[2])
+        rope = jnp.concatenate([rdq[h, ROWS:, :64], rdq[h, ROWS:, 64:]], axis=0)
+        qg_ref[:, h * 192 : (h + 1) * 192] = jnp.concatenate([rdq[h, :ROWS, :], rope], axis=1)
+
+    landed(rfin, s_h.at[4], r_h.at[4])
     lg_ref[core] = lfin[...]
     lg_ref[1 - core] = rfin[...]
 
@@ -348,9 +387,6 @@
                     ugv.at[(a + NA - e) % NA, (b + NB - d) % NB * NY + (y + f) % NY],
                     s_vb.at[d - 1, e, f], r_vb.at[d - 1, e, f],
                 )
-    for h in range(NA):
-        kug_ref[:, h * 128 : (h + 1) * 128] = ugk[h].reshape(D_LAT, 128)
-        vug_ref[:, h * 128 : (h + 1) * 128] = ugv[h].reshape(D_LAT, 128)
     for j in range(NB):
 
         @pl.when(b != j)
@@ -359,73 +395,112 @@
 
     for c in done:
         c.wait_send()
+
+
+def final_kernel(qg_in, lg_in, ugk, ugv, qg_ref, lg_ref, kug_ref, vug_ref, kf, vf, sem):
+    outs = [
+        pltpu.make_async_copy(qg_in, qg_ref, sem.at[0]),
+        pltpu.make_async_copy(lg_in, lg_ref, sem.at[1]),
+    ]
+    for c in outs:
+        c.start()
+    quarter = D_LAT // 4
+    for i in range(4):
+        at = pl.ds(i * quarter, quarter)
+        for n, (src, dst, out) in enumerate([(ugk, kf, kug_ref), (ugv, vf, vug_ref)]):
+            for h in range(NA):
+                dst[i * quarter : (i + 1) * quarter, h * 128 : (h + 1) * 128] = (
+                    src[h, 2 * i : 2 * i + 2].reshape(quarter, 128).astype(F32)
+                )
+            c = pltpu.make_async_copy(dst.at[at], out.at[at], sem.at[2 + 2 * i + n])
+            c.start()
+            outs.append(c)
+    for c in outs:
+        c.wait()
 
 
 def shards(queries, latents, key_up, value_up, out_grad, positions):
     half = NA * ROWS
     dma = pltpu.SemaphoreType.DMA
     scratch = [
+        pltpu.VMEM((ROWS, 768), BF16),
+        pltpu.VMEM((576, ROWS), BF16),
+        pltpu.VMEM((D_LAT, 512), BF16),
+        pltpu.VMEM((D_LAT, 512), BF16),
+        pltpu.VMEM((ROWS, 512), BF16),
         pltpu.VMEM((NA, ROWS, QW), BF16),
         pltpu.VMEM((NA, ROWS, KW), BF16),
         pltpu.VMEM((NB, NA, ROWS, QW), BF16),
         pltpu.VMEM((NY, NA, ROWS, KW), BF16),
-        pltpu.VMEM((NA, D_LAT, ROWS), BF16),
+        pltpu.VMEM((NY, NA, D_LAT, ROWS), BF16),
         pltpu.VMEM((KTOK, TILE), F32),
         pltpu.VMEM((NB, KTOK, half), F32),
         pltpu.VMEM((NB, KTOK, half), F32),
         pltpu.VMEM((NB, 8, half), F32),
         pltpu.VMEM((NB, NB, 8, half), F32),
         pltpu.VMEM((NB, 8, half), F32),
-        pltpu.VMEM((NB, half, 256), F32),
-        pltpu.VMEM((NB, half, 256), BF16),
-        pltpu.VMEM((NB, half, 256), BF16),
+        pltpu.VMEM((NB, KTOK, half), BF16),
+        pltpu.VMEM((NB, NA, 192, 128), BF16),
+        pltpu.VMEM((NB, NA, 192, 128), BF16),
         pltpu.VMEM((KTOK, 256), F32),
         pltpu.VMEM((KTOK, 128), F32),
-        pltpu.VMEM((half, KW), BF16),
-        pltpu.VMEM((half, KW), BF16),
-        pltpu.VMEM((NA, 576, ROWS), BF16),
-        pltpu.VMEM((NA, 576, ROWS), BF16),
+        pltpu.VMEM((NA, ROWS, 384), BF16),
         pltpu.VMEM((NA, ROWS, 256), BF16),
+        pltpu.VMEM((NA, ROWS, 384), BF16),
         pltpu.VMEM((NA, ROWS, 256), BF16),
+        pltpu.VMEM((NA, 192, 128), BF16),
+        pltpu.VMEM((NA, 192, 128), BF16),
         pltpu.VMEM((NB * NY, 64, 256), BF16),
         pltpu.VMEM((NB * NY, 64, 256), BF16),
         pltpu.VMEM((64, 128), BF16),
         pltpu.VMEM((64, 128), BF16),
-        pltpu.VMEM((NA, NB * NY, 64, 128), BF16),
-        pltpu.VMEM((NA, NB * NY, 64, 128), BF16),
-        pltpu.VMEM((2, 288, ROWS), F32),
-        pltpu.VMEM((288, ROWS), BF16),
-        pltpu.VMEM((288, ROWS), BF16),
-        pltpu.VMEM((288, ROWS), BF16),
-        pltpu.VMEM((288, ROWS), BF16),
+        pltpu.VMEM((NY, 2, 288, ROWS), F32),
+        pltpu.VMEM((NY, 288, ROWS), BF16),
+        pltpu.VMEM((NY, 288, ROWS), BF16),
+        pltpu.VMEM((NY, 288, ROWS), BF16),
+        pltpu.VMEM((3, 288, ROWS), BF16),
         pltpu.VMEM((288, ROWS), F32),
         pltpu.VMEM((288, ROWS), F32),
     ]
     sems = [
-        dma((3,)), dma((3,)), dma((3,)), dma((3,)), dma((3,)), dma((3,)),
+        dma((5,)), dma((3,)), dma((3,)), dma((3,)), dma((3,)), dma((3,)), dma((3,)),
+        dma((3, 4)), dma((4, 4)), dma((4,)), dma((4,)), dma((4,)), dma((4,)),
         dma((3, 4)), dma((4, 4)), dma((4,)), dma((4,)),
-        dma((3, 4)), dma((4, 4)), dma((4,)), dma((4,)), dma, dma,
-        dma((3,)), dma((3,)), dma((3,)), dma((3,)), dma((7,)), dma((7,)),
+        dma((3,)), dma((3,)), dma((3,)), dma((3,)), dma((3,)), dma((3,)), dma((7,)), dma((7,)),
         dma, dma, dma((3, 2)), dma((3, 2)), dma((3, 4, 2)), dma((3, 4, 2)),
         dma, dma, dma((3, 2)), dma((3, 2)), dma((3, 4, 2)), dma((3, 4, 2)),
-        dma((3,)), dma((3,)),
+        dma((5,)), dma((5,)),
     ]
-    qg, lg, kug, vug = pl.pallas_call(
+    hbm = pl.BlockSpec(memory_space=pltpu.HBM)
+    qg, lg, ugk, ugv = pl.pallas_call(
         whole_kernel,
         out_shape=(
             shape((ROWS, 768)),
             shape((2, 288, ROWS), F32),
-            shape((D_LAT, 512)),
-            shape((D_LAT, 512)),
+            shape((NA, NB * NY, 64, 128)),
+            shape((NA, NB * NY, 64, 128)),
         ),
-        in_specs=[SMEM] + [VMEM] * 5,
+        in_specs=[SMEM] + [hbm] * 5,
         out_specs=(VMEM,) * 4,
         scratch_shapes=scratch + sems,
         compiler_params=pltpu.CompilerParams(
-            collective_id=0, has_side_effects=True, vmem_limit_bytes=58 * 1024 * 1024
+            collective_id=0, has_side_effects=True, vmem_limit_bytes=LIMIT * 1024 * 1024
         ),
     )(positions, queries, latents.T, key_up, value_up, out_grad)
-    return (qg, lg.reshape(576, ROWS).T, kug.astype(F32), vug.astype(F32))
+    qg, lg, kug, vug = pl.pallas_call(
+        final_kernel,
+        out_shape=(
+            shape((ROWS, 768)),
+            shape((2, 288, ROWS), F32),
+            shape((D_LAT, 512), F32),
+            shape((D_LAT, 512), F32),
+        ),
+        in_specs=[VMEM] * 4,
+        out_specs=(hbm,) * 4,
+        scratch_shapes=[pltpu.VMEM((D_LAT, 512), F32), pltpu.VMEM((D_LAT, 512), F32), dma((10,))],
+        compiler_params=pltpu.CompilerParams(vmem_limit_bytes=8 * 1024 * 1024),
+    )(qg, lg, ugk, ugv)
+    return (qg, lg.reshape(576, ROWS).T, kug, vug)
 
 
 def solution(mesh):

time: 74.4 us -> 66.2 us (0.89)
  Pallas kernels: 68.5 us -> 61.5 us
  other arithmetic: 3.3 us -> 0 us
  local copies, waits for them, and re-layouts: 1.75 us -> 3.39 us
    pallas_call x1, Pallas kernels: 68.5 us -> 59.9 us  [shards(): pl.pallas_call(whole_kernel, out_shape=(shape((ROWS, 768)), shape((2, 288...]
    convert_element_type x2 -> x0, other arithmetic: 3.3 us -> none  [shards(): return (qg, lg.reshape(576, ROWS).T, kug.astype(F32), vug.astype(F32))]
    unnamed x8, local copies, waits for them, and re-layouts: 1.75 us -> 3.39 us
    pallas_call x0 -> x1, Pallas kernels: none -> 1.56 us  [shards(): pl.pallas_call(final_kernel, out_shape=(shape((ROWS, 768)), shape((2, 288...]
where the time goes in v3:
time: 66.2 us; the launch traced here: 65.5 us
  Pallas kernels  61.5 us (93%)
  local copies, waits for them, and re-layouts  3.39 us (5%)
    pallas_call x1, Pallas kernels, shards(): pl.pallas_call(whole_kernel, out_shape=(shape((ROWS, 768)), shape((2, 288...  59.9 us
    unnamed x8, local copies, waits for them, and re-layouts  3.39 us
    pallas_call x1, Pallas kernels, shards(): pl.pallas_call(final_kernel, out_shape=(shape((ROWS, 768)), shape((2, 288...  1.56 us

profile of v3, /device:TPU:0, one launch (start us, length us, event | category | flops | bytes accessed | tf_op | source)
XLA Modules:
  0.0 65.5 jit_solution(4601606062171140626)
XLA Ops:
  0.6 0.0 copy-start.3
  0.6 0.6 copy-done.3
  1.3 0.0 copy-start
  1.3 0.9 %copy-done = bf16[128,768]{1,0:T(8,128)(2,1)S(1)} copy-done((bf16[128,768]{1,0:T(8,128)(2,1)S(1)}, bf16[128,768]{1,0:T(8,128)(2,1)}, u32[]{:S(2)}) %copy-start) | copy-done | bytes 196632
  2.2 0.0 copy-start.1
  2.2 0.9 %copy-done.1 = bf16[128,576]{0,1:T(8,128)(2,1)S(1)} copy-done((bf16[128,576]{0,1:T(8,128)(2,1)S(1)}, bf16[128,576]{0,1:T(8,128)(2,1)}, u32[]{:S(2)}) %copy-start.1) | copy-done | bytes 147480
  3.1 0.0 copy-start.2
  3.1 0.9 %copy-done.2 = bf16[128,512]{1,0:T(8,128)(2,1)S(1)} copy-done((bf16[128,512]{1,0:T(8,128)(2,1)S(1)}, bf16[128,512]{1,0:T(8,128)(2,1)}, u32[]{:S(2)}) %copy-start.2) | copy-done | bytes 131096
  4.0 59.9 %shard_map.93 = (bf16[128,768]{1,0:T(8,128)(2,1)S(1)}, f32[2,288,128]{2,1,0:T(8,128)S(1)}, bf16[4,8,64,128]{3,2,1,0:T(8,128)(2,1)S(1)}, bf16[4,8,64,128]{3,2,1,0:T(8,128)(2,1)S(1)}) custom-call(s32[128]{0:T(128)S(1)} %copy-done.3, bf16[128,768]{1,0:T(8,128)(2,1)S(1)} %copy-done, bf16[576,128]{1,0:T(8,128)(2,1)S(1)} %bitcast.4, bf16[512,512]{1,0:T(8,128)(2,1)} %ku_hbm.1, ...), custom_call_target="tpu_custom_call" | custom-call | tf_op jit(solution)/shard_map/pallas_call | solution.py:475
  64.0 1.6 %shard_map.94 = (bf16[128,768]{1,0:T(8,128)(2,1)}, f32[2,288,128]{2,1,0:T(8,128)}, f32[512,512]{1,0:T(8,128)}, f32[512,512]{1,0:T(8,128)}) custom-call(bf16[128,768]{1,0:T(8,128)(2,1)S(1)} %get-tuple-element.12.qg_in, f32[2,288,128]{2,1,0:T(8,128)S(1)} %get-tuple-element.13.lg_in, bf16[4,8,64,128]{3,2,1,0:T(8,128)(2,1)S(1)} %get-tuple-element.14.ugk, ...), custom_call_target="tpu_custom_call" | custom-call | tf_op jit(solution)/shard_map/pallas_call | solution.py:490
Async XLA Ops:
  0.6 0.7 %copy-start.3 = (s32[128]{0:T(128)S(1)}, s32[128]{0:T(128)}, u32[]{:S(2)}) copy-start(s32[128]{0:T(128)} %pos_ref.1) | copy-start | bytes 1540
  1.3 0.9 %copy-start = (bf16[128,768]{1,0:T(8,128)(2,1)S(1)}, bf16[128,768]{1,0:T(8,128)(2,1)}, u32[]{:S(2)}) copy-start(bf16[128,768]{1,0:T(8,128)(2,1)} %q_hbm.1) | copy-start | bytes 589828
  2.2 0.9 %copy-start.1 = (bf16[128,576]{0,1:T(8,128)(2,1)S(1)}, bf16[128,576]{0,1:T(8,128)(2,1)}, u32[]{:S(2)}) copy-start(bf16[128,576]{0,1:T(8,128)(2,1)} %param.7) | copy-start | bytes 442372
  3.1 0.9 %copy-start.2 = (bf16[128,512]{1,0:T(8,128)(2,1)S(1)}, bf16[128,512]{1,0:T(8,128)(2,1)}, u32[]{:S(2)}) copy-start(bf16[128,512]{1,0:T(8,128)(2,1)} %g_hbm.1) | copy-start | bytes 393220

commit v4 on v3

v4 whole, which is shorter than its diff:
```python
import math

import jax
import jax.numpy as jnp
from jax import lax
from jax.experimental import pallas as pl
from jax.experimental.pallas import tpu as pltpu
from jax.sharding import PartitionSpec as P


D_LAT = 512
D_ROPE = 64
D_NOPE = 128
D_V = 128
ROWS = 128
NA = 4
NB = 4
NY = 2
BLOCK = 336
KTOK = NY * NA * ROWS
TILE = 256
NEG = -1e30
LIMIT = 60
FLOOR = -1e29
SCALE = 1.0 / math.sqrt(D_NOPE + D_ROPE)
LOG2E = math.log2(math.e)
MESH = pl.DeviceIdType.MESH
F32 = jnp.float32
BF16 = jnp.bfloat16
VMEM = pl.BlockSpec(memory_space=pltpu.VMEM)
SMEM = pl.BlockSpec(memory_space=pltpu.SMEM)
NT = (((1,), (1,)), ((), ()))
TN = (((0,), (0,)), ((), ()))


def coords():
    seq = lax.axis_index("seq")
    head = lax.axis_index("head")
    core = head % 2
    y = seq // 16
    z = (seq // 4) % 4
    x = seq % 4
    a = x + core * (z - x)
    b = z + core * (x - z)
    sa = 1 + 3 * core
    sb = 4 - 3 * core

    def dev(a2, b2, y2):
        return (y2 * 16 + a2 * sa + b2 * sb, head)

    return seq, head, y, a, b, dev


def rcopy(src, dst, send, recv, device):
    return pltpu.make_async_remote_copy(
        src_ref=src, dst_ref=dst, send_sem=send, recv_sem=recv, device_id=device, device_id_type=MESH
    )


def dot(u, v, dims=(((1,), (0,)), ((), ()))):
    return lax.dot_general(u, v, dims, preferred_element_type=F32)


def shape(dims, dtype=BF16):
    return jax.ShapeDtypeStruct(dims, dtype)


def whole_kernel(
    pos_ref, q_hbm, latt_hbm, ku_hbm, vu_hbm, g_hbm,
    qg_hbm, lg_hbm, ugk_hbm, ugv_hbm,
    q_ref, latt_ref, ku_ref, vu_ref, g_ref,
    pq, pk, qb, kb, qp, kp, kpt, cl, kpos, s_all, dp_all, stl, sb, rows, ds_all, dqs, rq, dka, dva, gs0, gs1, rg0, rg1,
    dqf, rdq, ups, rup, usk, usv, lsum, lhalf, rhalf, hs, rh, lfin, rfin, qg_ref, ugk, ugv,
    s_in, s_aq, r_aq, s_ak, r_ak, s_al, r_al, s_bq, r_bq, s_yk, r_yk, s_yl, r_yl, s_st, r_st, s_dq, r_dq,
    s_g0, r_g0, s_g1, r_g1, s_qf, r_qf, s_up, r_up,
    s_kb, r_kb, s_ka, r_ka, s_va, r_va, s_vb, r_vb, s_h, r_h, s_out,
):
    seq, head, y, a, b, dev = coords()
    core = head % 2
    twin = (seq, head + 1 - 2 * core)
    far = (seq, (head + 2) % 4)
    across = dev(a, b, 1 - y)
    corner = (across[0], (head + 2) % 4)
    near = (1, 3, 2)
    others = [(0, 1), (1, 0), (1, 1), (2, 0), (2, 1), (3, 0), (3, 1)]
    by_reach = (1, 5, 0, 3, 2, 6, 4)

    barrier = pltpu.get_barrier_semaphore()
    for p in (
        [dev((a + d) % NA, b, y) for d in near]
        + [dev(a, (b + e) % NB, (y + f) % NY) for e, f in others]
        + [dev((a + d) % NA, b, 1 - y) for d in near]
        + [twin, far, corner]
    ):
        pl.semaphore_signal(barrier, inc=1, device_id=p, device_id_type=MESH)

    done = []

    def go(src, dst, send, recv, device):
        c = rcopy(src, dst, send, recv, device)
        c.start()
        done.append(c)

    def landed(ref, send, recv):
        rcopy(ref, ref, send, recv, across).wait_recv()

    loads = [
        pltpu.make_async_copy(src, dst, s_in.at[i])
        for i, (src, dst) in enumerate(
            [(latt_hbm, latt_ref), (ku_hbm, ku_ref), (vu_hbm, vu_ref), (q_hbm, q_ref), (g_hbm, g_ref)]
        )
    ]
    for c in loads:
        c.start()
    for c in loads:
        c.wait()

    stripe = lax.shift_right_logical(pos_ref[0], 7).astype(F32)
    stripes = jnp.full((16, 128), stripe, F32).astype(BF16)
    comp = latt_ref[:D_LAT, :]
    kn = dot(comp, ku_ref[...], TN).astype(BF16)
    vv = dot(comp, vu_ref[...], TN).astype(BF16)
    eye = (
        lax.broadcasted_iota(jnp.int32, (64, 128), 0) == lax.broadcasted_iota(jnp.int32, (64, 128), 1)
    ).astype(F32).astype(BF16)
    k_rope = dot(latt_ref[D_LAT:, :], eye, TN).astype(BF16)
    k_rope = jnp.concatenate([k_rope[:64, :64], k_rope[64:, :64]], axis=1)
    for h in range(NA):
        pk[h, 0:128, :] = kn[:, h * 128 : (h + 1) * 128]
        pk[h, 128:256, :] = vv[:, h * 128 : (h + 1) * 128]
        pk[h, 256:320, :] = k_rope
        pk[h, 320:, :] = stripes
        q = q_ref[:, h * 192 : (h + 1) * 192]
        pq[h, 0:128, :] = q[:, :128]
        pq[h, 128:256, :] = g_ref[:, h * 128 : (h + 1) * 128]
        pq[h, 256:320, :] = jnp.concatenate([q[:64, 128:], q[64:, 128:]], axis=1)
        pq[h, 320:, :] = stripes

    pl.semaphore_wait(barrier, 6 + len(others) + 3)

    def on_a(d):
        return dev((a + d) % NA, b, y)

    def on_b(e):
        return dev(a, (b + e) % NB, y)

    for d in near:
        to = (a + d) % NA
        go(pk.at[to], kb.at[0, d], s_ak.at[d - 1], r_ak.at[d - 1], on_a(d))
        go(pq.at[to], qb.at[0, d], s_aq.at[d - 1], r_aq.at[d - 1], on_a(d))
    go(pk.at[a], kb.at[1, 0], s_yk.at[0], r_yk.at[0], across)
    for e in near:
        go(pq.at[a], qb.at[e, 0], s_bq.at[e - 1, 0], r_bq.at[e - 1, 0], on_b(e))
    qb[0, 0] = pq[a]
    kb[0, 0] = pk[a]
    cl[0, 0] = comp
    for d in near:
        landed(kb.at[0, d], s_ak.at[d - 1], r_ak.at[d - 1])
        go(kb.at[0, d], kb.at[1, d], s_yk.at[d], r_yk.at[d], across)
        landed(qb.at[0, d], s_aq.at[d - 1], r_aq.at[d - 1])
        for e in near:
            go(qb.at[0, d], qb.at[e, d], s_bq.at[e - 1, d], r_bq.at[e - 1, d], on_b(e))
    go(latt_ref.at[pl.ds(0, D_LAT)], cl.at[1, 0], s_yl, r_yl, across)

    half = NA * ROWS
    row = lax.broadcasted_iota(jnp.int32, (ROWS, TILE), 0).astype(F32)
    col = lax.broadcasted_iota(jnp.int32, (1, ROWS), 1).astype(F32)
    blank = jnp.zeros((ROWS, 64), BF16)
    pairs = ((0, 1), (3, 2))

    def wide(block):
        rope = jnp.concatenate([block[256:320, :64], block[256:320, 64:]], axis=0)
        return jnp.concatenate([block[:128, :], rope, blank], axis=1)

    def open_keys(k):
        for d in range(NA):
            at = slice(d * ROWS, (d + 1) * ROWS)
            block = kb[k, d]
            kp[k, at, :] = wide(block)
            stripe = block[320:321, :].astype(F32) * 128.0
            kpos[k, at, :] = jnp.concatenate([stripe, stripe], axis=1) + row

    def open_queries(e, t):
        for i, d in enumerate(pairs[t]):
            at = slice(t * TILE + i * ROWS, t * TILE + (i + 1) * ROWS)
            qp[e, at, :] = wide(qb[e, d])

    def wait_q(e, t):
        for d in pairs[t]:
            landed(qb.at[e, d], s_bq.at[e - 1, d], r_bq.at[e - 1, d])

    def grads_of(e, t):
        d0, d1 = pairs[t]
        return jnp.concatenate([qb[e, d0, 128:256, :], qb[e, d1, 128:256, :]], axis=0)

    def unit(k, e, t, first):
        at = slice(t * TILE, (t + 1) * TILE)
        if first:
            open_queries(e, t)
        qpos = jnp.concatenate([qb[e, d, 320:321, :].astype(F32) * 128.0 + col for d in pairs[t]], axis=1)
        raw = dot(kp[k], qp[e, at, :], NT)
        s = jnp.where(kpos[k] <= qpos, raw * (SCALE * LOG2E), NEG)
        s_all[k, e, :, at] = s
        dp = dot(kb[k, :, 128:256, :].reshape(half, 128), grads_of(e, t), NT)
        dp_all[k, e, :, at] = dp
        top = jnp.max(s, axis=0, keepdims=True)
        if not first:
            old = stl[e, 0:1, at]
            top = jnp.maximum(top, old)
        w = jnp.exp2(s - jnp.maximum(top, FLOOR))
        total = jnp.sum(w, axis=0, keepdims=True)
        weighted = jnp.sum(w * dp, axis=0, keepdims=True)
        if not first:
            fade = jnp.exp2(old - top)
            total = total + fade * stl[e, 1:2, at]
            weighted = weighted + fade * stl[e, 2:3, at]
        stl[e, 0:1, at] = top
        stl[e, 1:2, at] = total
        stl[e, 2:3, at] = weighted

    def tell(e):
        for g in near:
            go(stl.at[e], sb.at[(e + g) % NB, g], s_st.at[e, g - 1], r_st.at[(e + g) % NB, g - 1], on_b(g))

    stl[...] = jnp.zeros_like(stl)
    open_keys(0)
    unit(0, 0, 0, True)
    unit(0, 0, 1, True)
    for e in near:
        wait_q(e, 0)
        unit(0, e, 0, True)
    for d in (0, 1, 3, 2):
        landed(kb.at[1, d], s_yk.at[d], r_yk.at[d])
    open_keys(1)
    unit(1, 0, 0, False)
    unit(1, 0, 1, False)
    tell(0)
    for e in near:
        unit(1, e, 0, False)
    for e in near:
        wait_q(e, 1)
        if e == 2:
            landed(cl.at[1, 0], s_yl, r_yl)
            for d in near:
                go(latt_ref.at[pl.ds(0, D_LAT)], cl.at[0, d], s_al.at[0, d - 1], r_al.at[0, d - 1], on_a(d))
                go(cl.at[1, 0], cl.at[1, d], s_al.at[1, d - 1], r_al.at[1, d - 1], on_a(d))
        unit(0, e, 1, True)
        unit(1, e, 1, False)
        tell(e)
    kpt[...] = kp[...].reshape(KTOK, 256).T

    for k in (1, 0):
        ks = slice(k * half, (k + 1) * half)
        for n, e in enumerate((0, 1, 3, 2)):
            if k == 1:
                for g in near:
                    landed(sb.at[e, g], s_st.at[e, g - 1], r_st.at[e, g - 1])
                got = [stl[e]] + [sb[e, g] for g in near]
                tops = [r[0:1, :] for r in got]
                top = jnp.maximum(jnp.maximum(tops[0], tops[1]), jnp.maximum(tops[2], tops[3]))
                fades = [jnp.exp2(t - top) for t in tops]
                total = sum(f * r[1:2, :] for f, r in zip(fades, got))
                rows[e, 1:2, :] = sum(f * r[2:3, :] for f, r in zip(fades, got)) / total
                rows[e, 0:1, :] = top + jnp.log(total) * LOG2E
            grads = jnp.concatenate([grads_of(e, 0), grads_of(e, 1)], axis=0)
            p = jnp.exp2(s_all[k, e] - rows[e, 0:1, :])
            ds = (p * (dp_all[k, e] - rows[e, 1:2, :]) * SCALE).astype(BF16)
            ds_all[e, ks, :] = ds
            dv = dot(p.astype(BF16), grads)
            dk = dot(ds, qp[e])
            if n == 0:
                dva[ks, :] = dv
                dka[ks, :] = dk
            else:
                dva[ks, :] += dv
                dka[ks, :] += dk
        if k == 1:
            for d in range(NA):
                at = slice(half + d * ROWS, half + (d + 1) * ROWS)
                gs1[d, :, :128] = dka[at, :128].astype(BF16)
                gs1[d, :, 128:] = dva[at, :].astype(BF16)
            for d in near:
                go(gs1.at[d], rg1.at[a], s_g1.at[d - 1], r_g1.at[d - 1], on_a(NA - d))
        else:
            for d in range(NA):
                at = slice(d * ROWS, (d + 1) * ROWS)
                at1 = slice(half + d * ROWS, half + (d + 1) * ROWS)
                gs0[d, :, :128] = dka[at, :128].astype(BF16)
                gs0[d, :, 128:256] = dva[at, :].astype(BF16)
                gs0[d, :, 256:] = jnp.concatenate([dka[at, 128:192], dka[at1, 128:192]], axis=1).astype(BF16)
            for d in near:
                go(gs0.at[d], rg0.at[a], s_g0.at[d - 1], r_g0.at[d - 1], on_a(NA - d))

    for d in near:
        for k in range(NY):
            landed(cl.at[k, d], s_al.at[k, d - 1], r_al.at[k, d - 1])
    g = jnp.concatenate([dka[:, :128], dva[...]], axis=1).astype(BF16)
    comps = jnp.concatenate([cl[k, i] for k in range(NY) for i in range(NA)], axis=1)
    up = dot(comps, g)
    for i in range(NB * NY):
        ups[i] = up[i * 64 : (i + 1) * 64, :].astype(BF16)
    mine = b * NY + y
    for i, (e, f) in enumerate(others):
        tb, ty = (b + e) % NB, (y + f) % NY
        go(ups.at[tb * NY + ty], rup.at[mine], s_up.at[i], r_up.at[i], dev(a, tb, ty))
    rup[mine] = ups[mine]

    for e in (2, 1, 3, 0):
        dq = dot(kpt[:192, :], ds_all[e]).astype(BF16)
        for t, (d0, d1) in enumerate(pairs):
            dqs[e, d0] = dq[:, t * TILE : t * TILE + ROWS]
            dqs[e, d1] = dq[:, t * TILE + ROWS : (t + 1) * TILE]
        if e:
            go(dqs.at[e], rq.at[e], s_dq.at[e], r_dq.at[e], on_b(NB - e))
    rg0[a] = gs0[0]
    rg1[a] = gs1[0]

    for d in near:
        landed(rg1.at[(a + d) % NA], s_g1.at[d - 1], r_g1.at[d - 1])
        landed(rg0.at[(a + d) % NA], s_g0.at[d - 1], r_g0.at[d - 1])
    dk_all = jnp.concatenate(
        [jnp.concatenate([r[h, :, :128] for h in range(NA)], axis=1) for r in (rg0, rg1)], axis=0
    )
    dv_all = jnp.concatenate(
        [jnp.concatenate([r[h, :, 128:256] for h in range(NA)], axis=1) for r in (rg0, rg1)], axis=0
    )
    lp = dot(ku_ref[...], dk_all, NT) + dot(vu_ref[...], dv_all, NT)
    rope = sum(rg0[h, :, 256:].astype(F32) for h in range(NA)).T
    for k in range(NY):
        whole = jnp.concatenate([lp[:, k * 128 : (k + 1) * 128], rope[k * 64 : (k + 1) * 64, :]], axis=0)
        lsum[k] = whole.reshape(2, 288, ROWS)
    for k in range(NY):
        lhalf[k] = lsum[k, 1 - core].astype(BF16)
    go(lhalf, rhalf, s_h.at[0], r_h.at[0], twin)

    for i, (e, f) in enumerate(others):
        fb, fy = (b + NB - e) % NB, (y + f) % NY
        landed(rup.at[fb * NY + fy], s_up.at[i], r_up.at[i])
    us = sum(rup[i].astype(F32) for i in range(NB * NY)).astype(BF16)
    usk[...] = us[:, :128]
    usv[...] = us[:, 128:]
    ugk[a, mine] = us[:, :128]
    ugv[a, mine] = us[:, 128:]
    for i, (e, f) in enumerate(others):
        fy = (y + f) % NY
        go(usk, ugk.at[a, mine], s_kb.at[i], r_kb.at[i], dev(a, (b + e) % NB, fy))
        go(usv, ugv.at[a, mine], s_va.at[i], r_va.at[i], dev((a + e) % NA, b, fy))

    def k_over_a(slot, i):
        for d in near:
            go(slot, slot, s_ka.at[d - 1, i], r_ka.at[d - 1, i], dev((a + d) % NA, b, y))

    def v_over_b(slot, i):
        for d in near:
            go(slot, slot, s_vb.at[d - 1, i], r_vb.at[d - 1, i], dev(a, (b + d) % NB, y))

    k_over_a(ugk.at[a, mine], 7)
    v_over_b(ugv.at[a, mine], 7)

    landed(rhalf, s_h.at[0], r_h.at[0])
    for k in range(NY):
        hs[k] = (lsum[k, core] + rhalf[k].astype(F32)).astype(BF16)
    go(hs.at[0], rh.at[0], s_h.at[1], r_h.at[1], far)
    go(hs.at[1], rh.at[1], s_h.at[2], r_h.at[2], across)
    go(hs.at[1], rh.at[2], s_h.at[3], r_h.at[3], corner)

    for e in near:
        landed(rq.at[e], s_dq.at[e], r_dq.at[e])
    dqf[...] = (dqs[0].astype(F32) + sum(rq[e].astype(F32) for e in near)).astype(BF16)
    for d in near:
        go(dqf.at[d], rdq.at[a], s_qf.at[d - 1], r_qf.at[d - 1], on_a(NA - d))
    rdq[a] = dqf[0]

    def piece(i, axis):
        e, f = others[i]
        if axis == "b":
            return (b + NB - e) % NB * NY + (y + f) % NY
        return (a + NA - e) % NA, (y + f) % NY

    for i in by_reach:
        slot = ugk.at[a, piece(i, "b")]
        landed(slot, s_kb.at[i], r_kb.at[i])
        k_over_a(slot, i)
        fa, fy = piece(i, "a")
        slot = ugv.at[fa, b * NY + fy]
        landed(slot, s_va.at[i], r_va.at[i])
        v_over_b(slot, i)

    for i in range(3):
        landed(rh.at[i], s_h.at[1 + i], r_h.at[1 + i])
    whole = hs[0].astype(F32) + rh[0].astype(F32) + rh[1].astype(F32) + rh[2].astype(F32)
    lfin[...] = whole
    go(lfin, rfin, s_h.at[4], r_h.at[4], twin)

    for d in near:
        landed(rdq.at[(a + d) % NA], s_qf.at[d - 1], r_qf.at[d - 1])
    for h in range(NA):
        qg_ref[:, h * 192 : (h + 1) * 192] = rdq[h].T

    outs = []

    def write(src, dst):
        c = pltpu.make_async_copy(src, dst, s_out.at[len(outs)])
        c.start()
        outs.append(c)

    write(qg_ref, qg_hbm)
    landed(rfin, s_h.at[4], r_h.at[4])
    write(lfin, lg_hbm.at[core])
    write(rfin, lg_hbm.at[1 - core])
    write(ugk.at[a], ugk_hbm.at[a])
    own_b = pl.ds(b * NY, NY)
    write(ugv.at[:, own_b], ugv_hbm.at[:, own_b])

    for d in near:
        fa, fb = (a + NA - d) % NA, (b + NB - d) % NB
        for i in range(8):
            p = mine if i == 7 else piece(i, "b")
            landed(ugk.at[fa, p], s_ka.at[d - 1, i], r_ka.at[d - 1, i])
            pa, py = (a, y) if i == 7 else piece(i, "a")
            landed(ugv.at[pa, fb * NY + py], s_vb.at[d - 1, i], r_vb.at[d - 1, i])
        write(ugk.at[fa], ugk_hbm.at[fa])
        from_b = pl.ds(fb * NY, NY)
        write(ugv.at[:, from_b], ugv_hbm.at[:, from_b])
    for c in outs:
        c.wait()
    for c in done:
        c.wait_send()


def final_kernel(
    qg_hbm, lg_hbm, ugk_hbm, ugv_hbm, qg_ref, lg_ref, kug_ref, vug_ref, qv, lv, kv, vv, kf, vf, s_in, s_out
):
    quarter = D_LAT // 4
    loads, outs = [], []

    def start(pile, src, dst, sem):
        c = pltpu.make_async_copy(src, dst, sem)
        c.start()
        pile.append(c)

    for i in range(4):
        at = pl.ds(2 * i, 2)
        start(loads, ugk_hbm.at[:, at], kv.at[:, at], s_in.at[2 * i])
        start(loads, ugv_hbm.at[:, at], vv.at[:, at], s_in.at[2 * i + 1])
    start(loads, qg_hbm, qv, s_in.at[8])
    start(loads, lg_hbm, lv, s_in.at[9])
    for i in range(4):
        at = pl.ds(i * quarter, quarter)
        for n, (src, dst, out) in enumerate([(kv, kf, kug_ref), (vv, vf, vug_ref)]):
            loads[2 * i + n].wait()
            for h in range(NA):
                dst[i * quarter : (i + 1) * quarter, h * 128 : (h + 1) * 128] = (
                    src[h, 2 * i : 2 * i + 2].reshape(quarter, 128).astype(F32)
                )
            start(outs, dst.at[at], out.at[at], s_out.at[2 * i + n])
    loads[8].wait()
    start(outs, qv, qg_ref, s_out.at[8])
    loads[9].wait()
    start(outs, lv, lg_ref, s_out.at[9])
    for c in outs:
        c.wait()


def shards(queries, latents, key_up, value_up, out_grad, positions):
    half = NA * ROWS
    dma = pltpu.SemaphoreType.DMA
    scratch = [
        pltpu.VMEM((ROWS, 768), BF16),
        pltpu.VMEM((576, ROWS), BF16),
        pltpu.VMEM((D_LAT, 512), BF16),
        pltpu.VMEM((D_LAT, 512), BF16),
        pltpu.VMEM((ROWS, 512), BF16),
        pltpu.VMEM((NA, BLOCK, 128), BF16),
        pltpu.VMEM((NA, BLOCK, 128), BF16),
        pltpu.VMEM((NB, NA, BLOCK, 128), BF16),
        pltpu.VMEM((NY, NA, BLOCK, 128), BF16),
        pltpu.VMEM((NB, half, 256), BF16),
        pltpu.VMEM((NY, half, 256), BF16),
        pltpu.VMEM((256, KTOK), BF16),
        pltpu.VMEM((NY, NA, D_LAT, ROWS), BF16),
        pltpu.VMEM((NY, half, TILE), F32),
        pltpu.VMEM((NY, NB, half, half), F32),
        pltpu.VMEM((NY, NB, half, half), F32),
        pltpu.VMEM((NB, 8, half), F32),
        pltpu.VMEM((NB, NB, 8, half), F32),
        pltpu.VMEM((NB, 8, half), F32),
        pltpu.VMEM((NB, KTOK, half), BF16),
        pltpu.VMEM((NB, NA, 192, 128), BF16),
        pltpu.VMEM((NB, NA, 192, 128), BF16),
        pltpu.VMEM((KTOK, 256), F32),
        pltpu.VMEM((KTOK, 128), F32),
        pltpu.VMEM((NA, ROWS, 384), BF16),
        pltpu.VMEM((NA, ROWS, 256), BF16),
        pltpu.VMEM((NA, ROWS, 384), BF16),
        pltpu.VMEM((NA, ROWS, 256), BF16),
        pltpu.VMEM((NA, 192, 128), BF16),
        pltpu.VMEM((NA, 192, 128), BF16),
        pltpu.VMEM((NB * NY, 64, 256), BF16),
        pltpu.VMEM((NB * NY, 64, 256), BF16),
        pltpu.VMEM((64, 128), BF16),
        pltpu.VMEM((64, 128), BF16),
        pltpu.VMEM((NY, 2, 288, ROWS), F32),
        pltpu.VMEM((NY, 288, ROWS), BF16),
        pltpu.VMEM((NY, 288, ROWS), BF16),
        pltpu.VMEM((NY, 288, ROWS), BF16),
        pltpu.VMEM((3, 288, ROWS), BF16),
        pltpu.VMEM((288, ROWS), F32),
        pltpu.VMEM((288, ROWS), F32),
        pltpu.VMEM((ROWS, 768), BF16),
        pltpu.VMEM((NA, NB * NY, 64, 128), BF16),
        pltpu.VMEM((NA, NB * NY, 64, 128), BF16),
    ]
    sems = [
        dma((5,)), dma((3,)), dma((3,)), dma((3,)), dma((3,)), dma((2, 3)), dma((2, 3)),
        dma((3, 4)), dma((3, 4)), dma((4,)), dma((4,)), dma, dma,
        dma((4, 3)), dma((4, 3)), dma((4,)), dma((4,)),
        dma((3,)), dma((3,)), dma((3,)), dma((3,)), dma((3,)), dma((3,)), dma((7,)), dma((7,)),
        dma((7,)), dma((7,)), dma((3, 8)), dma((3, 8)), dma((7,)), dma((7,)), dma((3, 8)), dma((3, 8)),
        dma((5,)), dma((5,)), dma((11,)),
    ]
    hbm = pl.BlockSpec(memory_space=pltpu.HBM)
    qg, lg, ugk, ugv = pl.pallas_call(
        whole_kernel,
        out_shape=(
            shape((ROWS, 768)),
            shape((2, 288, ROWS), F32),
            shape((NA, NB * NY, 64, 128)),
            shape((NA, NB * NY, 64, 128)),
        ),
        in_specs=[SMEM] + [hbm] * 5,
        out_specs=(hbm,) * 4,
        scratch_shapes=scratch + sems,
        compiler_params=pltpu.CompilerParams(
            collective_id=0, has_side_effects=True, vmem_limit_bytes=LIMIT * 1024 * 1024
        ),
    )(positions, queries, latents.T, key_up, value_up, out_grad)
    qg, lg, kug, vug = pl.pallas_call(
        final_kernel,
        out_shape=(
            shape((ROWS, 768)),
            shape((2, 288, ROWS), F32),
            shape((D_LAT, 512), F32),
            shape((D_LAT, 512), F32),
        ),
        in_specs=[hbm] * 4,
        out_specs=(hbm,) * 4,
        scratch_shapes=[
            pltpu.VMEM((ROWS, 768), BF16),
            pltpu.VMEM((2, 288, ROWS), F32),
            pltpu.VMEM((NA, NB * NY, 64, 128), BF16),
            pltpu.VMEM((NA, NB * NY, 64, 128), BF16),
            pltpu.VMEM((D_LAT, 512), F32),
            pltpu.VMEM((D_LAT, 512), F32),
            dma((10,)),
            dma((10,)),
        ],
        compiler_params=pltpu.CompilerParams(vmem_limit_bytes=LIMIT * 1024 * 1024),
    )(qg, lg, ugk, ugv)
    return (qg, lg.reshape(576, ROWS).T, kug, vug)


def solution(mesh):
    in_specs = (
        P("seq", "head"),
        P("seq", None),
        P(None, "head"),
        P(None, "head"),
        P("seq", "head"),
        P("seq"),
    )
    out_specs = (P("seq", "head"), P("seq", None), P(None, "head"), P(None, "head"))
    return jax.shard_map(shards, mesh=mesh, in_specs=in_specs, out_specs=out_specs, check_vma=False)
```

time: 66.2 us -> 59 us (0.89)
  local copies, waits for them, and re-layouts: 3.39 us -> 0 us
  Pallas kernels: 61.5 us -> 58.2 us
    pallas_call x1, Pallas kernels: 59.9 us -> 55.6 us  [shards(): pl.pallas_call(whole_kernel, out_shape=(shape((ROWS, 768)), shape((2, 288...]
    unnamed x8 -> x0, local copies, waits for them, and re-layouts: 3.39 us -> none
    pallas_call x1, Pallas kernels: 1.56 us -> 2.57 us  [shards(): pl.pallas_call(final_kernel, out_shape=(shape((ROWS, 768)), shape((2, 288...]
where the time goes in v4:
time: 59 us; the launch traced here: 58.8 us
  Pallas kernels  58.2 us (99%)
  between operations  0.64 us (1%)
    pallas_call x1, Pallas kernels, shards(): pl.pallas_call(whole_kernel, out_shape=(shape((ROWS, 768)), shape((2, 288...  55.6 us
    pallas_call x1, Pallas kernels, shards(): pl.pallas_call(final_kernel, out_shape=(shape((ROWS, 768)), shape((2, 288...  2.57 us

profile of v4, /device:TPU:0, one launch (start us, length us, event | category | flops | bytes accessed | tf_op | source)
XLA Modules:
  0.0 58.8 jit_solution(16205747959551582678)
XLA Ops:
  0.6 55.6 %shard_map.93 = (bf16[128,768]{1,0:T(8,128)(2,1)}, f32[2,288,128]{2,1,0:T(8,128)}, bf16[4,8,64,128]{3,2,1,0:T(8,128)(2,1)}, bf16[4,8,64,128]{3,2,1,0:T(8,128)(2,1)}) custom-call(s32[128]{0:T(128)} %pos_ref.1, bf16[128,768]{1,0:T(8,128)(2,1)} %q_hbm.1, bf16[576,128]{1,0:T(8,128)(2,1)} %bitcast.4, bf16[512,512]{1,0:T(8,128)(2,1)} %ku_hbm.1, ...), custom_call_target="tpu_custom_call" | custom-call | tf_op jit(solution)/shard_map/pallas_call | solution.py:523
  56.2 2.6 %shard_map.94 = (bf16[128,768]{1,0:T(8,128)(2,1)}, f32[2,288,128]{2,1,0:T(8,128)}, f32[512,512]{1,0:T(8,128)}, f32[512,512]{1,0:T(8,128)}) custom-call(bf16[128,768]{1,0:T(8,128)(2,1)} %get-tuple-element.12.qg_hbm, f32[2,288,128]{2,1,0:T(8,128)} %get-tuple-element.13.lg_hbm, bf16[4,8,64,128]{3,2,1,0:T(8,128)(2,1)} %get-tuple-element.14.ugk_hbm, ...), custom_call_target="tpu_custom_call" | custom-call | tf_op jit(solution)/shard_map/pallas_call | solution.py:538

commit v5 on v4

--- a/solution.py
+++ b/solution.py
@@ -94,29 +94,37 @@
     ):
         pl.semaphore_signal(barrier, inc=1, device_id=p, device_id_type=MESH)
 
-    done = []
-
     def go(src, dst, send, recv, device):
-        c = rcopy(src, dst, send, recv, device)
-        c.start()
-        done.append(c)
-
-    def landed(ref, send, recv):
-        rcopy(ref, ref, send, recv, across).wait_recv()
+        rcopy(src, dst, send, recv, device).start()
+
+    def landed(ref, recv):
+        rcopy(ref, ref, recv, recv, across).wait_recv()
+
+    def left(ref, send):
+        rcopy(ref, ref, send, send, across).wait_send()
 
     loads = [
         pltpu.make_async_copy(src, dst, s_in.at[i])
         for i, (src, dst) in enumerate(
-            [(latt_hbm, latt_ref), (ku_hbm, ku_ref), (vu_hbm, vu_ref), (q_hbm, q_ref), (g_hbm, g_ref)]
+            [(q_hbm, q_ref), (g_hbm, g_ref), (latt_hbm, latt_ref), (ku_hbm, ku_ref), (vu_hbm, vu_ref)]
         )
     ]
     for c in loads:
         c.start()
-    for c in loads:
-        c.wait()
+    loads[0].wait()
+    loads[1].wait()
 
     stripe = lax.shift_right_logical(pos_ref[0], 7).astype(F32)
     stripes = jnp.full((16, 128), stripe, F32).astype(BF16)
+    for h in range(NA):
+        q = q_ref[:, h * 192 : (h + 1) * 192]
+        pq[h, 0:128, :] = q[:, :128]
+        pq[h, 128:256, :] = g_ref[:, h * 128 : (h + 1) * 128]
+        pq[h, 256:320, :] = jnp.concatenate([q[:64, 128:], q[64:, 128:]], axis=1)
+        pq[h, 320:, :] = stripes
+    qb[0, 0] = pq[a]
+    for c in loads[2:]:
+        c.wait()
     comp = latt_ref[:D_LAT, :]
     kn = dot(comp, ku_ref[...], TN).astype(BF16)
     vv = dot(comp, vu_ref[...], TN).astype(BF16)
@@ -130,11 +138,8 @@
         pk[h, 128:256, :] = vv[:, h * 128 : (h + 1) * 128]
         pk[h, 256:320, :] = k_rope
         pk[h, 320:, :] = stripes
-        q = q_ref[:, h * 192 : (h + 1) * 192]
-        pq[h, 0:128, :] = q[:, :128]
-        pq[h, 128:256, :] = g_ref[:, h * 128 : (h + 1) * 128]
-        pq[h, 256:320, :] = jnp.concatenate([q[:64, 128:], q[64:, 128:]], axis=1)
-        pq[h, 320:, :] = stripes
+    kb[0, 0] = pk[a]
+    cl[0, 0] = comp
 
     pl.semaphore_wait(barrier, 6 + len(others) + 3)
 
@@ -144,22 +149,31 @@
     def on_b(e):
         return dev(a, (b + e) % NB, y)
 
+    def tile_of(d):
+        return 0 if d < 2 else 1
+
     for d in near:
-        to = (a + d) % NA
-        go(pk.at[to], kb.at[0, d], s_ak.at[d - 1], r_ak.at[d - 1], on_a(d))
-        go(pq.at[to], qb.at[0, d], s_aq.at[d - 1], r_aq.at[d - 1], on_a(d))
-    go(pk.at[a], kb.at[1, 0], s_yk.at[0], r_yk.at[0], across)
+        go(pk.at[(a + d) % NA], kb.at[0, d], s_ak, r_ak.at[d - 1], on_a(d))
+    go(pk.at[a], kb.at[1, 0], s_yk, r_yk, across)
+    for d in near:
+        go(pq.at[(a + d) % NA], qb.at[0, d], s_aq, r_aq.at[d - 1], on_a(d))
     for e in near:
-        go(pq.at[a], qb.at[e, 0], s_bq.at[e - 1, 0], r_bq.at[e - 1, 0], on_b(e))
-    qb[0, 0] = pq[a]
-    kb[0, 0] = pk[a]
-    cl[0, 0] = comp
-    for d in near:
-        landed(kb.at[0, d], s_ak.at[d - 1], r_ak.at[d - 1])
-        go(kb.at[0, d], kb.at[1, d], s_yk.at[d], r_yk.at[d], across)
-        landed(qb.at[0, d], s_aq.at[d - 1], r_aq.at[d - 1])
+        go(pq.at[a], qb.at[e, 0], s_bq, r_bq.at[e - 1, 0], on_b(e))
+    def pass_q(d):
+        landed(qb.at[0, d], r_aq.at[d - 1])
         for e in near:
-            go(qb.at[0, d], qb.at[e, d], s_bq.at[e - 1, d], r_bq.at[e - 1, d], on_b(e))
+            go(qb.at[0, d], qb.at[e, d], s_bq, r_bq.at[e - 1, tile_of(d)], on_b(e))
+
+    def pass_k(d):
+        landed(kb.at[0, d], r_ak.at[d - 1])
+        go(kb.at[0, d], kb.at[1, d], s_yk, r_yk, across)
+
+    pass_k(1)
+    pass_k(3)
+    pass_k(2)
+    pass_q(1)
+    pass_q(3)
+    pass_q(2)
     go(latt_ref.at[pl.ds(0, D_LAT)], cl.at[1, 0], s_yl, r_yl, across)
 
     half = NA * ROWS
@@ -186,8 +200,7 @@
             qp[e, at, :] = wide(qb[e, d])
 
     def wait_q(e, t):
-        for d in pairs[t]:
-            landed(qb.at[e, d], s_bq.at[e - 1, d], r_bq.at[e - 1, d])
+        landed(qb.at[e, pl.ds(2 * t, 2)], r_bq.at[e - 1, t])
 
     def grads_of(e, t):
         d0, d1 = pairs[t]
@@ -205,22 +218,23 @@
         dp_all[k, e, :, at] = dp
         top = jnp.max(s, axis=0, keepdims=True)
         if not first:
-            old = stl[e, 0:1, at]
+            old = stl[t, e, 0:1, :]
             top = jnp.maximum(top, old)
         w = jnp.exp2(s - jnp.maximum(top, FLOOR))
         total = jnp.sum(w, axis=0, keepdims=True)
         weighted = jnp.sum(w * dp, axis=0, keepdims=True)
         if not first:
             fade = jnp.exp2(old - top)
-            total = total + fade * stl[e, 1:2, at]
-            weighted = weighted + fade * stl[e, 2:3, at]
-        stl[e, 0:1, at] = top
-        stl[e, 1:2, at] = total
-        stl[e, 2:3, at] = weighted
-
-    def tell(e):
+            total = total + fade * stl[t, e, 1:2, :]
+            weighted = weighted + fade * stl[t, e, 2:3, :]
+        stl[t, e, 0:1, :] = top
+        stl[t, e, 1:2, :] = total
+        stl[t, e, 2:3, :] = weighted
+
+    def tell(t, e):
         for g in near:
-            go(stl.at[e], sb.at[(e + g) % NB, g], s_st.at[e, g - 1], r_st.at[(e + g) % NB, g - 1], on_b(g))
+            to = (e + g) % NB
+            go(stl.at[t, e], sb.at[t, to, g], s_st, r_st.at[t, to], on_b(g))
 
     stl[...] = jnp.zeros_like(stl)
     open_keys(0)
@@ -229,71 +243,83 @@
     for e in near:
         wait_q(e, 0)
         unit(0, e, 0, True)
-    for d in (0, 1, 3, 2):
-        landed(kb.at[1, d], s_yk.at[d], r_yk.at[d])
+    landed(kb.at[1], r_yk)
+    for d in near:
+        go(latt_ref.at[pl.ds(0, D_LAT)], cl.at[0, d], s_al, r_al, on_a(d))
     open_keys(1)
     unit(1, 0, 0, False)
-    unit(1, 0, 1, False)
-    tell(0)
+    tell(0, 0)
     for e in near:
         unit(1, e, 0, False)
+        tell(0, e)
+    unit(1, 0, 1, False)
+    tell(1, 0)
     for e in near:
         wait_q(e, 1)
-        if e == 2:
-            landed(cl.at[1, 0], s_yl, r_yl)
+        if e == 1:
+            landed(cl.at[1, 0], r_yl)
             for d in near:
-                go(latt_ref.at[pl.ds(0, D_LAT)], cl.at[0, d], s_al.at[0, d - 1], r_al.at[0, d - 1], on_a(d))
-                go(cl.at[1, 0], cl.at[1, d], s_al.at[1, d - 1], r_al.at[1, d - 1], on_a(d))
+                go(cl.at[1, 0], cl.at[1, d], s_al, r_al, on_a(d))
         unit(0, e, 1, True)
         unit(1, e, 1, False)
-        tell(e)
+        tell(1, e)
     kpt[...] = kp[...].reshape(KTOK, 256).T
 
-    for k in (1, 0):
+    def backward(k, t):
         ks = slice(k * half, (k + 1) * half)
+        at = slice(t * TILE, (t + 1) * TILE)
         for n, e in enumerate((0, 1, 3, 2)):
             if k == 1:
-                for g in near:
-                    landed(sb.at[e, g], s_st.at[e, g - 1], r_st.at[e, g - 1])
-                got = [stl[e]] + [sb[e, g] for g in near]
+                landed(sb.at[t, e, pl.ds(1, 3)], r_st.at[t, e])
+                got = [stl[t, e]] + [sb[t, e, g] for g in near]
                 tops = [r[0:1, :] for r in got]
                 top = jnp.maximum(jnp.maximum(tops[0], tops[1]), jnp.maximum(tops[2], tops[3]))
-                fades = [jnp.exp2(t - top) for t in tops]
+                fades = [jnp.exp2(u - top) for u in tops]
                 total = sum(f * r[1:2, :] for f, r in zip(fades, got))
-                rows[e, 1:2, :] = sum(f * r[2:3, :] for f, r in zip(fades, got)) / total
-                rows[e, 0:1, :] = top + jnp.log(total) * LOG2E
-            grads = jnp.concatenate([grads_of(e, 0), grads_of(e, 1)], axis=0)
-            p = jnp.exp2(s_all[k, e] - rows[e, 0:1, :])
-            ds = (p * (dp_all[k, e] - rows[e, 1:2, :]) * SCALE).astype(BF16)
-            ds_all[e, ks, :] = ds
-            dv = dot(p.astype(BF16), grads)
-            dk = dot(ds, qp[e])
-            if n == 0:
+                rows[e, 1:2, at] = sum(f * r[2:3, :] for f, r in zip(fades, got)) / total
+                rows[e, 0:1, at] = top + jnp.log(total) * LOG2E
+            p = jnp.exp2(s_all[k, e, :, at] - rows[e, 0:1, at])
+            ds = (p * (dp_all[k, e, :, at] - rows[e, 1:2, at]) * SCALE).astype(BF16)
+            ds_all[e, ks, at] = ds
+            dv = dot(p.astype(BF16), grads_of(e, t))
+            dk = dot(ds, qp[e, at, :])
+            if n == 0 and t == 0:
                 dva[ks, :] = dv
                 dka[ks, :] = dk
             else:
                 dva[ks, :] += dv
                 dka[ks, :] += dk
-        if k == 1:
-            for d in range(NA):
-                at = slice(half + d * ROWS, half + (d + 1) * ROWS)
-                gs1[d, :, :128] = dka[at, :128].astype(BF16)
-                gs1[d, :, 128:] = dva[at, :].astype(BF16)
-            for d in near:
-                go(gs1.at[d], rg1.at[a], s_g1.at[d - 1], r_g1.at[d - 1], on_a(NA - d))
-        else:
-            for d in range(NA):
-                at = slice(d * ROWS, (d + 1) * ROWS)
-                at1 = slice(half + d * ROWS, half + (d + 1) * ROWS)
-                gs0[d, :, :128] = dka[at, :128].astype(BF16)
-                gs0[d, :, 128:256] = dva[at, :].astype(BF16)
-                gs0[d, :, 256:] = jnp.concatenate([dka[at, 128:192], dka[at1, 128:192]], axis=1).astype(BF16)
-            for d in near:
-                go(gs0.at[d], rg0.at[a], s_g0.at[d - 1], r_g0.at[d - 1], on_a(NA - d))
-
+
+    def query_sums(t):
+        at = slice(t * TILE, (t + 1) * TILE)
+        for e in (2, 1, 3, 0):
+            dq = dot(kpt[:192, :], ds_all[e, :, at]).astype(BF16)
+            dqs[t, e, 0] = dq[:, :ROWS]
+            dqs[t, e, 1] = dq[:, ROWS:]
+            if e:
+                go(dqs.at[t, e], rq.at[t, e], s_dq, r_dq, on_b(NB - e))
+
+    backward(1, 0)
+    backward(0, 0)
+    query_sums(0)
+    backward(1, 1)
+    for d in range(NA):
+        at = slice(half + d * ROWS, half + (d + 1) * ROWS)
+        gs1[d, :, :128] = dka[at, :128].astype(BF16)
+        gs1[d, :, 128:] = dva[at, :].astype(BF16)
     for d in near:
-        for k in range(NY):
-            landed(cl.at[k, d], s_al.at[k, d - 1], r_al.at[k, d - 1])
+        go(gs1.at[d], rg1.at[a], s_g1, r_g1, on_a(NA - d))
+    backward(0, 1)
+    for d in range(NA):
+        at = slice(d * ROWS, (d + 1) * ROWS)
+        at1 = slice(half + d * ROWS, half + (d + 1) * ROWS)
+        gs0[d, :, :128] = dka[at, :128].astype(BF16)
+        gs0[d, :, 128:256] = dva[at, :].astype(BF16)
+        gs0[d, :, 256:] = jnp.concatenate([dka[at, 128:192], dka[at1, 128:192]], axis=1).astype(BF16)
+    for d in near:
+        go(gs0.at[d], rg0.at[a], s_g0, r_g0, on_a(NA - d))
+
+    landed(cl.at[:, pl.ds(1, 3)], r_al)
     g = jnp.concatenate([dka[:, :128], dva[...]], axis=1).astype(BF16)
     comps = jnp.concatenate([cl[k, i] for k in range(NY) for i in range(NA)], axis=1)
     up = dot(comps, g)
@@ -302,22 +328,15 @@
     mine = b * NY + y
     for i, (e, f) in enumerate(others):
         tb, ty = (b + e) % NB, (y + f) % NY
-        go(ups.at[tb * NY + ty], rup.at[mine], s_up.at[i], r_up.at[i], dev(a, tb, ty))
+        go(ups.at[tb * NY + ty], rup.at[mine], s_up, r_up, dev(a, tb, ty))
     rup[mine] = ups[mine]
 
-    for e in (2, 1, 3, 0):
-        dq = dot(kpt[:192, :], ds_all[e]).astype(BF16)
-        for t, (d0, d1) in enumerate(pairs):
-            dqs[e, d0] = dq[:, t * TILE : t * TILE + ROWS]
-            dqs[e, d1] = dq[:, t * TILE + ROWS : (t + 1) * TILE]
-        if e:
-            go(dqs.at[e], rq.at[e], s_dq.at[e], r_dq.at[e], on_b(NB - e))
+    query_sums(1)
     rg0[a] = gs0[0]
     rg1[a] = gs1[0]
 
-    for d in near:
-        landed(rg1.at[(a + d) % NA], s_g1.at[d - 1], r_g1.at[d - 1])
-        landed(rg0.at[(a + d) % NA], s_g0.at[d - 1], r_g0.at[d - 1])
+    landed(rg1.at[pl.ds(0, 3)], r_g1)
+    landed(rg0.at[pl.ds(0, 3)], r_g0)
     dk_all = jnp.concatenate(
         [jnp.concatenate([r[h, :, :128] for h in range(NA)], axis=1) for r in (rg0, rg1)], axis=0
     )
@@ -333,9 +352,7 @@
         lhalf[k] = lsum[k, 1 - core].astype(BF16)
     go(lhalf, rhalf, s_h.at[0], r_h.at[0], twin)
 
-    for i, (e, f) in enumerate(others):
-        fb, fy = (b + NB - e) % NB, (y + f) % NY
-        landed(rup.at[fb * NY + fy], s_up.at[i], r_up.at[i])
+    landed(rup.at[pl.ds(0, 7)], r_up)
     us = sum(rup[i].astype(F32) for i in range(NB * NY)).astype(BF16)
     usk[...] = us[:, :128]
     usv[...] = us[:, 128:]
@@ -343,32 +360,33 @@
     ugv[a, mine] = us[:, 128:]
     for i, (e, f) in enumerate(others):
         fy = (y + f) % NY
-        go(usk, ugk.at[a, mine], s_kb.at[i], r_kb.at[i], dev(a, (b + e) % NB, fy))
-        go(usv, ugv.at[a, mine], s_va.at[i], r_va.at[i], dev((a + e) % NA, b, fy))
-
-    def k_over_a(slot, i):
+        go(usk, ugk.at[a, mine], s_kb, r_kb.at[i], dev(a, (b + e) % NB, fy))
+        go(usv, ugv.at[a, mine], s_va, r_va.at[i], dev((a + e) % NA, b, fy))
+
+    def k_over_a(slot):
         for d in near:
-            go(slot, slot, s_ka.at[d - 1, i], r_ka.at[d - 1, i], dev((a + d) % NA, b, y))
-
-    def v_over_b(slot, i):
-        for d in near:
-            go(slot, slot, s_vb.at[d - 1, i], r_vb.at[d - 1, i], dev(a, (b + d) % NB, y))
-
-    k_over_a(ugk.at[a, mine], 7)
-    v_over_b(ugv.at[a, mine], 7)
-
-    landed(rhalf, s_h.at[0], r_h.at[0])
+            go(slot, slot, s_ka, r_ka.at[d - 1], on_a(d))
+
+    def v_over_b(slot):
+        for e in near:
+            go(slot, slot, s_vb, r_vb.at[e - 1], on_b(e))
+
+    k_over_a(ugk.at[a, mine])
+    v_over_b(ugv.at[a, mine])
+
+    landed(rhalf, r_h.at[0])
     for k in range(NY):
         hs[k] = (lsum[k, core] + rhalf[k].astype(F32)).astype(BF16)
     go(hs.at[0], rh.at[0], s_h.at[1], r_h.at[1], far)
-    go(hs.at[1], rh.at[1], s_h.at[2], r_h.at[2], across)
-    go(hs.at[1], rh.at[2], s_h.at[3], r_h.at[3], corner)
-
-    for e in near:
-        landed(rq.at[e], s_dq.at[e], r_dq.at[e])
-    dqf[...] = (dqs[0].astype(F32) + sum(rq[e].astype(F32) for e in near)).astype(BF16)
+    go(hs.at[1], rh.at[1], s_h.at[1], r_h.at[1], across)
+    go(hs.at[1], rh.at[2], s_h.at[1], r_h.at[1], corner)
+
+    landed(rq.at[:, pl.ds(1, 3)], r_dq)
+    for t in range(2):
+        for i, d in enumerate(pairs[t]):
+            dqf[d] = (dqs[t, 0, i].astype(F32) + sum(rq[t, e, i].astype(F32) for e in near)).astype(BF16)
     for d in near:
-        go(dqf.at[d], rdq.at[a], s_qf.at[d - 1], r_qf.at[d - 1], on_a(NA - d))
+        go(dqf.at[d], rdq.at[a], s_qf, r_qf, on_a(NA - d))
     rdq[a] = dqf[0]
 
     def piece(i, axis):
@@ -379,53 +397,62 @@
 
     for i in by_reach:
         slot = ugk.at[a, piece(i, "b")]
-        landed(slot, s_kb.at[i], r_kb.at[i])
-        k_over_a(slot, i)
+        landed(slot, r_kb.at[i])
+        k_over_a(slot)
         fa, fy = piece(i, "a")
         slot = ugv.at[fa, b * NY + fy]
-        landed(slot, s_va.at[i], r_va.at[i])
-        v_over_b(slot, i)
-
-    for i in range(3):
-        landed(rh.at[i], s_h.at[1 + i], r_h.at[1 + i])
+        landed(slot, r_va.at[i])
+        v_over_b(slot)
+
+    landed(rh, r_h.at[1])
     whole = hs[0].astype(F32) + rh[0].astype(F32) + rh[1].astype(F32) + rh[2].astype(F32)
     lfin[...] = whole
-    go(lfin, rfin, s_h.at[4], r_h.at[4], twin)
-
-    for d in near:
-        landed(rdq.at[(a + d) % NA], s_qf.at[d - 1], r_qf.at[d - 1])
+    go(lfin, rfin, s_h.at[2], r_h.at[2], twin)
+
+    landed(rdq.at[pl.ds(0, 3)], r_qf)
     for h in range(NA):
         qg_ref[:, h * 192 : (h + 1) * 192] = rdq[h].T
 
-    outs = []
-
-    def write(src, dst):
-        c = pltpu.make_async_copy(src, dst, s_out.at[len(outs)])
-        c.start()
-        outs.append(c)
-
-    write(qg_ref, qg_hbm)
-    landed(rfin, s_h.at[4], r_h.at[4])
-    write(lfin, lg_hbm.at[core])
-    write(rfin, lg_hbm.at[1 - core])
-    write(ugk.at[a], ugk_hbm.at[a])
+    def write(src, dst, sem):
+        pltpu.make_async_copy(src, dst, s_out.at[sem]).start()
+
+    write(qg_ref, qg_hbm, 0)
+    landed(rfin, r_h.at[2])
+    write(lfin, lg_hbm.at[core], 1)
+    write(rfin, lg_hbm.at[1 - core], 1)
+    write(ugk.at[a], ugk_hbm.at[a], 2)
     own_b = pl.ds(b * NY, NY)
-    write(ugv.at[:, own_b], ugv_hbm.at[:, own_b])
+    write(ugv.at[:, own_b], ugv_hbm.at[:, own_b], 3)
 
     for d in near:
-        fa, fb = (a + NA - d) % NA, (b + NB - d) % NB
-        for i in range(8):
-            p = mine if i == 7 else piece(i, "b")
-            landed(ugk.at[fa, p], s_ka.at[d - 1, i], r_ka.at[d - 1, i])
-            pa, py = (a, y) if i == 7 else piece(i, "a")
-            landed(ugv.at[pa, fb * NY + py], s_vb.at[d - 1, i], r_vb.at[d - 1, i])
-        write(ugk.at[fa], ugk_hbm.at[fa])
-        from_b = pl.ds(fb * NY, NY)
-        write(ugv.at[:, from_b], ugv_hbm.at[:, from_b])
-    for c in outs:
-        c.wait()
-    for c in done:
-        c.wait_send()
+        fa, from_b = (a + NA - d) % NA, pl.ds((b + NB - d) % NB * NY, NY)
+        landed(ugk.at[fa], r_ka.at[d - 1])
+        write(ugk.at[fa], ugk_hbm.at[fa], 2)
+        landed(ugv.at[:, from_b], r_vb.at[d - 1])
+        write(ugv.at[:, from_b], ugv_hbm.at[:, from_b], 3)
+    left(pq.at[pl.ds(0, 3)], s_aq)
+    left(pk.at[pl.ds(0, 3)], s_ak)
+    left(qb.at[pl.ds(0, 3)], s_bq)
+    left(kb.at[0], s_yk)
+    left(cl.at[1, 0], s_yl)
+    left(cl.at[:, pl.ds(1, 3)], s_al)
+    left(sb.at[:, pl.ds(0, 3)], s_st)
+    left(rq.at[:, pl.ds(1, 3)], s_dq)
+    left(rg0.at[pl.ds(0, 3)], s_g0)
+    left(rg1.at[pl.ds(0, 3)], s_g1)
+    left(rdq.at[pl.ds(0, 3)], s_qf)
+    left(rup.at[pl.ds(0, 7)], s_up)
+    left(ugk.at[0, pl.ds(0, 7)], s_kb)
+    left(ugk.at[0, pl.ds(0, 7)], s_va)
+    left(ugk.at[pl.ds(0, 3)], s_ka)
+    left(ugv.at[pl.ds(0, 3)], s_vb)
+    left(lhalf, s_h.at[0])
+    left(rh, s_h.at[1])
+    left(lfin, s_h.at[2])
+    pltpu.make_async_copy(qg_ref, qg_hbm, s_out.at[0]).wait()
+    pltpu.make_async_copy(lsum.at[0], lg_hbm, s_out.at[1]).wait()
+    pltpu.make_async_copy(ugk, ugk_hbm, s_out.at[2]).wait()
+    pltpu.make_async_copy(ugv, ugv_hbm, s_out.at[3]).wait()
 
 
 def final_kernel(
@@ -482,12 +509,12 @@
         pltpu.VMEM((NY, half, TILE), F32),
         pltpu.VMEM((NY, NB, half, half), F32),
         pltpu.VMEM((NY, NB, half, half), F32),
-        pltpu.VMEM((NB, 8, half), F32),
-        pltpu.VMEM((NB, NB, 8, half), F32),
+        pltpu.VMEM((2, NB, 8, TILE), F32),
+        pltpu.VMEM((2, NB, NB, 8, TILE), F32),
         pltpu.VMEM((NB, 8, half), F32),
         pltpu.VMEM((NB, KTOK, half), BF16),
-        pltpu.VMEM((NB, NA, 192, 128), BF16),
-        pltpu.VMEM((NB, NA, 192, 128), BF16),
+        pltpu.VMEM((2, NB, 2, 192, 128), BF16),
+        pltpu.VMEM((2, NB, 2, 192, 128), BF16),
         pltpu.VMEM((KTOK, 256), F32),
         pltpu.VMEM((KTOK, 128), F32),
         pltpu.VMEM((NA, ROWS, 384), BF16),
@@ -512,12 +539,12 @@
         pltpu.VMEM((NA, NB * NY, 64, 128), BF16),
     ]
     sems = [
-        dma((5,)), dma((3,)), dma((3,)), dma((3,)), dma((3,)), dma((2, 3)), dma((2, 3)),
-        dma((3, 4)), dma((3, 4)), dma((4,)), dma((4,)), dma, dma,
-        dma((4, 3)), dma((4, 3)), dma((4,)), dma((4,)),
-        dma((3,)), dma((3,)), dma((3,)), dma((3,)), dma((3,)), dma((3,)), dma((7,)), dma((7,)),
-        dma((7,)), dma((7,)), dma((3, 8)), dma((3, 8)), dma((7,)), dma((7,)), dma((3, 8)), dma((3, 8)),
-        dma((5,)), dma((5,)), dma((11,)),
+        dma((5,)), dma, dma((3,)), dma, dma((3,)), dma, dma,
+        dma, dma((3, 2)), dma, dma, dma, dma,
+        dma, dma((2, 4)), dma, dma,
+        dma, dma, dma, dma, dma, dma, dma, dma,
+        dma, dma((7,)), dma, dma((3,)), dma, dma((7,)), dma, dma((3,)),
+        dma((3,)), dma((3,)), dma((4,)),
     ]
     hbm = pl.BlockSpec(memory_space=pltpu.HBM)
     qg, lg, ugk, ugv = pl.pallas_call(

time: 59 us -> 57.2 us (0.969)
  Pallas kernels: 58.2 us -> 56.4 us
    pallas_call x1, Pallas kernels: 55.6 us -> 53.8 us  [shards(): pl.pallas_call(whole_kernel, out_shape=(shape((ROWS, 768)), shape((2, 288...]
where the time goes in v5:
time: 57.2 us; the launch traced here: 57.1 us
  Pallas kernels  56.4 us (99%)
  between operations  0.64 us (1%)
    pallas_call x1, Pallas kernels, shards(): pl.pallas_call(whole_kernel, out_shape=(shape((ROWS, 768)), shape((2, 288...  53.8 us
    pallas_call x1, Pallas kernels, shards(): pl.pallas_call(final_kernel, out_shape=(shape((ROWS, 768)), shape((2, 288...  2.57 us

profile of v5, /device:TPU:0, one launch (start us, length us, event | category | flops | bytes accessed | tf_op | source)
XLA Modules:
  0.0 57.1 jit_solution(6005351507055683748)
XLA Ops:
  0.6 53.8 %shard_map.93 = (bf16[128,768]{1,0:T(8,128)(2,1)}, f32[2,288,128]{2,1,0:T(8,128)}, bf16[4,8,64,128]{3,2,1,0:T(8,128)(2,1)}, bf16[4,8,64,128]{3,2,1,0:T(8,128)(2,1)}) custom-call(s32[128]{0:T(128)} %pos_ref.1, bf16[128,768]{1,0:T(8,128)(2,1)} %q_hbm.1, bf16[576,128]{1,0:T(8,128)(2,1)} %bitcast.4, bf16[512,512]{1,0:T(8,128)(2,1)} %ku_hbm.1, ...), custom_call_target="tpu_custom_call" | custom-call | tf_op jit(solution)/shard_map/pallas_call | solution.py:550
  54.5 2.6 %shard_map.94 = (bf16[128,768]{1,0:T(8,128)(2,1)}, f32[2,288,128]{2,1,0:T(8,128)}, f32[512,512]{1,0:T(8,128)}, f32[512,512]{1,0:T(8,128)}) custom-call(bf16[128,768]{1,0:T(8,128)(2,1)} %get-tuple-element.12.qg_hbm, f32[2,288,128]{2,1,0:T(8,128)} %get-tuple-element.13.lg_hbm, bf16[4,8,64,128]{3,2,1,0:T(8,128)(2,1)} %get-tuple-element.14.ugk_hbm, ...), custom_call_target="tpu_custom_call" | custom-call | tf_op jit(solution)/shard_map/pallas_call | solution.py:565

commit v6 on v5

--- a/solution.py
+++ b/solution.py
@@ -84,6 +84,7 @@
     near = (1, 3, 2)
     others = [(0, 1), (1, 0), (1, 1), (2, 0), (2, 1), (3, 0), (3, 1)]
     by_reach = (1, 5, 0, 3, 2, 6, 4)
+    far_first = by_reach[::-1]
 
     barrier = pltpu.get_barrier_semaphore()
     for p in (
@@ -326,7 +327,8 @@
     for i in range(NB * NY):
         ups[i] = up[i * 64 : (i + 1) * 64, :].astype(BF16)
     mine = b * NY + y
-    for i, (e, f) in enumerate(others):
+    for i in far_first:
+        e, f = others[i]
         tb, ty = (b + e) % NB, (y + f) % NY
         go(ups.at[tb * NY + ty], rup.at[mine], s_up, r_up, dev(a, tb, ty))
     rup[mine] = ups[mine]
@@ -334,6 +336,29 @@
     query_sums(1)
     rg0[a] = gs0[0]
     rg1[a] = gs1[0]
+
+    landed(rup.at[pl.ds(0, 7)], r_up)
+    us = sum(rup[i].astype(F32) for i in range(NB * NY)).astype(BF16)
+    usk[...] = us[:, :128]
+    usv[...] = us[:, 128:]
+    ugk[a, mine] = us[:, :128]
+    ugv[a, mine] = us[:, 128:]
+    for i in far_first:
+        e, f = others[i]
+        fy = (y + f) % NY
+        go(usk, ugk.at[a, mine], s_kb, r_kb.at[i], dev(a, (b + e) % NB, fy))
+        go(usv, ugv.at[a, mine], s_va, r_va.at[i], dev((a + e) % NA, b, fy))
+
+    def k_over_a(slot):
+        for d in near:
+            go(slot, slot, s_ka, r_ka.at[d - 1], on_a(d))
+
+    def v_over_b(slot):
+        for e in near:
+            go(slot, slot, s_vb, r_vb.at[e - 1], on_b(e))
+
+    k_over_a(ugk.at[a, mine])
+    v_over_b(ugv.at[a, mine])
 
     landed(rg1.at[pl.ds(0, 3)], r_g1)
     landed(rg0.at[pl.ds(0, 3)], r_g0)
@@ -352,28 +377,23 @@
         lhalf[k] = lsum[k, 1 - core].astype(BF16)
     go(lhalf, rhalf, s_h.at[0], r_h.at[0], twin)
 
-    landed(rup.at[pl.ds(0, 7)], r_up)
-    us = sum(rup[i].astype(F32) for i in range(NB * NY)).astype(BF16)
-    usk[...] = us[:, :128]
-    usv[...] = us[:, 128:]
-    ugk[a, mine] = us[:, :128]
-    ugv[a, mine] = us[:, 128:]
-    for i, (e, f) in enumerate(others):
-        fy = (y + f) % NY
-        go(usk, ugk.at[a, mine], s_kb, r_kb.at[i], dev(a, (b + e) % NB, fy))
-        go(usv, ugv.at[a, mine], s_va, r_va.at[i], dev((a + e) % NA, b, fy))
-
-    def k_over_a(slot):
-        for d in near:
-            go(slot, slot, s_ka, r_ka.at[d - 1], on_a(d))
-
-    def v_over_b(slot):
-        for e in near:
-            go(slot, slot, s_vb, r_vb.at[e - 1], on_b(e))
-
-    k_over_a(ugk.at[a, mine])
-    v_over_b(ugv.at[a, mine])
-
+    def piece(i, axis):
+        e, f = others[i]
+        if axis == "b":
+            return (b + NB - e) % NB * NY + (y + f) % NY
+        return (a + NA - e) % NA, (y + f) % NY
+
+    def pass_on(i):
+        slot = ugk.at[a, piece(i, "b")]
+        landed(slot, r_kb.at[i])
+        k_over_a(slot)
+        fa, fy = piece(i, "a")
+        slot = ugv.at[fa, b * NY + fy]
+        landed(slot, r_va.at[i])
+        v_over_b(slot)
+
+    for i in by_reach[:4]:
+        pass_on(i)
     landed(rhalf, r_h.at[0])
     for k in range(NY):
         hs[k] = (lsum[k, core] + rhalf[k].astype(F32)).astype(BF16)
@@ -381,6 +401,8 @@
     go(hs.at[1], rh.at[1], s_h.at[1], r_h.at[1], across)
     go(hs.at[1], rh.at[2], s_h.at[1], r_h.at[1], corner)
 
+    for i in by_reach[4:]:
+        pass_on(i)
     landed(rq.at[:, pl.ds(1, 3)], r_dq)
     for t in range(2):
         for i, d in enumerate(pairs[t]):
@@ -389,21 +411,6 @@
         go(dqf.at[d], rdq.at[a], s_qf, r_qf, on_a(NA - d))
     rdq[a] = dqf[0]
 
-    def piece(i, axis):
-        e, f = others[i]
-        if axis == "b":
-            return (b + NB - e) % NB * NY + (y + f) % NY
-        return (a + NA - e) % NA, (y + f) % NY
-
-    for i in by_reach:
-        slot = ugk.at[a, piece(i, "b")]
-        landed(slot, r_kb.at[i])
-        k_over_a(slot)
-        fa, fy = piece(i, "a")
-        slot = ugv.at[fa, b * NY + fy]
-        landed(slot, r_va.at[i])
-        v_over_b(slot)
-
     landed(rh, r_h.at[1])
     whole = hs[0].astype(F32) + rh[0].astype(F32) + rh[1].astype(F32) + rh[2].astype(F32)
     lfin[...] = whole
@@ -417,9 +424,6 @@
         pltpu.make_async_copy(src, dst, s_out.at[sem]).start()
 
     write(qg_ref, qg_hbm, 0)
-    landed(rfin, r_h.at[2])
-    write(lfin, lg_hbm.at[core], 1)
-    write(rfin, lg_hbm.at[1 - core], 1)
     write(ugk.at[a], ugk_hbm.at[a], 2)
     own_b = pl.ds(b * NY, NY)
     write(ugv.at[:, own_b], ugv_hbm.at[:, own_b], 3)
@@ -430,6 +434,9 @@
         write(ugk.at[fa], ugk_hbm.at[fa], 2)
         landed(ugv.at[:, from_b], r_vb.at[d - 1])
         write(ugv.at[:, from_b], ugv_hbm.at[:, from_b], 3)
+    landed(rfin, r_h.at[2])
+    write(lfin, lg_hbm.at[core], 1)
+    write(rfin, lg_hbm.at[1 - core], 1)
     left(pq.at[pl.ds(0, 3)], s_aq)
     left(pk.at[pl.ds(0, 3)], s_ak)
     left(qb.at[pl.ds(0, 3)], s_bq)

time: 57.2 us -> 55.5 us (0.970)
  Pallas kernels: 56.4 us -> 54.5 us
    pallas_call x1, Pallas kernels: 53.8 us -> 51.9 us  [shards(): pl.pallas_call(whole_kernel, out_shape=(shape((ROWS, 768)), shape((2, 288...]
where the time goes in v6:
time: 55.5 us; the launch traced here: 55.2 us
  Pallas kernels  54.5 us (98%)
  between operations  0.64 us (1%)
    pallas_call x1, Pallas kernels, shards(): pl.pallas_call(whole_kernel, out_shape=(shape((ROWS, 768)), shape((2, 288...  51.9 us
    pallas_call x1, Pallas kernels, shards(): pl.pallas_call(final_kernel, out_shape=(shape((ROWS, 768)), shape((2, 288...  2.57 us

profile of v6, /device:TPU:0, one launch (start us, length us, event | category | flops | bytes accessed | tf_op | source)
XLA Modules:
  0.0 55.2 jit_solution(10011417634645907856)
XLA Ops:
  0.6 51.9 %shard_map.93 = (bf16[128,768]{1,0:T(8,128)(2,1)}, f32[2,288,128]{2,1,0:T(8,128)}, bf16[4,8,64,128]{3,2,1,0:T(8,128)(2,1)}, bf16[4,8,64,128]{3,2,1,0:T(8,128)(2,1)}) custom-call(s32[128]{0:T(128)} %pos_ref.1, bf16[128,768]{1,0:T(8,128)(2,1)} %q_hbm.1, bf16[576,128]{1,0:T(8,128)(2,1)} %bitcast.4, bf16[512,512]{1,0:T(8,128)(2,1)} %ku_hbm.1, ...), custom_call_target="tpu_custom_call" | custom-call | tf_op jit(solution)/shard_map/pallas_call | solution.py:557
  52.6 2.6 %shard_map.94 = (bf16[128,768]{1,0:T(8,128)(2,1)}, f32[2,288,128]{2,1,0:T(8,128)}, f32[512,512]{1,0:T(8,128)}, f32[512,512]{1,0:T(8,128)}) custom-call(bf16[128,768]{1,0:T(8,128)(2,1)} %get-tuple-element.12.qg_hbm, f32[2,288,128]{2,1,0:T(8,128)} %get-tuple-element.13.lg_hbm, bf16[4,8,64,128]{3,2,1,0:T(8,128)(2,1)} %get-tuple-element.14.ugk_hbm, ...), custom_call_target="tpu_custom_call" | custom-call | tf_op jit(solution)/shard_map/pallas_call | solution.py:572

commit v7 on v6

--- a/solution.py
+++ b/solution.py
@@ -28,7 +28,6 @@
 F32 = jnp.float32
 BF16 = jnp.bfloat16
 VMEM = pl.BlockSpec(memory_space=pltpu.VMEM)
-SMEM = pl.BlockSpec(memory_space=pltpu.SMEM)
 NT = (((1,), (1,)), ((), ()))
 TN = (((0,), (0,)), ((), ()))
 
@@ -66,9 +65,9 @@
 
 
 def whole_kernel(
-    pos_ref, q_hbm, latt_hbm, ku_hbm, vu_hbm, g_hbm,
+    pos_hbm, q_hbm, latt_hbm, ku_hbm, vu_hbm, g_hbm,
     qg_hbm, lg_hbm, ugk_hbm, ugv_hbm,
-    q_ref, latt_ref, ku_ref, vu_ref, g_ref,
+    pos_ref, q_ref, latt_ref, ku_ref, vu_ref, g_ref,
     pq, pk, qb, kb, qp, kp, kpt, cl, kpos, s_all, dp_all, stl, sb, rows, ds_all, dqs, rq, dka, dva, gs0, gs1, rg0, rg1,
     dqf, rdq, ups, rup, usk, usv, lsum, lhalf, rhalf, hs, rh, lfin, rfin, qg_ref, ugk, ugv,
     s_in, s_aq, r_aq, s_ak, r_ak, s_al, r_al, s_bq, r_bq, s_yk, r_yk, s_yl, r_yl, s_st, r_st, s_dq, r_dq,
@@ -107,13 +106,13 @@
     loads = [
         pltpu.make_async_copy(src, dst, s_in.at[i])
         for i, (src, dst) in enumerate(
-            [(q_hbm, q_ref), (g_hbm, g_ref), (latt_hbm, latt_ref), (ku_hbm, ku_ref), (vu_hbm, vu_ref)]
+            [(pos_hbm, pos_ref), (q_hbm, q_ref), (g_hbm, g_ref), (latt_hbm, latt_ref), (ku_hbm, ku_ref), (vu_hbm, vu_ref)]
         )
     ]
     for c in loads:
         c.start()
-    loads[0].wait()
-    loads[1].wait()
+    for c in loads[:3]:
+        c.wait()
 
     stripe = lax.shift_right_logical(pos_ref[0], 7).astype(F32)
     stripes = jnp.full((16, 128), stripe, F32).astype(BF16)
@@ -124,7 +123,7 @@
         pq[h, 256:320, :] = jnp.concatenate([q[:64, 128:], q[64:, 128:]], axis=1)
         pq[h, 320:, :] = stripes
     qb[0, 0] = pq[a]
-    for c in loads[2:]:
+    for c in loads[3:]:
         c.wait()
     comp = latt_ref[:D_LAT, :]
     kn = dot(comp, ku_ref[...], TN).astype(BF16)
@@ -500,6 +499,7 @@
     half = NA * ROWS
     dma = pltpu.SemaphoreType.DMA
     scratch = [
+        pltpu.SMEM((ROWS,), jnp.int32),
         pltpu.VMEM((ROWS, 768), BF16),
         pltpu.VMEM((576, ROWS), BF16),
         pltpu.VMEM((D_LAT, 512), BF16),
@@ -546,7 +546,7 @@
         pltpu.VMEM((NA, NB * NY, 64, 128), BF16),
     ]
     sems = [
-        dma((5,)), dma, dma((3,)), dma, dma((3,)), dma, dma,
+        dma((6,)), dma, dma((3,)), dma, dma((3,)), dma, dma,
         dma, dma((3, 2)), dma, dma, dma, dma,
         dma, dma((2, 4)), dma, dma,
         dma, dma, dma, dma, dma, dma, dma, dma,
@@ -562,7 +562,7 @@
             shape((NA, NB * NY, 64, 128)),
             shape((NA, NB * NY, 64, 128)),
         ),
-        in_specs=[SMEM] + [hbm] * 5,
+        in_specs=[hbm] * 6,
         out_specs=(hbm,) * 4,
         scratch_shapes=scratch + sems,
         compiler_params=pltpu.CompilerParams(

time: 55.5 us -> 54.8 us (0.987)
  no operation moved by 1% of the time
where the time goes in v7:
time: 54.8 us; the launch traced here: 54.7 us
  Pallas kernels  54 us (99%)
  between operations  0.64 us (1%)
    pallas_call x1, Pallas kernels, shards(): pl.pallas_call(whole_kernel, out_shape=(shape((ROWS, 768)), shape((2, 288...  51.4 us
    pallas_call x1, Pallas kernels, shards(): pl.pallas_call(final_kernel, out_shape=(shape((ROWS, 768)), shape((2, 288...  2.57 us

profile of v7, /device:TPU:0, one launch (start us, length us, event | category | flops | bytes accessed | tf_op | source)
XLA Modules:
  0.0 54.7 jit_solution(16446821838329789234)
XLA Ops:
  0.6 51.4 %shard_map.93 = (bf16[128,768]{1,0:T(8,128)(2,1)}, f32[2,288,128]{2,1,0:T(8,128)}, bf16[4,8,64,128]{3,2,1,0:T(8,128)(2,1)}, bf16[4,8,64,128]{3,2,1,0:T(8,128)(2,1)}) custom-call(s32[128]{0:T(128)} %pos_hbm.1, bf16[128,768]{1,0:T(8,128)(2,1)} %q_hbm.1, bf16[576,128]{1,0:T(8,128)(2,1)} %bitcast.4, bf16[512,512]{1,0:T(8,128)(2,1)} %ku_hbm.1, ...), custom_call_target="tpu_custom_call" | custom-call | tf_op jit(solution)/shard_map/pallas_call | solution.py:557
  52.1 2.6 %shard_map.94 = (bf16[128,768]{1,0:T(8,128)(2,1)}, f32[2,288,128]{2,1,0:T(8,128)}, f32[512,512]{1,0:T(8,128)}, f32[512,512]{1,0:T(8,128)}) custom-call(bf16[128,768]{1,0:T(8,128)(2,1)} %get-tuple-element.12.qg_hbm, f32[2,288,128]{2,1,0:T(8,128)} %get-tuple-element.13.lg_hbm, bf16[4,8,64,128]{3,2,1,0:T(8,128)(2,1)} %get-tuple-element.14.ugk_hbm, ...), custom_call_target="tpu_custom_call" | custom-call | tf_op jit(solution)/shard_map/pallas_call | solution.py:572

commit v8 on v7

--- a/solution.py
+++ b/solution.py
@@ -170,9 +170,9 @@
 
     pass_k(1)
     pass_k(3)
-    pass_k(2)
     pass_q(1)
     pass_q(3)
+    pass_k(2)
     pass_q(2)
     go(latt_ref.at[pl.ds(0, D_LAT)], cl.at[1, 0], s_yl, r_yl, across)
 
@@ -376,6 +376,14 @@
         lhalf[k] = lsum[k, 1 - core].astype(BF16)
     go(lhalf, rhalf, s_h.at[0], r_h.at[0], twin)
 
+    landed(rq.at[:, pl.ds(1, 3)], r_dq)
+    for t in range(2):
+        for i, d in enumerate(pairs[t]):
+            dqf[d] = (dqs[t, 0, i].astype(F32) + sum(rq[t, e, i].astype(F32) for e in near)).astype(BF16)
+    for d in near:
+        go(dqf.at[d], rdq.at[a], s_qf, r_qf, on_a(NA - d))
+    rdq[a] = dqf[0]
+
     def piece(i, axis):
         e, f = others[i]
         if axis == "b":
@@ -402,14 +410,6 @@
 
     for i in by_reach[4:]:
         pass_on(i)
-    landed(rq.at[:, pl.ds(1, 3)], r_dq)
-    for t in range(2):
-        for i, d in enumerate(pairs[t]):
-            dqf[d] = (dqs[t, 0, i].astype(F32) + sum(rq[t, e, i].astype(F32) for e in near)).astype(BF16)
-    for d in near:
-        go(dqf.at[d], rdq.at[a], s_qf, r_qf, on_a(NA - d))
-    rdq[a] = dqf[0]
-
     landed(rh, r_h.at[1])
     whole = hs[0].astype(F32) + rh[0].astype(F32) + rh[1].astype(F32) + rh[2].astype(F32)
     lfin[...] = whole

time: 54.8 us -> 54.8 us (level); the launches traced: 54.7 us -> 54.1 us
  Pallas kernels: 54 us -> 53.4 us
    pallas_call x1, Pallas kernels: 51.4 us -> 50.9 us  [shards(): pl.pallas_call(whole_kernel, out_shape=(shape((ROWS, 768)), shape((2, 288...]
where the time goes in v8:
time: 54.8 us; the launch traced here: 54.1 us
  Pallas kernels  53.4 us (97%)
  between operations  0.64 us (1%)
    pallas_call x1, Pallas kernels, shards(): pl.pallas_call(whole_kernel, out_shape=(shape((ROWS, 768)), shape((2, 288...  50.9 us
    pallas_call x1, Pallas kernels, shards(): pl.pallas_call(final_kernel, out_shape=(shape((ROWS, 768)), shape((2, 288...  2.57 us

profile of v8, /device:TPU:0, one launch (start us, length us, event | category | flops | bytes accessed | tf_op | source)
XLA Modules:
  0.0 54.1 jit_solution(16911298262878206093)
XLA Ops:
  0.6 50.9 %shard_map.93 = (bf16[128,768]{1,0:T(8,128)(2,1)}, f32[2,288,128]{2,1,0:T(8,128)}, bf16[4,8,64,128]{3,2,1,0:T(8,128)(2,1)}, bf16[4,8,64,128]{3,2,1,0:T(8,128)(2,1)}) custom-call(s32[128]{0:T(128)} %pos_hbm.1, bf16[128,768]{1,0:T(8,128)(2,1)} %q_hbm.1, bf16[576,128]{1,0:T(8,128)(2,1)} %bitcast.4, bf16[512,512]{1,0:T(8,128)(2,1)} %ku_hbm.1, ...), custom_call_target="tpu_custom_call" | custom-call | tf_op jit(solution)/shard_map/pallas_call | solution.py:557
  51.5 2.6 %shard_map.94 = (bf16[128,768]{1,0:T(8,128)(2,1)}, f32[2,288,128]{2,1,0:T(8,128)}, f32[512,512]{1,0:T(8,128)}, f32[512,512]{1,0:T(8,128)}) custom-call(bf16[128,768]{1,0:T(8,128)(2,1)} %get-tuple-element.12.qg_hbm, f32[2,288,128]{2,1,0:T(8,128)} %get-tuple-element.13.lg_hbm, bf16[4,8,64,128]{3,2,1,0:T(8,128)(2,1)} %get-tuple-element.14.ugk_hbm, ...), custom_call_target="tpu_custom_call" | custom-call | tf_op jit(solution)/shard_map/pallas_call | solution.py:572
